TPU v7x, 128 devices: a whole 4x4x4 slice. The times are simulated.
128 devices in a mesh: gx: 16 (over y, z), gy: 8 (over x, core).
Axes of the slice: x: 4, y: 4, z: 4, core: 2. Of those that a mesh axis runs over, the one named last changes fastest.
Arguments:
- table: float32 [4, 131072, 128], P(None, 'gx'), may hold values from -2.1 to 2.1
- lookup_owner: int32 [4, 32768, 16, 1], P(None, ('gx', 'gy')), may hold values from 0 to 15; in each aligned block of 4096 rows (0 to 4095, 4096 to 8191, ..., all dimensions but the last counted through in order) at most 512 rows name the same one
- lookup_row: int32 [4, 32768, 16], P(None, ('gx', 'gy')), may hold values from 0 to 8191
- bag_length: int32 [4, 32768], P(None, ('gx', 'gy')), may hold values from 1 to 16
- top_in: bfloat16 [512, 8192], P(None, 'gy'), may hold values from -0.25 to 0.25
- top_bias: float32 [8192], P('gy'), may hold values from -3 to 3
- top_out: bfloat16 [8192, 1024], P('gy'), may hold values from -0.0625 to 0.0625
Outputs:
- scored: bfloat16 [32768, 1024], P(('gx', 'gy'))
Inputs may be any that keep to these rules, and one draw needn't show every extreme that they name: `lookup_owner`: in every aligned block of 4096 entries (the lookups of one table from the samples of one device) no owner is named more than 512 times; some blocks reach 512.
All inputs are finite; a program needn't handle non-finite values.
Results may differ from a plain program's by a relative error of at most 0.0057.
Values may be sent and summed in bfloat16 or wider, within the bound.
No kernel may reach another device: no remote copies, remote signals or barrier semaphores. Data moves between devices by JAX's collectives and lax.ppermute only.
A program may use at most 128 MiB of HBM per device.

v0:
```python
import functools

import jax
import jax.numpy as jnp
from jax import lax
from jax.experimental import pallas as pl
from jax.experimental.pallas import tpu as pltpu
from jax.sharding import PartitionSpec as P


TABLES = 4
SAMPLES = 256
BAG = 16
OWNERS = 16
CAP = 512
ROWS_DEV = 8192
EMB = 128
UNROLL = 16
STEP = 4
VALID = 1 << 13
BAG_SHIFT = 14
CHUNKS = (2, 2)


def iota(shape, dim):
    return lax.broadcasted_iota(jnp.int32, shape, dim)


def ones_where(mask):
    return jnp.where(mask, 1.0, 0.0).astype(jnp.bfloat16)


def dispatch_kernel(own_ref, row_ref, out_ref):
    before = ones_where(iota((256, 256), 0) < iota((256, 256), 1))
    r, c = iota((256, 256), 0), iota((256, 256), 1)
    earlier = ones_where(((r & 15) == (c & 15)) & ((c >> 4) < (r >> 4)))
    ones = jnp.ones((256, 256), jnp.bfloat16)
    same = ones_where(iota((16, 256), 0) == (iota((16, 256), 1) & 15))
    owner_iota = iota((16, 16, 256), 1)
    for t in range(TABLES):
        own = own_ref[t]
        mark = (own[:, None, :] == owner_iota).reshape(256, 256)
        onehot = ones_where(mark)
        rank = jnp.dot(onehot, before, preferred_element_type=jnp.float32)
        lead = jnp.dot(earlier, onehot, preferred_element_type=jnp.float32)
        rank += jnp.dot(lead.astype(jnp.bfloat16), ones, preferred_element_type=jnp.float32)
        rank = jnp.sum(jnp.where(mark, rank, 0.0).reshape(16, 16, 256), axis=1).astype(jnp.int32)
        total = jnp.dot(same, onehot, preferred_element_type=jnp.float32)
        total = jnp.dot(total.astype(jnp.bfloat16), ones, preferred_element_type=jnp.float32)
        out_ref[:, 16 + t, :] = total[:, :128].astype(jnp.int32)
        hi = own * 4 + (rank >> 7)
        lo = rank & 127
        row = row_ref[t]
        low = (row & 255).astype(jnp.float32)
        high = ((row >> 8) + (VALID >> 8)).astype(jnp.float32)
        bag = iota((1, 256), 1).astype(jnp.float32)
        acc = jnp.zeros((192, 128), jnp.float32)
        for s in range(BAG):
            left = hi[s : s + 1, :] == iota((64, 256), 0)
            planes = jnp.concatenate(
                [
                    jnp.where(left, low[s : s + 1, :], 0.0),
                    jnp.where(left, high[s : s + 1, :], 0.0),
                    jnp.where(left, bag, 0.0),
                ],
                axis=0,
            ).astype(jnp.bfloat16)
            right = ones_where(lo[s : s + 1, :] == iota((128, 256), 0))
            acc += lax.dot_general(
                planes, right, (((1,), (1,)), ((), ())), preferred_element_type=jnp.float32
            )
        acc = acc.astype(jnp.int32)
        code = acc[:64] | (acc[64:128] << 8) | (acc[128:] << BAG_SHIFT)
        out_ref[:, 4 * t : 4 * t + 4, :] = code.reshape(OWNERS, 4, 128)
    out_ref[:, 20:, :] = jnp.zeros((OWNERS, 4, 128), jnp.int32)


def pool_kernel(first, rows_ref, count_ref, bags_ref, table_ref, out_ref, buf_ref, held_ref, sem):
    tables = held_ref.shape[0]
    turn, step = pl.program_id(0), pl.program_id(1)

    def load(t):
        return pltpu.make_async_copy(table_ref.at[first + t], held_ref.at[t], sem.at[t])

    @pl.when((turn == 0) & (step == 0))
    def _():
        for t in range(tables):
            load(t).start()
        buf_ref[...] = jnp.zeros_like(buf_ref)

    for t in range(tables):

        @pl.when((turn == t) & (step == 0))
        def _(t=t):
            load(t).wait()

    for q in range(STEP):
        source = (turn * (OWNERS // STEP) + step) * STEP + q
        start = pl.multiple_of(source * CAP, CAP)

        def fetch(group, carry, start=start, q=q):
            base = pl.multiple_of(group * UNROLL, UNROLL)
            for k in range(UNROLL):
                row = rows_ref[start + base + k]
                buf_ref[q, pl.ds(base + k, 1), :] = held_ref[turn, pl.ds(row, 1), :]
            return carry

        lax.fori_loop(0, (count_ref[source] + UNROLL - 1) // UNROLL, fetch, 0)
    for q in range(STEP):
        pick = ones_where(bags_ref[q : q + 1, :] == iota((SAMPLES, CAP), 0))
        out_ref[q] = jnp.dot(
            pick, buf_ref[q].astype(jnp.bfloat16), preferred_element_type=jnp.float32
        ).astype(out_ref.dtype)


def pool_tables(first, tables, rows, counts, bags, table):
    steps = OWNERS // STEP
    return pl.pallas_call(
        functools.partial(pool_kernel, first),
        grid_spec=pltpu.PrefetchScalarGridSpec(
            num_scalar_prefetch=2,
            grid=(tables, steps),
            in_specs=[
                pl.BlockSpec((None, STEP, CAP), lambda t, i, *_: (t * steps + i, 0, 0)),
                pl.BlockSpec(memory_space=pltpu.HBM),
            ],
            out_specs=pl.BlockSpec((STEP, SAMPLES, EMB), lambda t, i, *_: (i, 0, t)),
            scratch_shapes=[
                pltpu.VMEM((STEP, CAP, EMB), jnp.float32),
                pltpu.VMEM((tables, ROWS_DEV, EMB), jnp.float32),
                pltpu.SemaphoreType.DMA((tables,)),
            ],
        ),
        out_shape=jax.ShapeDtypeStruct((OWNERS, SAMPLES, tables * EMB), jnp.bfloat16),
        compiler_params=pltpu.CompilerParams(vmem_limit_bytes=54 << 20),
        cost_estimate=pl.CostEstimate(
            flops=10_000_000_000 * tables, transcendentals=0, bytes_accessed=6_000_000
        ),
    )(rows.reshape(-1), counts.reshape(-1), bags.reshape(tables * steps, STEP, CAP), table)


def score_kernel(pieces, chunks, *refs):
    features = refs[:chunks]
    biases = refs[chunks : chunks + pieces]
    w_in = refs[chunks + pieces : chunks + 2 * pieces]
    w_out = refs[chunks + 2 * pieces : chunks + 3 * pieces]
    out_ref, in_buf, out_buf, in_sem, out_sem = refs[chunks + 3 * pieces :]
    copies = []
    for p in range(pieces):
        first = pltpu.make_async_copy(w_in[p], in_buf.at[p], in_sem.at[p])
        second = pltpu.make_async_copy(w_out[p], out_buf.at[p], out_sem.at[p])
        first.start()
        second.start()
        copies.append((first, second))
    total = None
    for p in range(pieces):
        copies[p][0].wait()
        pre = biases[p][...]
        base = 0
        for feature in features:
            width = feature.shape[1]
            pre = pre + jnp.dot(
                feature[...],
                in_buf[p, base : base + width, :],
                preferred_element_type=jnp.float32,
            )
            base += width
        hidden = jnp.maximum(pre, 0.0).astype(jnp.bfloat16)
        copies[p][1].wait()
        part = jnp.dot(hidden, out_buf[p], preferred_element_type=jnp.float32)
        total = part if total is None else total + part
    out_ref[...] = total.astype(out_ref.dtype)


def score(features, biases, w_in, w_out, dtype):
    pieces, chunks = len(w_in), len(features)
    vmem = pl.BlockSpec(memory_space=pltpu.VMEM)
    hbm = pl.BlockSpec(memory_space=pltpu.HBM)
    return pl.pallas_call(
        functools.partial(score_kernel, pieces, chunks),
        in_specs=[vmem] * (chunks + pieces) + [hbm] * (2 * pieces),
        out_specs=vmem,
        scratch_shapes=[
            pltpu.VMEM((pieces, *w_in[0].shape), jnp.bfloat16),
            pltpu.VMEM((pieces, *w_out[0].shape), jnp.bfloat16),
            pltpu.SemaphoreType.DMA((pieces,)),
            pltpu.SemaphoreType.DMA((pieces,)),
        ],
        out_shape=jax.ShapeDtypeStruct((SAMPLES, w_out[0].shape[1]), dtype),
        compiler_params=pltpu.CompilerParams(vmem_limit_bytes=40 << 20),
        cost_estimate=pl.CostEstimate(
            flops=10_000_000_000, transcendentals=0, bytes_accessed=14_000_000
        ),
    )(*features, *biases, *w_in, *w_out)


def to_chip(array, target):
    return lax.ppermute(
        array, "gy", [(x * 2 + c, target(x) * 2 + c) for x in range(4) for c in range(2)]
    )


def to_core(array):
    return lax.ppermute(array, "gy", [(k, k ^ 1) for k in range(8)])


def local(table, lookup_owner, lookup_row, bag_length, top_in, top_bias, top_out):
    own = (top_in, top_bias.reshape(1, -1), top_out)
    far = []
    for array in own:
        far.append(to_chip(array, lambda x: 3 - x))
    near = [to_core(array) for array in own]
    far_near = [to_core(array) for array in far]
    w_in, biases, w_out = zip(own, near, far, far_near)

    owner = jnp.transpose(lookup_owner[..., 0], (0, 2, 1))
    live = jnp.arange(BAG, dtype=jnp.int32)[None, :, None] < bag_length[:, None, :]
    owner = jnp.where(live, owner, OWNERS)
    row = jnp.transpose(lookup_row, (0, 2, 1))
    codes = pl.pallas_call(
        dispatch_kernel,
        out_shape=jax.ShapeDtypeStruct((OWNERS, 24, 128), jnp.int32),
        name="dispatch",
    )(owner, row)
    codes = lax.all_to_all(codes, "gx", 0, 0, tiled=True)
    counts = codes[:, 16:20, 0].T
    codes = jnp.transpose(codes[:, :16, :].reshape(OWNERS, TABLES, CAP), (1, 0, 2))
    rows = (codes & (ROWS_DEV - 1)).reshape(TABLES, OWNERS * CAP)
    bags = jnp.where((codes & VALID) != 0, codes >> BAG_SHIFT, SAMPLES)

    mine, theirs = [], []
    first = 0
    for number in CHUNKS:
        part = slice(first, first + number)
        share = pool_tables(first, number, rows[part], counts[part], bags[part], table)
        first += number
        share = lax.all_to_all(share, "gx", 0, 0, tiled=True)
        chunk = jnp.sum(share.astype(jnp.float32), axis=0).astype(jnp.bfloat16)
        mine.append(chunk)
        theirs.append(to_chip(chunk, lambda x: x ^ 1))
    kept = score(mine, biases, w_in, w_out, jnp.float32)
    sent = score(theirs, biases, w_in, w_out, jnp.bfloat16)
    received = to_chip(sent, lambda x: x ^ 1)
    return (kept + received.astype(jnp.float32)).astype(jnp.bfloat16)


def solution(mesh):
    return jax.shard_map(
        local,
        mesh=mesh,
        in_specs=(
            P(None, "gx", None),
            P(None, ("gx", "gy"), None, None),
            P(None, ("gx", "gy"), None),
            P(None, ("gx", "gy")),
            P(None, "gy"),
            P("gy"),
            P("gy", None),
        ),
        out_specs=P(("gx", "gy"), None),
        check_vma=False,
    )
```

profile of v0, /device:TPU:1, one launch (start us, length us, event | category | flops | bytes accessed | tf_op | source)
XLA Modules:
  0.0 144.3 jit_solution(8535791659011147773)
XLA Ops:
  0.0 1.5 %bitcast_select_fusion.own_ref = s32[4,16,256]{2,1,0:T(8,128)} fusion(s32[4,256,16,1]{1,3,2,0:T(1,128)} %param.8, s32[4,256]{1,0:T(4,128)} %param.10), kind=kLoop, calls=%fused_computation.6 | loop fusion | flops 32768 | bytes 135168 | tf_op jit(solution)/shard_map/jit(_where)/select_n | solution.py:218
  1.5 4.5 %dispatch.1 = s32[16,24,128]{2,1,0:T(8,128)} custom-call(s32[4,16,256]{2,1,0:T(8,128)} %bitcast_select_fusion.own_ref, s32[4,16,256]{2,1,0:T(8,128)} %bitcast.27), custom_call_target="tpu_custom_call" | custom-call | tf_op jit(solution)/shard_map/dispatch/pallas_call | solution.py:220
  5.9 8.6 %all-to-all-start = ((s32[16,24,128]{2,1,0:T(8,128)}), s32[16,24,128]{2,1,0:T(8,128)S(1)}, u32[]{:S(2)}, u32[]{:S(2)}) async-start(s32[16,24,128]{2,1,0:T(8,128)} %dispatch.1), calls=%async_computation | async-start | bytes 393216 | tf_op jit(solution)/shard_map/all_to_all | solution.py:225
  14.5 2.6 %collective-permute-start.7 = (bf16[1024,1024]{1,0:T(8,128)(2,1)}, bf16[1024,1024]{1,0:T(8,128)(2,1)}, u32[]{:S(2)}, u32[]{:S(2)}) collective-permute-start(bf16[1024,1024]{1,0:T(8,128)(2,1)} %refs_10_.3), channel_id=1, source_target_pairs={{0,6},{1,7},{2,4},{3,5},{4,2},{5,3},{6,0},{7,1},{8,14},{9,15},{10,... | collective-permute-start | bytes 6291464 | tf_op jit(solution)/shard_map/ppermute | solution.py:198
  17.1 4.6 %all-to-all-done = s32[16,24,128]{2,1,0:T(8,128)S(1)} async-done(((s32[16,24,128]{2,1,0:T(8,128)}), s32[16,24,128]{2,1,0:T(8,128)S(1)}, u32[]{:S(2)}, u32[]{:S(2)}) %all-to-all-start) | async-done | bytes 196640 | tf_op jit(solution)/shard_map/all_to_all | solution.py:225
  21.7 0.1 copy.11
  21.8 0.6 reshape.39.count_ref
  22.6 0.6 reshape.40.bags_ref
  23.3 0.6 copy.14
  24.0 21.0 %shard_map.73 = bf16[16,256,256]{2,1,0:T(8,128)(2,1)} custom-call(s32[16384]{0:T(1024)} %bitcast.28, s32[32]{0:T(128)} %reshape.39.count_ref, s32[8,4,512]{2,1,0:T(4,128)} %reshape.40.bags_ref, f32[4,8192,128]{2,1,0:T(8,128)} %table_ref.3), custom_call_target="tpu_custom_call" | custom-call | flops 20000000000 | bytes 6000000 | tf_op jit(solution)/shard_map/pallas_call | solution.py:118
  45.0 4.4 %all-to-all-start.1 = ((bf16[16,256,256]{2,1,0:T(8,128)(2,1)}), bf16[16,256,256]{2,1,0:T(8,128)(2,1)}, u32[]{:S(2)}, u32[]{:S(2)}) async-start(bf16[16,256,256]{2,1,0:T(8,128)(2,1)} %shard_map.73), calls=%async_computation.1 | async-start | bytes 4194304 | tf_op jit(solution)/shard_map/all_to_all | solution.py:237
  49.4 0.6 reshape.42.count_ref
  50.0 0.6 reshape.43.bags_ref
  50.7 0.6 copy.15
  51.3 20.5 %shard_map.74 = bf16[16,256,256]{2,1,0:T(8,128)(2,1)} custom-call(s32[16384]{0:T(1024)} %bitcast.29, s32[32]{0:T(128)} %reshape.42.count_ref, s32[8,4,512]{2,1,0:T(4,128)} %reshape.43.bags_ref, f32[4,8192,128]{2,1,0:T(8,128)} %table_ref.3), custom_call_target="tpu_custom_call" | custom-call | flops 20000000000 | bytes 6000000 | tf_op jit(solution)/shard_map/pallas_call | solution.py:118
  71.8 0.0 copy-start.1
  71.8 0.0 copy-start
  71.8 0.0 copy-start.2
  71.8 3.4 %all-to-all-done.1 = bf16[16,256,256]{2,1,0:T(8,128)(2,1)} async-done(((bf16[16,256,256]{2,1,0:T(8,128)(2,1)}), bf16[16,256,256]{2,1,0:T(8,128)(2,1)}, u32[]{:S(2)}, u32[]{:S(2)}) %all-to-all-start.1) | async-done | bytes 2097184 | tf_op jit(solution)/shard_map/all_to_all | solution.py:237
  75.3 5.2 %all-to-all-start.2 = ((bf16[16,256,256]{2,1,0:T(8,128)(2,1)}), bf16[16,256,256]{2,1,0:T(8,128)(2,1)}, u32[]{:S(2)}, u32[]{:S(2)}) async-start(bf16[16,256,256]{2,1,0:T(8,128)(2,1)} %shard_map.74), calls=%async_computation.2 | async-start | bytes 4194304 | tf_op jit(solution)/shard_map/all_to_all | solution.py:237
  80.5 0.0 copy-done.1
  80.5 2.2 %collective-permute-start.4 = (bf16[512,1024]{1,0:T(8,128)(2,1)S(1)}, bf16[512,1024]{1,0:T(8,128)(2,1)}, u32[]{:S(2)}, u32[]{:S(2)}) collective-permute-start(bf16[512,1024]{1,0:T(8,128)(2,1)S(1)} %copy-done.1), channel_id=1, source_target_pairs={{0,6},{1,7},{2,4},{3,5},{4,2},{5,3},{6,0},{7,1},{8,14},{9,15},{10,... | collective-permute-start | bytes 3145736 | tf_op jit(solution)/shard_map/ppermute | solution.py:198
  82.7 0.0 copy-done
  82.7 4.2 %collective-permute-start.6 = (bf16[1024,1024]{1,0:T(8,128)(2,1)S(1)}, bf16[1024,1024]{1,0:T(8,128)(2,1)}, u32[]{:S(2)}, u32[]{:S(2)}) collective-permute-start(bf16[1024,1024]{1,0:T(8,128)(2,1)S(1)} %copy-done), channel_id=1, source_target_pairs={{0,1},{1,0},{2,3},{3,2},{4,5},{5,4},{6,7},{7,6},{8,9},{9,8},{10,11... | collective-permute-start | bytes 6291464 | tf_op jit(solution)/shard_map/ppermute | solution.py:204
  86.9 0.0 collective-permute-done.7.refs_12_
  86.9 0.1 collective-permute-start.8
  87.0 0.4 collective-permute-start.3
  87.4 15.2 %collective-permute-done.4.refs_8_ = bf16[512,1024]{1,0:T(8,128)(2,1)} collective-permute-done((bf16[512,1024]{1,0:T(8,128)(2,1)S(1)}, bf16[512,1024]{1,0:T(8,128)(2,1)}, u32[]{:S(2)}, u32[]{:S(2)}) %collective-permute-start.4) | collective-permute-done | bytes 1048608 | tf_op jit(solution)/shard_map/ppermute | solution.py:198
  102.6 4.9 %collective-permute-start.5 = (bf16[512,1024]{1,0:T(8,128)(2,1)}, bf16[512,1024]{1,0:T(8,128)(2,1)}, u32[]{:S(2)}, u32[]{:S(2)}) collective-permute-start(bf16[512,1024]{1,0:T(8,128)(2,1)} %collective-permute-done.4.refs_8_), channel_id=1, source_target_pairs={{0,1},{1,0},{2,3},{3,2},{4,5},{5,4},{6,7},{7,6},{8,9},{9,8},{10,11... | collective-permute-start | bytes 3145736 | tf_op jit(solution)/shard_map/ppermute | solution.py:204
  107.5 0.0 copy-done.2
  107.5 2.1 %collective-permute-start.1 = (f32[1,1024]{1,0:T(1,128)S(1)}, f32[1,1024]{1,0:T(1,128)S(1)}, u32[]{:S(2)}, u32[]{:S(2)}) collective-permute-start(f32[1,1024]{1,0:T(1,128)S(1)} %bitcast.19), channel_id=1, source_target_pairs={{0,6},{1,7},{2,4},{3,5},{4,2},{5,3},{6,0},{7,1},{8,14},{9,15},{10,... | collective-permute-start | bytes 12296 | tf_op jit(solution)/shard_map/ppermute | solution.py:198
  109.6 1.6 %collective-permute-done.1.refs_4_ = f32[1,1024]{1,0:T(1,128)S(1)} collective-permute-done((f32[1,1024]{1,0:T(1,128)S(1)}, f32[1,1024]{1,0:T(1,128)S(1)}, u32[]{:S(2)}, u32[]{:S(2)}) %collective-permute-start.1) | collective-permute-done | bytes 4128 | tf_op jit(solution)/shard_map/ppermute | solution.py:198
  111.2 1.2 collective-permute-start
  112.3 0.8 collective-permute-done.refs_3_
  113.1 0.3 collective-permute-start.2
  113.5 1.9 %reduce_sum.24.refs_0_ = bf16[256,256]{1,0:T(8,128)(2,1)S(1)} reduce(bf16[16,256,256]{2,1,0:T(8,128)(2,1)} %all-to-all-done.1, bf16[]{:T(256)} %constant.15.clone.1), dimensions={0}, to_apply=%region_0.1 | reduce | flops 983040 | bytes 2228226 | tf_op jit(solution)/shard_map/reduce_sum | solution.py:238
  115.4 0.0 all-to-all-done.2
  115.4 1.9 %reduce_sum.25.refs_1_ = bf16[256,256]{1,0:T(8,128)(2,1)S(1)} reduce(bf16[16,256,256]{2,1,0:T(8,128)(2,1)} %all-to-all-done.2, bf16[]{:T(256)} %constant.15.clone.1), dimensions={0}, to_apply=%region_1.2 | reduce | flops 983040 | bytes 2228226 | tf_op jit(solution)/shard_map/reduce_sum | solution.py:238
  117.3 0.0 collective-permute-done.2.refs_5_
  117.3 0.1 collective-permute-start.9
  117.4 0.0 collective-permute-done.3.refs_7_
  117.4 1.4 %collective-permute-start.10 = (bf16[256,256]{1,0:T(8,128)(2,1)S(1)}, bf16[256,256]{1,0:T(8,128)(2,1)S(1)}, u32[]{:S(2)}, u32[]{:S(2)}) collective-permute-start(bf16[256,256]{1,0:T(8,128)(2,1)S(1)} %reduce_sum.25.refs_1_), channel_id=1, source_target_pairs={{0,2},{1,3},{2,0},{3,1},{4,6},{5,7},{6,4},{7,5},{8,10},{9,11},{10,... | collective-permute-start | bytes 393224 | tf_op jit(solution)/shard_map/ppermute | solution.py:198
  118.8 0.0 collective-permute-done.5.refs_9_
  118.8 0.0 collective-permute-done.6.refs_11_
  118.8 3.4 %collective-permute-done.9.refs_0_ = bf16[256,256]{1,0:T(8,128)(2,1)S(1)} collective-permute-done((bf16[256,256]{1,0:T(8,128)(2,1)S(1)}, bf16[256,256]{1,0:T(8,128)(2,1)S(1)}, u32[]{:S(2)}, u32[]{:S(2)}) %collective-permute-start.9) | collective-permute-done | bytes 131104 | tf_op jit(solution)/shard_map/ppermute | solution.py:198
  122.3 2.8 %collective-permute-done.10.refs_1_ = bf16[256,256]{1,0:T(8,128)(2,1)S(1)} collective-permute-done((bf16[256,256]{1,0:T(8,128)(2,1)S(1)}, bf16[256,256]{1,0:T(8,128)(2,1)S(1)}, u32[]{:S(2)}, u32[]{:S(2)}) %collective-permute-start.10) | collective-permute-done | bytes 131104 | tf_op jit(solution)/shard_map/ppermute | solution.py:198
  125.1 0.0 collective-permute-done.8.refs_13_
  125.1 5.5 %shard_map.76 = bf16[256,1024]{1,0:T(8,128)(2,1)S(1)} custom-call(bf16[256,256]{1,0:T(8,128)(2,1)S(1)} %collective-permute-done.9.refs_0_, bf16[256,256]{1,0:T(8,128)(2,1)S(1)} %collective-permute-done.10.refs_1_, f32[1,1024]{1,0:T(1,128)S(1)} %bitcast.21, f32[1,1024]{1,0:T(1,128)S(1)} %collective-permute-done.refs_3_, ...), custom_call_target="tpu_custom_call" | custom-call | flops 10000000000 | bytes 14000000 | tf_op jit(solution)/shard_map/pallas_call | solution.py:179
  130.6 0.5 collective-permute-start.11
  131.1 5.5 %shard_map.75 = f32[256,1024]{1,0:T(8,128)S(1)} custom-call(bf16[256,256]{1,0:T(8,128)(2,1)S(1)} %reduce_sum.24.refs_0_, bf16[256,256]{1,0:T(8,128)(2,1)S(1)} %reduce_sum.25.refs_1_, f32[1,1024]{1,0:T(1,128)S(1)} %bitcast.22, f32[1,1024]{1,0:T(1,128)S(1)} %collective-permute-done.refs_3_, f32[1,1024]{1,0:T(1,128)S(1)} %collective-permute-done.1.refs_4_, ...), custom_call_target="tpu_custom_call" | custom-call | flops 10000000000 | bytes 14000000 | tf_op jit(solution)/shard_map/pallas_call | solution.py:179
  136.7 6.6 %collective-permute-done.11 = bf16[256,1024]{1,0:T(8,128)(2,1)S(1)} collective-permute-done((bf16[256,1024]{1,0:T(8,128)(2,1)S(1)}, bf16[256,1024]{1,0:T(8,128)(2,1)S(1)}, u32[]{:S(2)}, u32[]{:S(2)}) %collective-permute-start.11) | collective-permute-done | bytes 524320 | tf_op jit(solution)/shard_map/ppermute | solution.py:198
  143.3 0.9 add_convert_fusion
  (9 shorter events, 0.2 us)
Async XLA Ops:
  5.9 15.7 %all-to-all-start = ((s32[16,24,128]{2,1,0:T(8,128)}), s32[16,24,128]{2,1,0:T(8,128)S(1)}, u32[]{:S(2)}, u32[]{:S(2)}) async-start(s32[16,24,128]{2,1,0:T(8,128)} %dispatch.1), calls=%async_computation | async-start | bytes 393216 | tf_op jit(solution)/shard_map/all_to_all | solution.py:225
  14.5 72.4 %collective-permute-start.7 = (bf16[1024,1024]{1,0:T(8,128)(2,1)}, bf16[1024,1024]{1,0:T(8,128)(2,1)}, u32[]{:S(2)}, u32[]{:S(2)}) collective-permute-start(bf16[1024,1024]{1,0:T(8,128)(2,1)} %refs_10_.3), channel_id=1, source_target_pairs={{0,6},{1,7},{2,4},{3,5},{4,2},{5,3},{6,0},{7,1},{8,14},{9,15},{10,... | collective-permute-start | bytes 6291464 | tf_op jit(solution)/shard_map/ppermute | solution.py:198
  45.0 30.3 %all-to-all-start.1 = ((bf16[16,256,256]{2,1,0:T(8,128)(2,1)}), bf16[16,256,256]{2,1,0:T(8,128)(2,1)}, u32[]{:S(2)}, u32[]{:S(2)}) async-start(bf16[16,256,256]{2,1,0:T(8,128)(2,1)} %shard_map.73), calls=%async_computation.1 | async-start | bytes 4194304 | tf_op jit(solution)/shard_map/all_to_all | solution.py:237
  71.8 8.7 %copy-start.1 = (bf16[512,1024]{1,0:T(8,128)(2,1)S(1)}, bf16[512,1024]{1,0:T(8,128)(2,1)}, u32[]{:S(2)}) copy-start(bf16[512,1024]{1,0:T(8,128)(2,1)} %refs_6_.3) | copy-start | bytes 3145732
  71.8 10.9 %copy-start = (bf16[1024,1024]{1,0:T(8,128)(2,1)S(1)}, bf16[1024,1024]{1,0:T(8,128)(2,1)}, u32[]{:S(2)}) copy-start(bf16[1024,1024]{1,0:T(8,128)(2,1)} %refs_10_.3) | copy-start | bytes 6291460
  71.8 35.7 %copy-start.2 = (f32[1024]{0:T(1024)S(1)}, f32[1024]{0:T(1024)}, u32[]{:S(2)}) copy-start(f32[1024]{0:T(1024)} %param.12) | copy-start | bytes 12292
  75.3 40.1 %all-to-all-start.2 = ((bf16[16,256,256]{2,1,0:T(8,128)(2,1)}), bf16[16,256,256]{2,1,0:T(8,128)(2,1)}, u32[]{:S(2)}, u32[]{:S(2)}) async-start(bf16[16,256,256]{2,1,0:T(8,128)(2,1)} %shard_map.74), calls=%async_computation.2 | async-start | bytes 4194304 | tf_op jit(solution)/shard_map/all_to_all | solution.py:237
  80.5 22.1 %collective-permute-start.4 = (bf16[512,1024]{1,0:T(8,128)(2,1)S(1)}, bf16[512,1024]{1,0:T(8,128)(2,1)}, u32[]{:S(2)}, u32[]{:S(2)}) collective-permute-start(bf16[512,1024]{1,0:T(8,128)(2,1)S(1)} %copy-done.1), channel_id=1, source_target_pairs={{0,6},{1,7},{2,4},{3,5},{4,2},{5,3},{6,0},{7,1},{8,14},{9,15},{10,... | collective-permute-start | bytes 3145736 | tf_op jit(solution)/shard_map/ppermute | solution.py:198
  82.7 36.2 %collective-permute-start.6 = (bf16[1024,1024]{1,0:T(8,128)(2,1)S(1)}, bf16[1024,1024]{1,0:T(8,128)(2,1)}, u32[]{:S(2)}, u32[]{:S(2)}) collective-permute-start(bf16[1024,1024]{1,0:T(8,128)(2,1)S(1)} %copy-done), channel_id=1, source_target_pairs={{0,1},{1,0},{2,3},{3,2},{4,5},{5,4},{6,7},{7,6},{8,9},{9,8},{10,11... | collective-permute-start | bytes 6291464 | tf_op jit(solution)/shard_map/ppermute | solution.py:204
  86.9 38.2 %collective-permute-start.8 = (bf16[1024,1024]{1,0:T(8,128)(2,1)}, bf16[1024,1024]{1,0:T(8,128)(2,1)}, u32[]{:S(2)}, u32[]{:S(2)}) collective-permute-start(bf16[1024,1024]{1,0:T(8,128)(2,1)} %collective-permute-done.7.refs_12_), channel_id=1, source_target_pairs={{0,1},{1,0},{2,3},{3,2},{4,5},{5,4},{6,7},{7,6},{8,9},{9,8},{10,11... | collective-permute-start | bytes 6291464 | tf_op jit(solution)/shard_map/ppermute | solution.py:204
  87.0 30.4 %collective-permute-start.3 = (bf16[512,1024]{1,0:T(8,128)(2,1)S(1)}, bf16[512,1024]{1,0:T(8,128)(2,1)}, u32[]{:S(2)}, u32[]{:S(2)}) collective-permute-start(bf16[512,1024]{1,0:T(8,128)(2,1)S(1)} %copy-done.1), channel_id=1, source_target_pairs={{0,1},{1,0},{2,3},{3,2},{4,5},{5,4},{6,7},{7,6},{8,9},{9,8},{10,11... | collective-permute-start | bytes 3145736 | tf_op jit(solution)/shard_map/ppermute | solution.py:204
  102.6 16.3 %collective-permute-start.5 = (bf16[512,1024]{1,0:T(8,128)(2,1)}, bf16[512,1024]{1,0:T(8,128)(2,1)}, u32[]{:S(2)}, u32[]{:S(2)}) collective-permute-start(bf16[512,1024]{1,0:T(8,128)(2,1)} %collective-permute-done.4.refs_8_), channel_id=1, source_target_pairs={{0,1},{1,0},{2,3},{3,2},{4,5},{5,4},{6,7},{7,6},{8,9},{9,8},{10,11... | collective-permute-start | bytes 3145736 | tf_op jit(solution)/shard_map/ppermute | solution.py:204
  107.5 3.7 %collective-permute-start.1 = (f32[1,1024]{1,0:T(1,128)S(1)}, f32[1,1024]{1,0:T(1,128)S(1)}, u32[]{:S(2)}, u32[]{:S(2)}) collective-permute-start(f32[1,1024]{1,0:T(1,128)S(1)} %bitcast.19), channel_id=1, source_target_pairs={{0,6},{1,7},{2,4},{3,5},{4,2},{5,3},{6,0},{7,1},{8,14},{9,15},{10,... | collective-permute-start | bytes 12296 | tf_op jit(solution)/shard_map/ppermute | solution.py:198
  111.2 2.0 %collective-permute-start = (f32[1,1024]{1,0:T(1,128)S(1)}, f32[1,1024]{1,0:T(1,128)S(1)}, u32[]{:S(2)}, u32[]{:S(2)}) collective-permute-start(f32[1,1024]{1,0:T(1,128)S(1)} %bitcast.20), channel_id=1, source_target_pairs={{0,1},{1,0},{2,3},{3,2},{4,5},{5,4},{6,7},{7,6},{8,9},{9,8},{10,11... | collective-permute-start | bytes 12296 | tf_op jit(solution)/shard_map/ppermute | solution.py:204
  113.1 4.1 %collective-permute-start.2 = (f32[1,1024]{1,0:T(1,128)S(1)}, f32[1,1024]{1,0:T(1,128)S(1)}, u32[]{:S(2)}, u32[]{:S(2)}) collective-permute-start(f32[1,1024]{1,0:T(1,128)S(1)} %collective-permute-done.1.refs_4_), channel_id=1, source_target_pairs={{0,1},{1,0},{2,3},{3,2},{4,5},{5,4},{6,7},{7,6},{8,9},{9,8},{10,11... | collective-permute-start | bytes 12296 | tf_op jit(solution)/shard_map/ppermute | solution.py:204
  117.3 5.0 %collective-permute-start.9 = (bf16[256,256]{1,0:T(8,128)(2,1)S(1)}, bf16[256,256]{1,0:T(8,128)(2,1)S(1)}, u32[]{:S(2)}, u32[]{:S(2)}) collective-permute-start(bf16[256,256]{1,0:T(8,128)(2,1)S(1)} %reduce_sum.24.refs_0_), channel_id=1, source_target_pairs={{0,2},{1,3},{2,0},{3,1},{4,6},{5,7},{6,4},{7,5},{8,10},{9,11},{10,... | collective-permute-start | bytes 393224 | tf_op jit(solution)/shard_map/ppermute | solution.py:198
  117.4 7.7 %collective-permute-start.10 = (bf16[256,256]{1,0:T(8,128)(2,1)S(1)}, bf16[256,256]{1,0:T(8,128)(2,1)S(1)}, u32[]{:S(2)}, u32[]{:S(2)}) collective-permute-start(bf16[256,256]{1,0:T(8,128)(2,1)S(1)} %reduce_sum.25.refs_1_), channel_id=1, source_target_pairs={{0,2},{1,3},{2,0},{3,1},{4,6},{5,7},{6,4},{7,5},{8,10},{9,11},{10,... | collective-permute-start | bytes 393224 | tf_op jit(solution)/shard_map/ppermute | solution.py:198
  130.6 12.7 %collective-permute-start.11 = (bf16[256,1024]{1,0:T(8,128)(2,1)S(1)}, bf16[256,1024]{1,0:T(8,128)(2,1)S(1)}, u32[]{:S(2)}, u32[]{:S(2)}) collective-permute-start(bf16[256,1024]{1,0:T(8,128)(2,1)S(1)} %shard_map.76), channel_id=1, source_target_pairs={{0,2},{1,3},{2,0},{3,1},{4,6},{5,7},{6,4},{7,5},{8,10},{9,11},{10,... | collective-permute-start | bytes 1572872 | tf_op jit(solution)/shard_map/ppermute | solution.py:198
where the time goes:
time: 145 us; the launch traced here: 144 us
  Pallas kernels  57 us (39%)
  waiting for transfers between devices  38.5 us (27%)
  starting transfers between devices  38.2 us (26%)
  other arithmetic  6.21 us (4%)
  local copies, waits for them, and re-layouts  4.17 us (3%)
    pallas_call x2, Pallas kernels, pool_tables(): pl.pallas_call(functools.partial(pool_kernel, first), grid_spec=pltpu.Pre...  41.5 us
    ppermute x6, waiting for transfers between devices, to_chip(): lax.ppermute(array, 'gy', [(x * 2 + c, target(x) * 2 + c) for x in range(...  29.6 us
    ppermute x6, starting transfers between devices, to_core(): return lax.ppermute(array, 'gy', [(k, k ^ 1) for k in range(8)])  11.1 us
    pallas_call x2, Pallas kernels, score(): pl.pallas_call(functools.partial(score_kernel, pieces, chunks), in_specs=...  11 us
    all_to_all x2, starting transfers between devices, local(): share = lax.all_to_all(share, 'gx', 0, 0, tiled=True)  9.66 us
    ppermute x6, starting transfers between devices, to_chip(): lax.ppermute(array, 'gy', [(x * 2 + c, target(x) * 2 + c) for x in range(...  8.87 us
    all_to_all x1, starting transfers between devices, local(): codes = lax.all_to_all(codes, 'gx', 0, 0, tiled=True)  8.59 us
    all_to_all x1, waiting for transfers between devices, local(): codes = lax.all_to_all(codes, 'gx', 0, 0, tiled=True)  4.58 us
  transfers between devices with their start and end apart: 15, of which 8 were waited for; matrix products, arithmetic and copies ran while one was open for 6% of the time, Pallas kernels for 33%

commit v1 on v0

--- a/solution.py
+++ b/solution.py
@@ -15,10 +15,10 @@
 CAP = 512
 ROWS_DEV = 8192
 EMB = 128
-UNROLL = 16
-STEP = 4
-VALID = 1 << 13
-BAG_SHIFT = 14
+BLOCK = 64
+PIECES = 4
+STEP = 8
+BAG_SHIFT = 13
 CHUNKS = (2, 2)
 
 
@@ -52,8 +52,8 @@
         lo = rank & 127
         row = row_ref[t]
         low = (row & 255).astype(jnp.float32)
-        high = ((row >> 8) + (VALID >> 8)).astype(jnp.float32)
-        bag = iota((1, 256), 1).astype(jnp.float32)
+        high = (row >> 8).astype(jnp.float32)
+        bag = (iota((1, 256), 1) + 1).astype(jnp.float32)
         acc = jnp.zeros((192, 128), jnp.float32)
         for s in range(BAG):
             left = hi[s : s + 1, :] == iota((64, 256), 0)
@@ -75,68 +75,92 @@
     out_ref[:, 20:, :] = jnp.zeros((OWNERS, 4, 128), jnp.int32)
 
 
-def pool_kernel(first, rows_ref, count_ref, bags_ref, table_ref, out_ref, buf_ref, held_ref, sem):
+def pool_kernel(first, lists_ref, table_ref, out_ref, buf_ref, held_ref, rows_vmem, rows_ref, sem, row_sem):
     tables = held_ref.shape[0]
-    turn, step = pl.program_id(0), pl.program_id(1)
-
-    def load(t):
-        return pltpu.make_async_copy(table_ref.at[first + t], held_ref.at[t], sem.at[t])
-
-    @pl.when((turn == 0) & (step == 0))
+    turn, part = pl.program_id(0), pl.program_id(1)
+
+    def load(t, k):
+        piece = pl.ds(k * (ROWS_DEV // PIECES), ROWS_DEV // PIECES)
+        return pltpu.make_async_copy(
+            table_ref.at[first + t, piece], held_ref.at[t, piece], sem.at[t, k]
+        )
+
+    def load_rows():
+        return pltpu.make_async_copy(rows_vmem, rows_ref, row_sem)
+
+    @pl.when((turn == 0) & (part == 0))
     def _():
         for t in range(tables):
-            load(t).start()
+            for k in range(PIECES):
+                load(t, k).start()
+        codes = lists_ref[:, 4 * first : 4 * (first + tables), :]
+        rows_vmem[:, : 4 * tables, :] = codes & (ROWS_DEV - 1)
+        rows_vmem[:, 4 * tables : 5 * tables, :] = lists_ref[:, 16 + first : 16 + first + tables, :]
+        load_rows().start()
         buf_ref[...] = jnp.zeros_like(buf_ref)
+        load_rows().wait()
 
     for t in range(tables):
 
-        @pl.when((turn == t) & (step == 0))
+        @pl.when((turn == t) & (part == 0))
         def _(t=t):
-            load(t).wait()
-
+            for k in range(PIECES):
+                load(t, k).wait()
+
+    def fetch(q, carry):
+        source = part * STEP + q
+        count = rows_ref[source, 4 * tables + turn, 0]
+        for line in range(CAP // 128):
+            for base in range(0, 128, BLOCK):
+
+                @pl.when(count > line * 128 + base)
+                def _(line=line, base=base):
+                    for k in range(base, base + BLOCK):
+                        row = rows_ref[source, 4 * turn + line, k]
+                        buf_ref[q, pl.ds(line * 128 + k, 1), :] = held_ref[turn, pl.ds(row, 1), :]
+
+        return carry
+
+    lax.fori_loop(0, STEP, fetch, 0)
+    bag = (iota((SAMPLES, 128), 0) + 1).astype(jnp.float32).astype(jnp.bfloat16)
     for q in range(STEP):
-        source = (turn * (OWNERS // STEP) + step) * STEP + q
-        start = pl.multiple_of(source * CAP, CAP)
-
-        def fetch(group, carry, start=start, q=q):
-            base = pl.multiple_of(group * UNROLL, UNROLL)
-            for k in range(UNROLL):
-                row = rows_ref[start + base + k]
-                buf_ref[q, pl.ds(base + k, 1), :] = held_ref[turn, pl.ds(row, 1), :]
-            return carry
-
-        lax.fori_loop(0, (count_ref[source] + UNROLL - 1) // UNROLL, fetch, 0)
-    for q in range(STEP):
-        pick = ones_where(bags_ref[q : q + 1, :] == iota((SAMPLES, CAP), 0))
+        source = part * STEP + q
+        picks = []
+        for line in range(CAP // 128):
+            named = lists_ref[source, pl.ds(4 * first + 4 * turn + line, 1), :] >> BAG_SHIFT
+            named = named.astype(jnp.float32).astype(jnp.bfloat16)
+            picks.append(jnp.where(named == bag, jnp.bfloat16(1), jnp.bfloat16(0)))
         out_ref[q] = jnp.dot(
-            pick, buf_ref[q].astype(jnp.bfloat16), preferred_element_type=jnp.float32
+            jnp.concatenate(picks, axis=1),
+            buf_ref[q].astype(jnp.bfloat16),
+            preferred_element_type=jnp.float32,
         ).astype(out_ref.dtype)
 
 
-def pool_tables(first, tables, rows, counts, bags, table):
-    steps = OWNERS // STEP
+def pool_tables(first, tables, lists, table):
+    width = -(-5 * tables // 8) * 8
     return pl.pallas_call(
         functools.partial(pool_kernel, first),
-        grid_spec=pltpu.PrefetchScalarGridSpec(
-            num_scalar_prefetch=2,
-            grid=(tables, steps),
-            in_specs=[
-                pl.BlockSpec((None, STEP, CAP), lambda t, i, *_: (t * steps + i, 0, 0)),
-                pl.BlockSpec(memory_space=pltpu.HBM),
-            ],
-            out_specs=pl.BlockSpec((STEP, SAMPLES, EMB), lambda t, i, *_: (i, 0, t)),
-            scratch_shapes=[
-                pltpu.VMEM((STEP, CAP, EMB), jnp.float32),
-                pltpu.VMEM((tables, ROWS_DEV, EMB), jnp.float32),
-                pltpu.SemaphoreType.DMA((tables,)),
-            ],
-        ),
+        grid=(tables, OWNERS // STEP),
+        in_specs=[
+            pl.BlockSpec(lists.shape, lambda t, i: (0, 0, 0)),
+            pl.BlockSpec(memory_space=pltpu.HBM),
+        ],
+        out_specs=pl.BlockSpec((STEP, SAMPLES, EMB), lambda t, i: (i, 0, t)),
+        scratch_shapes=[
+            pltpu.VMEM((STEP, CAP, EMB), jnp.float32),
+            pltpu.VMEM((tables, ROWS_DEV, EMB), jnp.float32),
+            pltpu.VMEM((OWNERS, width, 128), jnp.int32),
+            pltpu.SMEM((OWNERS, width, 128), jnp.int32),
+            pltpu.SemaphoreType.DMA((tables, PIECES)),
+            pltpu.SemaphoreType.DMA(()),
+        ],
         out_shape=jax.ShapeDtypeStruct((OWNERS, SAMPLES, tables * EMB), jnp.bfloat16),
-        compiler_params=pltpu.CompilerParams(vmem_limit_bytes=54 << 20),
+        compiler_params=pltpu.CompilerParams(vmem_limit_bytes=49 << 20),
         cost_estimate=pl.CostEstimate(
             flops=10_000_000_000 * tables, transcendentals=0, bytes_accessed=6_000_000
         ),
-    )(rows.reshape(-1), counts.reshape(-1), bags.reshape(tables * steps, STEP, CAP), table)
+    )(lists, table)
 
 
 def score_kernel(pieces, chunks, *refs):
@@ -194,10 +218,18 @@
     )(*features, *biases, *w_in, *w_out)
 
 
-def to_chip(array, target):
+def to_chip(array, targets):
     return lax.ppermute(
-        array, "gy", [(x * 2 + c, target(x) * 2 + c) for x in range(4) for c in range(2)]
+        array, "gy", [(x * 2 + c, targets[c](x) * 2 + c) for x in range(4) for c in range(2)]
     )
+
+
+def flip(x):
+    return x ^ 1
+
+
+def mirror(x):
+    return 3 - x
 
 
 def to_core(array):
@@ -205,42 +237,37 @@
 
 
 def local(table, lookup_owner, lookup_row, bag_length, top_in, top_bias, top_out):
-    own = (top_in, top_bias.reshape(1, -1), top_out)
-    far = []
-    for array in own:
-        far.append(to_chip(array, lambda x: 3 - x))
-    near = [to_core(array) for array in own]
-    far_near = [to_core(array) for array in far]
-    w_in, biases, w_out = zip(own, near, far, far_near)
+    own = (top_bias.reshape(1, -1), top_in, top_out)
+    near, far, far_near = [], [], []
+    for k, array in enumerate(own):
+        near.append(to_core(array))
+        far.append(to_chip(array, (mirror, flip)))
+        far_near.append(to_chip(near[k], (mirror, flip)))
+    biases, w_in, w_out = zip(own, near, far, far_near)
 
     owner = jnp.transpose(lookup_owner[..., 0], (0, 2, 1))
     live = jnp.arange(BAG, dtype=jnp.int32)[None, :, None] < bag_length[:, None, :]
     owner = jnp.where(live, owner, OWNERS)
     row = jnp.transpose(lookup_row, (0, 2, 1))
-    codes = pl.pallas_call(
+    lists = pl.pallas_call(
         dispatch_kernel,
         out_shape=jax.ShapeDtypeStruct((OWNERS, 24, 128), jnp.int32),
         name="dispatch",
     )(owner, row)
-    codes = lax.all_to_all(codes, "gx", 0, 0, tiled=True)
-    counts = codes[:, 16:20, 0].T
-    codes = jnp.transpose(codes[:, :16, :].reshape(OWNERS, TABLES, CAP), (1, 0, 2))
-    rows = (codes & (ROWS_DEV - 1)).reshape(TABLES, OWNERS * CAP)
-    bags = jnp.where((codes & VALID) != 0, codes >> BAG_SHIFT, SAMPLES)
+    lists = lax.all_to_all(lists, "gx", 0, 0, tiled=True)
 
     mine, theirs = [], []
     first = 0
     for number in CHUNKS:
-        part = slice(first, first + number)
-        share = pool_tables(first, number, rows[part], counts[part], bags[part], table)
-        first += number
+        share = pool_tables(first, number, lists, table)
         share = lax.all_to_all(share, "gx", 0, 0, tiled=True)
         chunk = jnp.sum(share.astype(jnp.float32), axis=0).astype(jnp.bfloat16)
         mine.append(chunk)
-        theirs.append(to_chip(chunk, lambda x: x ^ 1))
+        theirs.append(to_chip(chunk, (flip, mirror)))
+        first += number
     kept = score(mine, biases, w_in, w_out, jnp.float32)
     sent = score(theirs, biases, w_in, w_out, jnp.bfloat16)
-    received = to_chip(sent, lambda x: x ^ 1)
+    received = to_chip(sent, (flip, mirror))
     return (kept + received.astype(jnp.float32)).astype(jnp.bfloat16)
 
 

time: 145 us -> 181 us (1.25)
  waiting for transfers between devices: 38.5 us -> 87.2 us
  Pallas kernels: 57 us -> 52.3 us
  starting transfers between devices: 38.2 us -> 34 us
  local copies, waits for them, and re-layouts: 4.17 us -> 0.02 us
    ppermute x6 -> x9, waiting for transfers between devices: 29.6 us -> 72.9 us  [to_chip(): lax.ppermute(array, 'gy', [(x * 2 + c, targets[c](x) * 2 + c) for x in ra...]
    pallas_call x2, Pallas kernels: 41.5 us -> 36.7 us  [pool_tables(): pl.pallas_call(functools.partial(pool_kernel, first), grid=(tables, OWNER...]
    all_to_all x2, waiting for transfers between devices: 3.45 us -> 7.33 us  [local(): share = lax.all_to_all(share, 'gx', 0, 0, tiled=True)]
    ppermute x6 -> x3, starting transfers between devices: 11.1 us -> 7.32 us  [to_core(): return lax.ppermute(array, 'gy', [(k, k ^ 1) for k in range(8)])]
    reshape x4 -> x0, local copies, waits for them, and re-layouts: 2.53 us -> none  [the longest x2 1.27 us: pool_tables(): bags.reshape(tables * steps, STEP, CAP)]
    ppermute x6 -> x9, starting transfers between devices: 8.87 us -> 8.59 us  [to_chip(): lax.ppermute(array, 'gy', [(x * 2 + c, targets[c](x) * 2 + c) for x in ra...]
  transfers between devices with their start and end apart: 15 -> 15, of which waited for: 8 -> 7; matrix products, arithmetic and copies ran while one was open for 6% -> 2% of each run, Pallas kernels for 33% -> 24%
where the time goes in v1:
time: 181 us; the launch traced here: 180 us
  waiting for transfers between devices  87.2 us (48%)
  Pallas kernels  52.3 us (29%)
  starting transfers between devices  34 us (19%)
  other arithmetic  6.18 us (3%)
    ppermute x9, waiting for transfers between devices, to_chip(): lax.ppermute(array, 'gy', [(x * 2 + c, targets[c](x) * 2 + c) for x in ra...  72.9 us
    pallas_call x2, Pallas kernels, pool_tables(): pl.pallas_call(functools.partial(pool_kernel, first), grid=(tables, OWNER...  36.7 us
    pallas_call x2, Pallas kernels, score(): pl.pallas_call(functools.partial(score_kernel, pieces, chunks), in_specs=...  11.1 us
    all_to_all x2, starting transfers between devices, local(): share = lax.all_to_all(share, 'gx', 0, 0, tiled=True)  9.55 us
    ppermute x9, starting transfers between devices, to_chip(): lax.ppermute(array, 'gy', [(x * 2 + c, targets[c](x) * 2 + c) for x in ra...  8.59 us
    all_to_all x1, starting transfers between devices, local(): lists = lax.all_to_all(lists, 'gx', 0, 0, tiled=True)  8.57 us
    all_to_all x2, waiting for transfers between devices, local(): share = lax.all_to_all(share, 'gx', 0, 0, tiled=True)  7.33 us
    ppermute x3, starting transfers between devices, to_core(): return lax.ppermute(array, 'gy', [(k, k ^ 1) for k in range(8)])  7.32 us
  transfers between devices with their start and end apart: 15, of which 7 were waited for; matrix products, arithmetic and copies ran while one was open for 2% of the time, Pallas kernels for 24%

profile of v1, /device:TPU:1, one launch (start us, length us, event | category | flops | bytes accessed | tf_op | source)
XLA Modules:
  0.0 179.8 jit_solution(12016995192313905738)
XLA Ops:
  0.0 1.5 bitcast_select_fusion.own_ref
  1.5 4.5 %dispatch.1 = s32[16,24,128]{2,1,0:T(8,128)} custom-call(s32[4,16,256]{2,1,0:T(8,128)} %bitcast_select_fusion.own_ref, s32[4,16,256]{2,1,0:T(8,128)} %bitcast.10), custom_call_target="tpu_custom_call" | custom-call | tf_op jit(solution)/shard_map/dispatch/pallas_call | solution.py:252
  5.9 8.6 %all-to-all-start = ((s32[16,24,128]{2,1,0:T(8,128)}), s32[16,24,128]{2,1,0:T(8,128)S(1)}, u32[]{:S(2)}, u32[]{:S(2)}) async-start(s32[16,24,128]{2,1,0:T(8,128)} %dispatch.1), calls=%async_computation | async-start | bytes 393216 | tf_op jit(solution)/shard_map/all_to_all | solution.py:257
  14.5 1.0 collective-permute-start.6
  15.6 6.1 %all-to-all-done.lists_ref = s32[16,24,128]{2,1,0:T(8,128)S(1)} async-done(((s32[16,24,128]{2,1,0:T(8,128)}), s32[16,24,128]{2,1,0:T(8,128)S(1)}, u32[]{:S(2)}, u32[]{:S(2)}) %all-to-all-start) | async-done | bytes 196640 | tf_op jit(solution)/shard_map/all_to_all | solution.py:257
  21.7 18.1 %shard_map.74 = bf16[16,256,256]{2,1,0:T(8,128)(2,1)} custom-call(s32[16,24,128]{2,1,0:T(8,128)S(1)} %all-to-all-done.lists_ref, f32[4,8192,128]{2,1,0:T(8,128)} %table_ref.3), custom_call_target="tpu_custom_call" | custom-call | flops 20000000000 | bytes 6000000 | tf_op jit(solution)/shard_map/pallas_call | solution.py:142
  39.8 4.4 %all-to-all-start.2 = ((bf16[16,256,256]{2,1,0:T(8,128)(2,1)}), bf16[16,256,256]{2,1,0:T(8,128)(2,1)}, u32[]{:S(2)}, u32[]{:S(2)}) async-start(bf16[16,256,256]{2,1,0:T(8,128)(2,1)} %shard_map.74), calls=%async_computation.2 | async-start | bytes 4194304 | tf_op jit(solution)/shard_map/all_to_all | solution.py:263
  44.3 18.6 %shard_map.73 = bf16[16,256,256]{2,1,0:T(8,128)(2,1)} custom-call(s32[16,24,128]{2,1,0:T(8,128)S(1)} %all-to-all-done.lists_ref, f32[4,8192,128]{2,1,0:T(8,128)} %table_ref.3), custom_call_target="tpu_custom_call" | custom-call | flops 20000000000 | bytes 6000000 | tf_op jit(solution)/shard_map/pallas_call | solution.py:142
  62.9 0.0 copy-start.1
  62.9 0.0 copy-start
  62.9 0.0 copy-start.2
  62.9 7.3 %all-to-all-done.2 = bf16[16,256,256]{2,1,0:T(8,128)(2,1)} async-done(((bf16[16,256,256]{2,1,0:T(8,128)(2,1)}), bf16[16,256,256]{2,1,0:T(8,128)(2,1)}, u32[]{:S(2)}, u32[]{:S(2)}) %all-to-all-start.2) | async-done | bytes 2097184 | tf_op jit(solution)/shard_map/all_to_all | solution.py:263
  70.2 5.1 %all-to-all-start.1 = ((bf16[16,256,256]{2,1,0:T(8,128)(2,1)}), bf16[16,256,256]{2,1,0:T(8,128)(2,1)}, u32[]{:S(2)}, u32[]{:S(2)}) async-start(bf16[16,256,256]{2,1,0:T(8,128)(2,1)} %shard_map.73), calls=%async_computation.1 | async-start | bytes 4194304 | tf_op jit(solution)/shard_map/all_to_all | solution.py:263
  75.4 0.0 copy-done.1
  75.4 4.2 %collective-permute-start.3 = (bf16[512,1024]{1,0:T(8,128)(2,1)S(1)}, bf16[512,1024]{1,0:T(8,128)(2,1)}, u32[]{:S(2)}, u32[]{:S(2)}) collective-permute-start(bf16[512,1024]{1,0:T(8,128)(2,1)S(1)} %copy-done.1), channel_id=1, source_target_pairs={{0,1},{1,0},{2,3},{3,2},{4,5},{5,4},{6,7},{7,6},{8,9},{9,8},{10,11... | collective-permute-start | bytes 3145736 | tf_op jit(solution)/shard_map/ppermute | solution.py:236
  79.5 0.0 copy-done
  79.5 1.3 collective-permute-start.7
  80.8 0.0 collective-permute-done.6.refs_11_
  80.8 0.2 collective-permute-start.8
  81.0 1.3 collective-permute-start.4
  82.3 0.0 collective-permute-done.3.refs_7_
  82.3 0.9 collective-permute-start.5
  83.3 0.0 copy-done.2
  83.3 0.5 collective-permute-start.1
  83.8 66.0 %collective-permute-done.1.refs_4_ = f32[1,1024]{1,0:T(1,128)S(1)} collective-permute-done((f32[1,1024]{1,0:T(1,128)S(1)}, f32[1,1024]{1,0:T(1,128)S(1)}, u32[]{:S(2)}, u32[]{:S(2)}) %collective-permute-start.1) | collective-permute-done | bytes 4128 | tf_op jit(solution)/shard_map/ppermute | solution.py:222
  149.8 2.1 %collective-permute-start = (f32[1,1024]{1,0:T(1,128)S(1)}, f32[1,1024]{1,0:T(1,128)S(1)}, u32[]{:S(2)}, u32[]{:S(2)}) collective-permute-start(f32[1,1024]{1,0:T(1,128)S(1)} %bitcast.7), channel_id=1, source_target_pairs={{0,1},{1,0},{2,3},{3,2},{4,5},{5,4},{6,7},{7,6},{8,9},{9,8},{10,11... | collective-permute-start | bytes 12296 | tf_op jit(solution)/shard_map/ppermute | solution.py:236
  151.9 0.8 collective-permute-done.refs_3_
  152.7 0.1 collective-permute-start.2
  152.8 1.9 %reduce_sum.25.refs_1_ = bf16[256,256]{1,0:T(8,128)(2,1)S(1)} reduce(bf16[16,256,256]{2,1,0:T(8,128)(2,1)} %all-to-all-done.2, bf16[]{:T(256)} %constant.5.clone.1), dimensions={0}, to_apply=%region_1.2 | reduce | flops 983040 | bytes 2228226 | tf_op jit(solution)/shard_map/reduce_sum | solution.py:264
  154.7 0.0 all-to-all-done.1
  154.7 1.9 %reduce_sum.24.refs_0_ = bf16[256,256]{1,0:T(8,128)(2,1)S(1)} reduce(bf16[16,256,256]{2,1,0:T(8,128)(2,1)} %all-to-all-done.1, bf16[]{:T(256)} %constant.5.clone.1), dimensions={0}, to_apply=%region_0.1 | reduce | flops 983040 | bytes 2228226 | tf_op jit(solution)/shard_map/reduce_sum | solution.py:264
  156.6 0.0 collective-permute-done.2.refs_5_
  156.6 2.3 %collective-permute-start.10 = (bf16[256,256]{1,0:T(8,128)(2,1)S(1)}, bf16[256,256]{1,0:T(8,128)(2,1)S(1)}, u32[]{:S(2)}, u32[]{:S(2)}) collective-permute-start(bf16[256,256]{1,0:T(8,128)(2,1)S(1)} %reduce_sum.25.refs_1_), channel_id=1, source_target_pairs={{0,2},{1,7},{2,0},{3,5},{4,6},{5,3},{6,4},{7,1},{8,10},{9,15},{10,... | collective-permute-start | bytes 393224 | tf_op jit(solution)/shard_map/ppermute | solution.py:222
  159.0 0.0 collective-permute-done.4.refs_8_
  159.0 0.4 collective-permute-start.9
  159.4 0.0 collective-permute-done.5.refs_9_
  159.4 0.0 collective-permute-done.7.refs_12_
  159.4 2.3 %collective-permute-done.10.refs_1_ = bf16[256,256]{1,0:T(8,128)(2,1)S(1)} collective-permute-done((bf16[256,256]{1,0:T(8,128)(2,1)S(1)}, bf16[256,256]{1,0:T(8,128)(2,1)S(1)}, u32[]{:S(2)}, u32[]{:S(2)}) %collective-permute-start.10) | collective-permute-done | bytes 131104 | tf_op jit(solution)/shard_map/ppermute | solution.py:222
  161.7 2.3 %collective-permute-done.9.refs_0_ = bf16[256,256]{1,0:T(8,128)(2,1)S(1)} collective-permute-done((bf16[256,256]{1,0:T(8,128)(2,1)S(1)}, bf16[256,256]{1,0:T(8,128)(2,1)S(1)}, u32[]{:S(2)}, u32[]{:S(2)}) %collective-permute-start.9) | collective-permute-done | bytes 131104 | tf_op jit(solution)/shard_map/ppermute | solution.py:222
  164.0 0.0 collective-permute-done.8.refs_13_
  164.0 5.5 %shard_map.76 = bf16[256,1024]{1,0:T(8,128)(2,1)S(1)} custom-call(bf16[256,256]{1,0:T(8,128)(2,1)S(1)} %collective-permute-done.9.refs_0_, bf16[256,256]{1,0:T(8,128)(2,1)S(1)} %collective-permute-done.10.refs_1_, f32[1,1024]{1,0:T(1,128)S(1)} %bitcast.8, f32[1,1024]{1,0:T(1,128)S(1)} %collective-permute-done.refs_3_, ...), custom_call_target="tpu_custom_call" | custom-call | flops 10000000000 | bytes 14000000 | tf_op jit(solution)/shard_map/pallas_call | solution.py:203
  169.5 1.5 collective-permute-start.11
  171.0 5.5 %shard_map.75 = f32[256,1024]{1,0:T(8,128)S(1)} custom-call(bf16[256,256]{1,0:T(8,128)(2,1)S(1)} %reduce_sum.24.refs_0_, bf16[256,256]{1,0:T(8,128)(2,1)S(1)} %reduce_sum.25.refs_1_, f32[1,1024]{1,0:T(1,128)S(1)} %bitcast.9, f32[1,1024]{1,0:T(1,128)S(1)} %collective-permute-done.refs_3_, f32[1,1024]{1,0:T(1,128)S(1)} %collective-permute-done.1.refs_4_, ...), custom_call_target="tpu_custom_call" | custom-call | flops 10000000000 | bytes 14000000 | tf_op jit(solution)/shard_map/pallas_call | solution.py:203
  176.6 2.3 %collective-permute-done.11 = bf16[256,1024]{1,0:T(8,128)(2,1)S(1)} collective-permute-done((bf16[256,1024]{1,0:T(8,128)(2,1)S(1)}, bf16[256,1024]{1,0:T(8,128)(2,1)S(1)}, u32[]{:S(2)}, u32[]{:S(2)}) %collective-permute-start.11) | collective-permute-done | bytes 524320 | tf_op jit(solution)/shard_map/ppermute | solution.py:222
  178.9 0.9 add_convert_fusion
Async XLA Ops:
  5.9 15.7 %all-to-all-start = ((s32[16,24,128]{2,1,0:T(8,128)}), s32[16,24,128]{2,1,0:T(8,128)S(1)}, u32[]{:S(2)}, u32[]{:S(2)}) async-start(s32[16,24,128]{2,1,0:T(8,128)} %dispatch.1), calls=%async_computation | async-start | bytes 393216 | tf_op jit(solution)/shard_map/all_to_all | solution.py:257
  14.5 66.3 %collective-permute-start.6 = (bf16[1024,1024]{1,0:T(8,128)(2,1)}, bf16[1024,1024]{1,0:T(8,128)(2,1)}, u32[]{:S(2)}, u32[]{:S(2)}) collective-permute-start(bf16[1024,1024]{1,0:T(8,128)(2,1)} %refs_10_.3), channel_id=1, source_target_pairs={{0,1},{1,0},{2,3},{3,2},{4,5},{5,4},{6,7},{7,6},{8,9},{9,8},{10,11... | collective-permute-start | bytes 6291464 | tf_op jit(solution)/shard_map/ppermute | solution.py:236
  39.8 30.4 %all-to-all-start.2 = ((bf16[16,256,256]{2,1,0:T(8,128)(2,1)}), bf16[16,256,256]{2,1,0:T(8,128)(2,1)}, u32[]{:S(2)}, u32[]{:S(2)}) async-start(bf16[16,256,256]{2,1,0:T(8,128)(2,1)} %shard_map.74), calls=%async_computation.2 | async-start | bytes 4194304 | tf_op jit(solution)/shard_map/all_to_all | solution.py:263
  62.9 12.5 %copy-start.1 = (bf16[512,1024]{1,0:T(8,128)(2,1)S(1)}, bf16[512,1024]{1,0:T(8,128)(2,1)}, u32[]{:S(2)}) copy-start(bf16[512,1024]{1,0:T(8,128)(2,1)} %refs_6_.3) | copy-start | bytes 3145732
  62.9 16.6 %copy-start = (bf16[1024,1024]{1,0:T(8,128)(2,1)S(1)}, bf16[1024,1024]{1,0:T(8,128)(2,1)}, u32[]{:S(2)}) copy-start(bf16[1024,1024]{1,0:T(8,128)(2,1)} %refs_10_.3) | copy-start | bytes 6291460
  62.9 20.4 %copy-start.2 = (f32[1024]{0:T(1024)S(1)}, f32[1024]{0:T(1024)}, u32[]{:S(2)}) copy-start(f32[1024]{0:T(1024)} %param.12) | copy-start | bytes 12292
  70.2 84.5 %all-to-all-start.1 = ((bf16[16,256,256]{2,1,0:T(8,128)(2,1)}), bf16[16,256,256]{2,1,0:T(8,128)(2,1)}, u32[]{:S(2)}, u32[]{:S(2)}) async-start(bf16[16,256,256]{2,1,0:T(8,128)(2,1)} %shard_map.73), calls=%async_computation.1 | async-start | bytes 4194304 | tf_op jit(solution)/shard_map/all_to_all | solution.py:263
  75.4 6.9 %collective-permute-start.3 = (bf16[512,1024]{1,0:T(8,128)(2,1)S(1)}, bf16[512,1024]{1,0:T(8,128)(2,1)}, u32[]{:S(2)}, u32[]{:S(2)}) collective-permute-start(bf16[512,1024]{1,0:T(8,128)(2,1)S(1)} %copy-done.1), channel_id=1, source_target_pairs={{0,1},{1,0},{2,3},{3,2},{4,5},{5,4},{6,7},{7,6},{8,9},{9,8},{10,11... | collective-permute-start | bytes 3145736 | tf_op jit(solution)/shard_map/ppermute | solution.py:236
  79.5 79.9 %collective-permute-start.7 = (bf16[1024,1024]{1,0:T(8,128)(2,1)S(1)}, bf16[1024,1024]{1,0:T(8,128)(2,1)}, u32[]{:S(2)}, u32[]{:S(2)}) collective-permute-start(bf16[1024,1024]{1,0:T(8,128)(2,1)S(1)} %copy-done), channel_id=1, source_target_pairs={{0,6},{1,3},{2,4},{3,1},{4,2},{5,7},{6,0},{7,5},{8,14},{9,11},{10,... | collective-permute-start | bytes 6291464 | tf_op jit(solution)/shard_map/ppermute | solution.py:222
  80.8 83.2 %collective-permute-start.8 = (bf16[1024,1024]{1,0:T(8,128)(2,1)}, bf16[1024,1024]{1,0:T(8,128)(2,1)}, u32[]{:S(2)}, u32[]{:S(2)}) collective-permute-start(bf16[1024,1024]{1,0:T(8,128)(2,1)} %collective-permute-done.6.refs_11_), channel_id=1, source_target_pairs={{0,6},{1,3},{2,4},{3,1},{4,2},{5,7},{6,0},{7,5},{8,14},{9,11},{10,... | collective-permute-start | bytes 6291464 | tf_op jit(solution)/shard_map/ppermute | solution.py:222
  81.0 78.0 %collective-permute-start.4 = (bf16[512,1024]{1,0:T(8,128)(2,1)S(1)}, bf16[512,1024]{1,0:T(8,128)(2,1)}, u32[]{:S(2)}, u32[]{:S(2)}) collective-permute-start(bf16[512,1024]{1,0:T(8,128)(2,1)S(1)} %copy-done.1), channel_id=1, source_target_pairs={{0,6},{1,3},{2,4},{3,1},{4,2},{5,7},{6,0},{7,5},{8,14},{9,11},{10,... | collective-permute-start | bytes 3145736 | tf_op jit(solution)/shard_map/ppermute | solution.py:222
  82.3 77.1 %collective-permute-start.5 = (bf16[512,1024]{1,0:T(8,128)(2,1)}, bf16[512,1024]{1,0:T(8,128)(2,1)}, u32[]{:S(2)}, u32[]{:S(2)}) collective-permute-start(bf16[512,1024]{1,0:T(8,128)(2,1)} %collective-permute-done.3.refs_7_), channel_id=1, source_target_pairs={{0,6},{1,3},{2,4},{3,1},{4,2},{5,7},{6,0},{7,5},{8,14},{9,11},{10,... | collective-permute-start | bytes 3145736 | tf_op jit(solution)/shard_map/ppermute | solution.py:222
  83.3 66.5 %collective-permute-start.1 = (f32[1,1024]{1,0:T(1,128)S(1)}, f32[1,1024]{1,0:T(1,128)S(1)}, u32[]{:S(2)}, u32[]{:S(2)}) collective-permute-start(f32[1,1024]{1,0:T(1,128)S(1)} %bitcast.6), channel_id=1, source_target_pairs={{0,6},{1,3},{2,4},{3,1},{4,2},{5,7},{6,0},{7,5},{8,14},{9,11},{10,... | collective-permute-start | bytes 12296 | tf_op jit(solution)/shard_map/ppermute | solution.py:222
  149.8 2.9 %collective-permute-start = (f32[1,1024]{1,0:T(1,128)S(1)}, f32[1,1024]{1,0:T(1,128)S(1)}, u32[]{:S(2)}, u32[]{:S(2)}) collective-permute-start(f32[1,1024]{1,0:T(1,128)S(1)} %bitcast.7), channel_id=1, source_target_pairs={{0,1},{1,0},{2,3},{3,2},{4,5},{5,4},{6,7},{7,6},{8,9},{9,8},{10,11... | collective-permute-start | bytes 12296 | tf_op jit(solution)/shard_map/ppermute | solution.py:236
  152.7 3.9 %collective-permute-start.2 = (f32[1,1024]{1,0:T(1,128)S(1)}, f32[1,1024]{1,0:T(1,128)S(1)}, u32[]{:S(2)}, u32[]{:S(2)}) collective-permute-start(f32[1,1024]{1,0:T(1,128)S(1)} %collective-permute-done.refs_3_), channel_id=1, source_target_pairs={{0,6},{1,3},{2,4},{3,1},{4,2},{5,7},{6,0},{7,5},{8,14},{9,11},{10,... | collective-permute-start | bytes 12296 | tf_op jit(solution)/shard_map/ppermute | solution.py:222
  156.6 5.1 %collective-permute-start.10 = (bf16[256,256]{1,0:T(8,128)(2,1)S(1)}, bf16[256,256]{1,0:T(8,128)(2,1)S(1)}, u32[]{:S(2)}, u32[]{:S(2)}) collective-permute-start(bf16[256,256]{1,0:T(8,128)(2,1)S(1)} %reduce_sum.25.refs_1_), channel_id=1, source_target_pairs={{0,2},{1,7},{2,0},{3,5},{4,6},{5,3},{6,4},{7,1},{8,10},{9,15},{10,... | collective-permute-start | bytes 393224 | tf_op jit(solution)/shard_map/ppermute | solution.py:222
  159.0 5.0 %collective-permute-start.9 = (bf16[256,256]{1,0:T(8,128)(2,1)S(1)}, bf16[256,256]{1,0:T(8,128)(2,1)S(1)}, u32[]{:S(2)}, u32[]{:S(2)}) collective-permute-start(bf16[256,256]{1,0:T(8,128)(2,1)S(1)} %reduce_sum.24.refs_0_), channel_id=1, source_target_pairs={{0,2},{1,7},{2,0},{3,5},{4,6},{5,3},{6,4},{7,1},{8,10},{9,15},{10,... | collective-permute-start | bytes 393224 | tf_op jit(solution)/shard_map/ppermute | solution.py:222
  169.5 9.3 %collective-permute-start.11 = (bf16[256,1024]{1,0:T(8,128)(2,1)S(1)}, bf16[256,1024]{1,0:T(8,128)(2,1)S(1)}, u32[]{:S(2)}, u32[]{:S(2)}) collective-permute-start(bf16[256,1024]{1,0:T(8,128)(2,1)S(1)} %shard_map.76), channel_id=1, source_target_pairs={{0,2},{1,7},{2,0},{3,5},{4,6},{5,3},{6,4},{7,1},{8,10},{9,15},{10,... | collective-permute-start | bytes 1572872 | tf_op jit(solution)/shard_map/ppermute | solution.py:222

commit v2 on v1

--- a/solution.py
+++ b/solution.py
@@ -37,52 +37,57 @@
     ones = jnp.ones((256, 256), jnp.bfloat16)
     same = ones_where(iota((16, 256), 0) == (iota((16, 256), 1) & 15))
     owner_iota = iota((16, 16, 256), 1)
-    for t in range(TABLES):
-        own = own_ref[t]
-        mark = (own[:, None, :] == owner_iota).reshape(256, 256)
-        onehot = ones_where(mark)
-        rank = jnp.dot(onehot, before, preferred_element_type=jnp.float32)
-        lead = jnp.dot(earlier, onehot, preferred_element_type=jnp.float32)
-        rank += jnp.dot(lead.astype(jnp.bfloat16), ones, preferred_element_type=jnp.float32)
-        rank = jnp.sum(jnp.where(mark, rank, 0.0).reshape(16, 16, 256), axis=1).astype(jnp.int32)
-        total = jnp.dot(same, onehot, preferred_element_type=jnp.float32)
-        total = jnp.dot(total.astype(jnp.bfloat16), ones, preferred_element_type=jnp.float32)
-        out_ref[:, 16 + t, :] = total[:, :128].astype(jnp.int32)
-        hi = own * 4 + (rank >> 7)
-        lo = rank & 127
-        row = row_ref[t]
-        low = (row & 255).astype(jnp.float32)
-        high = (row >> 8).astype(jnp.float32)
-        bag = (iota((1, 256), 1) + 1).astype(jnp.float32)
-        acc = jnp.zeros((192, 128), jnp.float32)
-        for s in range(BAG):
-            left = hi[s : s + 1, :] == iota((64, 256), 0)
-            planes = jnp.concatenate(
-                [
-                    jnp.where(left, low[s : s + 1, :], 0.0),
-                    jnp.where(left, high[s : s + 1, :], 0.0),
-                    jnp.where(left, bag, 0.0),
-                ],
-                axis=0,
-            ).astype(jnp.bfloat16)
-            right = ones_where(lo[s : s + 1, :] == iota((128, 256), 0))
-            acc += lax.dot_general(
-                planes, right, (((1,), (1,)), ((), ())), preferred_element_type=jnp.float32
-            )
-        acc = acc.astype(jnp.int32)
-        code = acc[:64] | (acc[64:128] << 8) | (acc[128:] << BAG_SHIFT)
-        out_ref[:, 4 * t : 4 * t + 4, :] = code.reshape(OWNERS, 4, 128)
-    out_ref[:, 20:, :] = jnp.zeros((OWNERS, 4, 128), jnp.int32)
+    count64 = iota((64, 256), 0).astype(jnp.float32).astype(jnp.bfloat16)
+    count128 = iota((128, 256), 0).astype(jnp.float32).astype(jnp.bfloat16)
+    bag = (iota((1, 256), 1) + 1).astype(jnp.float32).astype(jnp.bfloat16)
+    zero, one = jnp.bfloat16(0), jnp.bfloat16(1)
+    own = own_ref[...]
+    mark = (own[:, None, :] == owner_iota).reshape(256, 256)
+    onehot = ones_where(mark)
+    rank = jnp.dot(onehot, before, preferred_element_type=jnp.float32)
+    lead = jnp.dot(earlier, onehot, preferred_element_type=jnp.float32)
+    rank += jnp.dot(lead.astype(jnp.bfloat16), ones, preferred_element_type=jnp.float32)
+    rank = jnp.sum(jnp.where(mark, rank, 0.0).reshape(16, 16, 256), axis=1).astype(jnp.int32)
+    total = jnp.dot(same, onehot, preferred_element_type=jnp.float32)
+    total = jnp.dot(total.astype(jnp.bfloat16), ones, preferred_element_type=jnp.float32)
+    hi = (own * 4 + (rank >> 7)).astype(jnp.float32)
+    lo = (rank & 127).astype(jnp.float32)
+    row = row_ref[...]
+    low = (row & 255).astype(jnp.float32)
+    high = (row >> 8).astype(jnp.float32)
+    acc = jnp.zeros((192, 128), jnp.float32)
+    for s in range(BAG):
+        line = slice(s, s + 1)
+        left = hi[line].astype(jnp.bfloat16) == count64
+        planes = jnp.concatenate(
+            [
+                jnp.where(left, low[line].astype(jnp.bfloat16), zero),
+                jnp.where(left, high[line].astype(jnp.bfloat16), zero),
+                jnp.where(left, bag, zero),
+            ],
+            axis=0,
+        )
+        right = jnp.where(lo[line].astype(jnp.bfloat16) == count128, one, zero)
+        acc += lax.dot_general(
+            planes, right, (((1,), (1,)), ((), ())), preferred_element_type=jnp.float32
+        )
+    acc = acc.astype(jnp.int32)
+    code = acc[:64] | (acc[64:128] << 8) | (acc[128:] << BAG_SHIFT)
+    out_ref[:, :4, :] = code.reshape(OWNERS, 4, 128)
+    out_ref[:, 4, :] = total[:, :128].astype(jnp.int32)
+    out_ref[:, 5:, :] = jnp.zeros((OWNERS, 3, 128), jnp.int32)
 
 
 def pool_kernel(first, lists_ref, table_ref, out_ref, buf_ref, held_ref, rows_vmem, rows_ref, sem, row_sem):
-    tables = held_ref.shape[0]
+    tables = held_ref.shape[0] // ROWS_DEV
     turn, part = pl.program_id(0), pl.program_id(1)
 
     def load(t, k):
-        piece = pl.ds(k * (ROWS_DEV // PIECES), ROWS_DEV // PIECES)
+        size = ROWS_DEV // PIECES
         return pltpu.make_async_copy(
-            table_ref.at[first + t, piece], held_ref.at[t, piece], sem.at[t, k]
+            table_ref.at[first + t, pl.ds(k * size, size)],
+            held_ref.at[pl.ds(t * ROWS_DEV + k * size, size)],
+            sem.at[t, k],
         )
 
     def load_rows():
@@ -93,9 +98,10 @@
         for t in range(tables):
             for k in range(PIECES):
                 load(t, k).start()
-        codes = lists_ref[:, 4 * first : 4 * (first + tables), :]
-        rows_vmem[:, : 4 * tables, :] = codes & (ROWS_DEV - 1)
-        rows_vmem[:, 4 * tables : 5 * tables, :] = lists_ref[:, 16 + first : 16 + first + tables, :]
+        codes = lists_ref[:, 8 * first : 8 * (first + tables), :]
+        line = iota(codes.shape, 1)
+        rows = (codes & (ROWS_DEV - 1)) + (line >> 3) * ROWS_DEV
+        rows_vmem[...] = jnp.where((line & 7) == 4, codes, rows)
         load_rows().start()
         buf_ref[...] = jnp.zeros_like(buf_ref)
         load_rows().wait()
@@ -109,15 +115,16 @@
 
     def fetch(q, carry):
         source = part * STEP + q
-        count = rows_ref[source, 4 * tables + turn, 0]
+        count = rows_ref[source, 8 * turn + 4, 0]
         for line in range(CAP // 128):
             for base in range(0, 128, BLOCK):
 
                 @pl.when(count > line * 128 + base)
                 def _(line=line, base=base):
                     for k in range(base, base + BLOCK):
-                        row = rows_ref[source, 4 * turn + line, k]
-                        buf_ref[q, pl.ds(line * 128 + k, 1), :] = held_ref[turn, pl.ds(row, 1), :]
+                        ids = rows_ref.at[source, 8 * turn + line, pl.ds(k // 8 * 8, 8)]
+                        row = ids[k % 8]
+                        buf_ref[q, pl.ds(line * 128 + k, 1), :] = held_ref[pl.ds(row, 1), :]
 
         return carry
 
@@ -127,7 +134,7 @@
         source = part * STEP + q
         picks = []
         for line in range(CAP // 128):
-            named = lists_ref[source, pl.ds(4 * first + 4 * turn + line, 1), :] >> BAG_SHIFT
+            named = lists_ref[source, pl.ds(8 * first + 8 * turn + line, 1), :] >> BAG_SHIFT
             named = named.astype(jnp.float32).astype(jnp.bfloat16)
             picks.append(jnp.where(named == bag, jnp.bfloat16(1), jnp.bfloat16(0)))
         out_ref[q] = jnp.dot(
@@ -138,7 +145,6 @@
 
 
 def pool_tables(first, tables, lists, table):
-    width = -(-5 * tables // 8) * 8
     return pl.pallas_call(
         functools.partial(pool_kernel, first),
         grid=(tables, OWNERS // STEP),
@@ -149,18 +155,38 @@
         out_specs=pl.BlockSpec((STEP, SAMPLES, EMB), lambda t, i: (i, 0, t)),
         scratch_shapes=[
             pltpu.VMEM((STEP, CAP, EMB), jnp.float32),
-            pltpu.VMEM((tables, ROWS_DEV, EMB), jnp.float32),
-            pltpu.VMEM((OWNERS, width, 128), jnp.int32),
-            pltpu.SMEM((OWNERS, width, 128), jnp.int32),
+            pltpu.VMEM((tables * ROWS_DEV, EMB), jnp.float32),
+            pltpu.VMEM((OWNERS, 8 * tables, 128), jnp.int32),
+            pltpu.SMEM((OWNERS, 8 * tables, 128), jnp.int32),
             pltpu.SemaphoreType.DMA((tables, PIECES)),
             pltpu.SemaphoreType.DMA(()),
         ],
         out_shape=jax.ShapeDtypeStruct((OWNERS, SAMPLES, tables * EMB), jnp.bfloat16),
-        compiler_params=pltpu.CompilerParams(vmem_limit_bytes=49 << 20),
+        compiler_params=pltpu.CompilerParams(vmem_limit_bytes=104 << 19),
         cost_estimate=pl.CostEstimate(
             flops=10_000_000_000 * tables, transcendentals=0, bytes_accessed=6_000_000
         ),
     )(lists, table)
+
+
+def add_kernel(shares_ref, out_ref):
+    total = shares_ref[0].astype(jnp.float32)
+    for k in range(1, OWNERS):
+        total += shares_ref[k].astype(jnp.float32)
+    out_ref[...] = total.astype(out_ref.dtype)
+
+
+def add_shares(shares):
+    width = shares.shape[2]
+    return pl.pallas_call(
+        add_kernel,
+        grid=(4,),
+        in_specs=[pl.BlockSpec((OWNERS, SAMPLES // 4, width), lambda i: (0, i, 0))],
+        out_specs=pl.BlockSpec((SAMPLES // 4, width), lambda i: (i, 0)),
+        out_shape=jax.ShapeDtypeStruct((SAMPLES, width), jnp.bfloat16),
+        compiler_params=pltpu.CompilerParams(vmem_limit_bytes=12 << 20),
+        name="add",
+    )(shares)
 
 
 def score_kernel(pieces, chunks, *refs):
@@ -251,7 +277,10 @@
     row = jnp.transpose(lookup_row, (0, 2, 1))
     lists = pl.pallas_call(
         dispatch_kernel,
-        out_shape=jax.ShapeDtypeStruct((OWNERS, 24, 128), jnp.int32),
+        grid=(TABLES,),
+        in_specs=[pl.BlockSpec((None, BAG, SAMPLES), lambda t: (t, 0, 0))] * 2,
+        out_specs=pl.BlockSpec((OWNERS, 8, 128), lambda t: (0, t, 0)),
+        out_shape=jax.ShapeDtypeStruct((OWNERS, 8 * TABLES, 128), jnp.int32),
         name="dispatch",
     )(owner, row)
     lists = lax.all_to_all(lists, "gx", 0, 0, tiled=True)
@@ -261,7 +290,7 @@
     for number in CHUNKS:
         share = pool_tables(first, number, lists, table)
         share = lax.all_to_all(share, "gx", 0, 0, tiled=True)
-        chunk = jnp.sum(share.astype(jnp.float32), axis=0).astype(jnp.bfloat16)
+        chunk = add_shares(share)
         mine.append(chunk)
         theirs.append(to_chip(chunk, (flip, mirror)))
         first += number

time: 181 us -> 179 us (0.989)
  waiting for transfers between devices: 87.2 us -> 92 us
  Pallas kernels: 52.3 us -> 48.5 us
  other arithmetic: 6.18 us -> 2.42 us
    pallas_call x2, Pallas kernels: 36.7 us -> 28.5 us  [pool_tables(): pl.pallas_call(functools.partial(pool_kernel, first), grid=(tables, OWNER...]
    pallas_call x1 -> x3, Pallas kernels: 4.48 us -> 8.92 us  [the longest x1 5.82 us: local(): pl.pallas_call(dispatch_kernel, grid=(TABLES,), in_specs=[pl.BlockSpec((N...]
    all_to_all x2, waiting for transfers between devices: 7.33 us -> 11.5 us  [local(): share = lax.all_to_all(share, 'gx', 0, 0, tiled=True)]
    reduce_sum x2 -> x0, other arithmetic: 3.77 us -> none  [local(): chunk = jnp.sum(share.astype(jnp.float32), axis=0).astype(jnp.bfloat16)]
  transfers between devices with their start and end apart: 15 -> 15, of which waited for: 7 -> 7; matrix products, arithmetic and copies ran while one was open for 2% -> 0% of each run, Pallas kernels for 24% -> 21%
where the time goes in v2:
time: 179 us; the launch traced here: 178 us
  waiting for transfers between devices  92 us (51%)
  Pallas kernels  48.5 us (27%)
  starting transfers between devices  33.4 us (19%)
  other arithmetic  2.42 us (1%)
    ppermute x9, waiting for transfers between devices, to_chip(): lax.ppermute(array, 'gy', [(x * 2 + c, targets[c](x) * 2 + c) for x in ra...  73.2 us
    pallas_call x2, Pallas kernels, pool_tables(): pl.pallas_call(functools.partial(pool_kernel, first), grid=(tables, OWNER...  28.5 us
    all_to_all x2, waiting for transfers between devices, local(): share = lax.all_to_all(share, 'gx', 0, 0, tiled=True)  11.5 us
    pallas_call x2, Pallas kernels, score(): pl.pallas_call(functools.partial(score_kernel, pieces, chunks), in_specs=...  11.1 us
    all_to_all x2, starting transfers between devices, local(): share = lax.all_to_all(share, 'gx', 0, 0, tiled=True)  8.87 us
    ppermute x9, starting transfers between devices, to_chip(): lax.ppermute(array, 'gy', [(x * 2 + c, targets[c](x) * 2 + c) for x in ra...  8.64 us
    all_to_all x1, starting transfers between devices, local(): lists = lax.all_to_all(lists, 'gx', 0, 0, tiled=True)  8.59 us
    ppermute x3, starting transfers between devices, to_core(): return lax.ppermute(array, 'gy', [(k, k ^ 1) for k in range(8)])  7.28 us
  transfers between devices with their start and end apart: 15, of which 7 were waited for; matrix products, arithmetic and copies ran while one was open for 0% of the time, Pallas kernels for 21%

profile of v2, /device:TPU:1, one launch (start us, length us, event | category | flops | bytes accessed | tf_op | source)
XLA Modules:
  0.0 177.9 jit_solution(2613708830814965396)
XLA Ops:
  0.0 1.5 bitcast_select_fusion.own_ref
  1.5 5.8 %dispatch.1 = s32[16,32,128]{2,1,0:T(8,128)} custom-call(s32[4,16,256]{2,1,0:T(8,128)} %bitcast_select_fusion.own_ref, s32[4,16,256]{2,1,0:T(8,128)} %bitcast.10), custom_call_target="tpu_custom_call" | custom-call | tf_op jit(solution)/shard_map/dispatch/pallas_call | solution.py:278
  7.3 8.6 %all-to-all-start = ((s32[16,32,128]{2,1,0:T(8,128)}), s32[16,32,128]{2,1,0:T(8,128)S(1)}, u32[]{:S(2)}, u32[]{:S(2)}) async-start(s32[16,32,128]{2,1,0:T(8,128)} %dispatch.1), calls=%async_computation | async-start | bytes 524288 | tf_op jit(solution)/shard_map/all_to_all | solution.py:286
  15.9 1.0 collective-permute-start.6
  16.9 6.4 %all-to-all-done.lists_ref = s32[16,32,128]{2,1,0:T(8,128)S(1)} async-done(((s32[16,32,128]{2,1,0:T(8,128)}), s32[16,32,128]{2,1,0:T(8,128)S(1)}, u32[]{:S(2)}, u32[]{:S(2)}) %all-to-all-start) | async-done | bytes 262176 | tf_op jit(solution)/shard_map/all_to_all | solution.py:286
  23.3 14.1 %shard_map.74 = bf16[16,256,256]{2,1,0:T(8,128)(2,1)} custom-call(s32[16,32,128]{2,1,0:T(8,128)S(1)} %all-to-all-done.lists_ref, f32[4,8192,128]{2,1,0:T(8,128)} %table_ref.3), custom_call_target="tpu_custom_call" | custom-call | flops 20000000000 | bytes 6000000 | tf_op jit(solution)/shard_map/pallas_call | solution.py:148
  37.5 3.7 %all-to-all-start.2 = ((bf16[16,256,256]{2,1,0:T(8,128)(2,1)}), bf16[16,256,256]{2,1,0:T(8,128)(2,1)S(1)}, u32[]{:S(2)}, u32[]{:S(2)}) async-start(bf16[16,256,256]{2,1,0:T(8,128)(2,1)} %shard_map.74), calls=%async_computation.2 | async-start | bytes 4194304 | tf_op jit(solution)/shard_map/all_to_all | solution.py:292
  41.2 14.4 %shard_map.73 = bf16[16,256,256]{2,1,0:T(8,128)(2,1)} custom-call(s32[16,32,128]{2,1,0:T(8,128)S(1)} %all-to-all-done.lists_ref, f32[4,8192,128]{2,1,0:T(8,128)} %table_ref.3), custom_call_target="tpu_custom_call" | custom-call | flops 20000000000 | bytes 6000000 | tf_op jit(solution)/shard_map/pallas_call | solution.py:148
  55.6 0.0 copy-start.2
  55.6 0.0 copy-start.3
  55.6 11.5 %all-to-all-done.2.shares_ref = bf16[16,256,256]{2,1,0:T(8,128)(2,1)S(1)} async-done(((bf16[16,256,256]{2,1,0:T(8,128)(2,1)}), bf16[16,256,256]{2,1,0:T(8,128)(2,1)S(1)}, u32[]{:S(2)}, u32[]{:S(2)}) %all-to-all-start.2) | async-done | bytes 2097184 | tf_op jit(solution)/shard_map/all_to_all | solution.py:292
  67.1 5.1 %all-to-all-start.1 = ((bf16[16,256,256]{2,1,0:T(8,128)(2,1)}), bf16[16,256,256]{2,1,0:T(8,128)(2,1)}, u32[]{:S(2)}, u32[]{:S(2)}) async-start(bf16[16,256,256]{2,1,0:T(8,128)(2,1)} %shard_map.73), calls=%async_computation.1 | async-start | bytes 4194304 | tf_op jit(solution)/shard_map/all_to_all | solution.py:292
  72.2 0.0 copy-done.2
  72.3 4.1 %collective-permute-start.3 = (bf16[512,1024]{1,0:T(8,128)(2,1)S(1)}, bf16[512,1024]{1,0:T(8,128)(2,1)}, u32[]{:S(2)}, u32[]{:S(2)}) collective-permute-start(bf16[512,1024]{1,0:T(8,128)(2,1)S(1)} %copy-done.2), channel_id=1, source_target_pairs={{0,1},{1,0},{2,3},{3,2},{4,5},{5,4},{6,7},{7,6},{8,9},{9,8},{10,11... | collective-permute-start | bytes 3145736 | tf_op jit(solution)/shard_map/ppermute | solution.py:262
  76.4 1.2 collective-permute-start.7
  77.6 0.0 collective-permute-done.6.refs_11_
  77.6 0.2 collective-permute-start.8
  77.9 1.2 collective-permute-start.4
  79.1 0.0 collective-permute-done.3.refs_7_
  79.1 0.9 collective-permute-start.5
  80.1 0.0 copy-done.3
  80.1 0.5 collective-permute-start.1
  80.6 66.3 %collective-permute-done.1.refs_4_ = f32[1,1024]{1,0:T(1,128)S(1)} collective-permute-done((f32[1,1024]{1,0:T(1,128)S(1)}, f32[1,1024]{1,0:T(1,128)S(1)}, u32[]{:S(2)}, u32[]{:S(2)}) %collective-permute-start.1) | collective-permute-done | bytes 4128 | tf_op jit(solution)/shard_map/ppermute | solution.py:248
  146.9 2.1 %collective-permute-start = (f32[1,1024]{1,0:T(1,128)S(1)}, f32[1,1024]{1,0:T(1,128)S(1)}, u32[]{:S(2)}, u32[]{:S(2)}) collective-permute-start(f32[1,1024]{1,0:T(1,128)S(1)} %bitcast.7), channel_id=1, source_target_pairs={{0,1},{1,0},{2,3},{3,2},{4,5},{5,4},{6,7},{7,6},{8,9},{9,8},{10,11... | collective-permute-start | bytes 12296 | tf_op jit(solution)/shard_map/ppermute | solution.py:262
  149.0 0.8 collective-permute-done.refs_3_
  149.8 0.0 collective-permute-start.2
  149.9 0.5 add.8.refs_1_
  150.4 0.0 all-to-all-done.1.shares_ref
  150.4 0.0 copy-start.1
  150.4 2.6 %add.7.refs_0_ = bf16[256,256]{1,0:T(8,128)(2,1)S(1)} custom-call(bf16[16,256,256]{2,1,0:T(8,128)(2,1)} %all-to-all-done.1.shares_ref), custom_call_target="tpu_custom_call" | custom-call | tf_op jit(solution)/shard_map/add/pallas_call | solution.py:181
  153.0 0.0 collective-permute-done.2.refs_5_
  153.0 2.3 %collective-permute-start.10 = (bf16[256,256]{1,0:T(8,128)(2,1)S(1)}, bf16[256,256]{1,0:T(8,128)(2,1)S(1)}, u32[]{:S(2)}, u32[]{:S(2)}) collective-permute-start(bf16[256,256]{1,0:T(8,128)(2,1)S(1)} %add.8.refs_1_), channel_id=1, source_target_pairs={{0,2},{1,7},{2,0},{3,5},{4,6},{5,3},{6,4},{7,1},{8,10},{9,15},{10,... | collective-permute-start | bytes 393224 | tf_op jit(solution)/shard_map/ppermute | solution.py:248
  155.3 0.0 collective-permute-done.4.refs_8_
  155.3 0.4 collective-permute-start.9
  155.8 0.0 collective-permute-done.5.refs_9_
  155.8 0.0 collective-permute-done.7.refs_12_
  155.8 2.3 %collective-permute-done.10.refs_1_ = bf16[256,256]{1,0:T(8,128)(2,1)S(1)} collective-permute-done((bf16[256,256]{1,0:T(8,128)(2,1)S(1)}, bf16[256,256]{1,0:T(8,128)(2,1)S(1)}, u32[]{:S(2)}, u32[]{:S(2)}) %collective-permute-start.10) | collective-permute-done | bytes 131104 | tf_op jit(solution)/shard_map/ppermute | solution.py:248
  158.1 2.2 %collective-permute-done.9.refs_0_ = bf16[256,256]{1,0:T(8,128)(2,1)S(1)} collective-permute-done((bf16[256,256]{1,0:T(8,128)(2,1)S(1)}, bf16[256,256]{1,0:T(8,128)(2,1)S(1)}, u32[]{:S(2)}, u32[]{:S(2)}) %collective-permute-start.9) | collective-permute-done | bytes 131104 | tf_op jit(solution)/shard_map/ppermute | solution.py:248
  160.4 0.0 collective-permute-done.8.refs_13_
  160.4 0.0 copy-start
  160.4 1.6 copy-done
  162.0 5.5 %shard_map.76 = bf16[256,1024]{1,0:T(8,128)(2,1)S(1)} custom-call(bf16[256,256]{1,0:T(8,128)(2,1)S(1)} %collective-permute-done.9.refs_0_, bf16[256,256]{1,0:T(8,128)(2,1)S(1)} %collective-permute-done.10.refs_1_, f32[1,1024]{1,0:T(1,128)S(1)} %bitcast.8, f32[1,1024]{1,0:T(1,128)S(1)} %collective-permute-done.refs_3_, ...), custom_call_target="tpu_custom_call" | custom-call | flops 10000000000 | bytes 14000000 | tf_op jit(solution)/shard_map/pallas_call | solution.py:229
  167.5 1.7 collective-permute-start.11
  169.2 0.0 copy-done.1
  169.2 5.5 %shard_map.75 = f32[256,1024]{1,0:T(8,128)S(1)} custom-call(bf16[256,256]{1,0:T(8,128)(2,1)S(1)} %add.7.refs_0_, bf16[256,256]{1,0:T(8,128)(2,1)S(1)} %add.8.refs_1_, f32[1,1024]{1,0:T(1,128)S(1)} %bitcast.9, f32[1,1024]{1,0:T(1,128)S(1)} %collective-permute-done.refs_3_, f32[1,1024]{1,0:T(1,128)S(1)} %collective-permute-done.1.refs_4_, ...), custom_call_target="tpu_custom_call" | custom-call | flops 10000000000 | bytes 14000000 | tf_op jit(solution)/shard_map/pallas_call | solution.py:229
  174.7 2.3 %collective-permute-done.11 = bf16[256,1024]{1,0:T(8,128)(2,1)S(1)} collective-permute-done((bf16[256,1024]{1,0:T(8,128)(2,1)S(1)}, bf16[256,1024]{1,0:T(8,128)(2,1)S(1)}, u32[]{:S(2)}, u32[]{:S(2)}) %collective-permute-start.11) | collective-permute-done | bytes 524320 | tf_op jit(solution)/shard_map/ppermute | solution.py:248
  177.0 0.9 add_convert_fusion
Async XLA Ops:
  7.3 16.0 %all-to-all-start = ((s32[16,32,128]{2,1,0:T(8,128)}), s32[16,32,128]{2,1,0:T(8,128)S(1)}, u32[]{:S(2)}, u32[]{:S(2)}) async-start(s32[16,32,128]{2,1,0:T(8,128)} %dispatch.1), calls=%async_computation | async-start | bytes 524288 | tf_op jit(solution)/shard_map/all_to_all | solution.py:286
  15.9 61.8 %collective-permute-start.6 = (bf16[1024,1024]{1,0:T(8,128)(2,1)}, bf16[1024,1024]{1,0:T(8,128)(2,1)}, u32[]{:S(2)}, u32[]{:S(2)}) collective-permute-start(bf16[1024,1024]{1,0:T(8,128)(2,1)} %refs_10_.3), channel_id=1, source_target_pairs={{0,1},{1,0},{2,3},{3,2},{4,5},{5,4},{6,7},{7,6},{8,9},{9,8},{10,11... | collective-permute-start | bytes 6291464 | tf_op jit(solution)/shard_map/ppermute | solution.py:262
  37.5 29.7 %all-to-all-start.2 = ((bf16[16,256,256]{2,1,0:T(8,128)(2,1)}), bf16[16,256,256]{2,1,0:T(8,128)(2,1)S(1)}, u32[]{:S(2)}, u32[]{:S(2)}) async-start(bf16[16,256,256]{2,1,0:T(8,128)(2,1)} %shard_map.74), calls=%async_computation.2 | async-start | bytes 4194304 | tf_op jit(solution)/shard_map/all_to_all | solution.py:292
  55.6 16.7 %copy-start.2 = (bf16[512,1024]{1,0:T(8,128)(2,1)S(1)}, bf16[512,1024]{1,0:T(8,128)(2,1)}, u32[]{:S(2)}) copy-start(bf16[512,1024]{1,0:T(8,128)(2,1)} %refs_6_.3) | copy-start | bytes 3145732
  55.6 24.5 %copy-start.3 = (f32[1024]{0:T(1024)S(1)}, f32[1024]{0:T(1024)}, u32[]{:S(2)}) copy-start(f32[1024]{0:T(1024)} %param.12) | copy-start | bytes 12292
  67.1 83.3 %all-to-all-start.1 = ((bf16[16,256,256]{2,1,0:T(8,128)(2,1)}), bf16[16,256,256]{2,1,0:T(8,128)(2,1)}, u32[]{:S(2)}, u32[]{:S(2)}) async-start(bf16[16,256,256]{2,1,0:T(8,128)(2,1)} %shard_map.73), calls=%async_computation.1 | async-start | bytes 4194304 | tf_op jit(solution)/shard_map/all_to_all | solution.py:292
  72.3 6.9 %collective-permute-start.3 = (bf16[512,1024]{1,0:T(8,128)(2,1)S(1)}, bf16[512,1024]{1,0:T(8,128)(2,1)}, u32[]{:S(2)}, u32[]{:S(2)}) collective-permute-start(bf16[512,1024]{1,0:T(8,128)(2,1)S(1)} %copy-done.2), channel_id=1, source_target_pairs={{0,1},{1,0},{2,3},{3,2},{4,5},{5,4},{6,7},{7,6},{8,9},{9,8},{10,11... | collective-permute-start | bytes 3145736 | tf_op jit(solution)/shard_map/ppermute | solution.py:262
  76.4 79.4 %collective-permute-start.7 = (bf16[1024,1024]{1,0:T(8,128)(2,1)}, bf16[1024,1024]{1,0:T(8,128)(2,1)}, u32[]{:S(2)}, u32[]{:S(2)}) collective-permute-start(bf16[1024,1024]{1,0:T(8,128)(2,1)} %refs_10_.3), channel_id=1, source_target_pairs={{0,6},{1,3},{2,4},{3,1},{4,2},{5,7},{6,0},{7,5},{8,14},{9,11},{10,... | collective-permute-start | bytes 6291464 | tf_op jit(solution)/shard_map/ppermute | solution.py:248
  77.6 82.7 %collective-permute-start.8 = (bf16[1024,1024]{1,0:T(8,128)(2,1)}, bf16[1024,1024]{1,0:T(8,128)(2,1)}, u32[]{:S(2)}, u32[]{:S(2)}) collective-permute-start(bf16[1024,1024]{1,0:T(8,128)(2,1)} %collective-permute-done.6.refs_11_), channel_id=1, source_target_pairs={{0,6},{1,3},{2,4},{3,1},{4,2},{5,7},{6,0},{7,5},{8,14},{9,11},{10,... | collective-permute-start | bytes 6291464 | tf_op jit(solution)/shard_map/ppermute | solution.py:248
  77.9 77.5 %collective-permute-start.4 = (bf16[512,1024]{1,0:T(8,128)(2,1)S(1)}, bf16[512,1024]{1,0:T(8,128)(2,1)}, u32[]{:S(2)}, u32[]{:S(2)}) collective-permute-start(bf16[512,1024]{1,0:T(8,128)(2,1)S(1)} %copy-done.2), channel_id=1, source_target_pairs={{0,6},{1,3},{2,4},{3,1},{4,2},{5,7},{6,0},{7,5},{8,14},{9,11},{10,... | collective-permute-start | bytes 3145736 | tf_op jit(solution)/shard_map/ppermute | solution.py:248
  79.1 76.7 %collective-permute-start.5 = (bf16[512,1024]{1,0:T(8,128)(2,1)}, bf16[512,1024]{1,0:T(8,128)(2,1)}, u32[]{:S(2)}, u32[]{:S(2)}) collective-permute-start(bf16[512,1024]{1,0:T(8,128)(2,1)} %collective-permute-done.3.refs_7_), channel_id=1, source_target_pairs={{0,6},{1,3},{2,4},{3,1},{4,2},{5,7},{6,0},{7,5},{8,14},{9,11},{10,... | collective-permute-start | bytes 3145736 | tf_op jit(solution)/shard_map/ppermute | solution.py:248
  80.1 66.8 %collective-permute-start.1 = (f32[1,1024]{1,0:T(1,128)S(1)}, f32[1,1024]{1,0:T(1,128)S(1)}, u32[]{:S(2)}, u32[]{:S(2)}) collective-permute-start(f32[1,1024]{1,0:T(1,128)S(1)} %bitcast.6), channel_id=1, source_target_pairs={{0,6},{1,3},{2,4},{3,1},{4,2},{5,7},{6,0},{7,5},{8,14},{9,11},{10,... | collective-permute-start | bytes 12296 | tf_op jit(solution)/shard_map/ppermute | solution.py:248
  146.9 2.9 %collective-permute-start = (f32[1,1024]{1,0:T(1,128)S(1)}, f32[1,1024]{1,0:T(1,128)S(1)}, u32[]{:S(2)}, u32[]{:S(2)}) collective-permute-start(f32[1,1024]{1,0:T(1,128)S(1)} %bitcast.7), channel_id=1, source_target_pairs={{0,1},{1,0},{2,3},{3,2},{4,5},{5,4},{6,7},{7,6},{8,9},{9,8},{10,11... | collective-permute-start | bytes 12296 | tf_op jit(solution)/shard_map/ppermute | solution.py:262
  149.8 3.2 %collective-permute-start.2 = (f32[1,1024]{1,0:T(1,128)S(1)}, f32[1,1024]{1,0:T(1,128)S(1)}, u32[]{:S(2)}, u32[]{:S(2)}) collective-permute-start(f32[1,1024]{1,0:T(1,128)S(1)} %collective-permute-done.refs_3_), channel_id=1, source_target_pairs={{0,6},{1,3},{2,4},{3,1},{4,2},{5,7},{6,0},{7,5},{8,14},{9,11},{10,... | collective-permute-start | bytes 12296 | tf_op jit(solution)/shard_map/ppermute | solution.py:248
  150.4 18.8 %copy-start.1 = (bf16[1024,1024]{1,0:T(8,128)(2,1)S(1)}, bf16[1024,1024]{1,0:T(8,128)(2,1)}, u32[]{:S(2)}) copy-start(bf16[1024,1024]{1,0:T(8,128)(2,1)} %refs_10_.3) | copy-start | bytes 6291460
  153.0 5.1 %collective-permute-start.10 = (bf16[256,256]{1,0:T(8,128)(2,1)S(1)}, bf16[256,256]{1,0:T(8,128)(2,1)S(1)}, u32[]{:S(2)}, u32[]{:S(2)}) collective-permute-start(bf16[256,256]{1,0:T(8,128)(2,1)S(1)} %add.8.refs_1_), channel_id=1, source_target_pairs={{0,2},{1,7},{2,0},{3,5},{4,6},{5,3},{6,4},{7,1},{8,10},{9,15},{10,... | collective-permute-start | bytes 393224 | tf_op jit(solution)/shard_map/ppermute | solution.py:248
  155.3 5.0 %collective-permute-start.9 = (bf16[256,256]{1,0:T(8,128)(2,1)S(1)}, bf16[256,256]{1,0:T(8,128)(2,1)S(1)}, u32[]{:S(2)}, u32[]{:S(2)}) collective-permute-start(bf16[256,256]{1,0:T(8,128)(2,1)S(1)} %add.7.refs_0_), channel_id=1, source_target_pairs={{0,2},{1,7},{2,0},{3,5},{4,6},{5,3},{6,4},{7,1},{8,10},{9,15},{10,... | collective-permute-start | bytes 393224 | tf_op jit(solution)/shard_map/ppermute | solution.py:248
  160.4 1.6 copy-start
  167.5 9.5 %collective-permute-start.11 = (bf16[256,1024]{1,0:T(8,128)(2,1)S(1)}, bf16[256,1024]{1,0:T(8,128)(2,1)S(1)}, u32[]{:S(2)}, u32[]{:S(2)}) collective-permute-start(bf16[256,1024]{1,0:T(8,128)(2,1)S(1)} %shard_map.76), channel_id=1, source_target_pairs={{0,2},{1,7},{2,0},{3,5},{4,6},{5,3},{6,4},{7,1},{8,10},{9,15},{10,... | collective-permute-start | bytes 1572872 | tf_op jit(solution)/shard_map/ppermute | solution.py:248

commit v3 on v1

--- a/solution.py
+++ b/solution.py
@@ -19,7 +19,7 @@
 PIECES = 4
 STEP = 8
 BAG_SHIFT = 13
-CHUNKS = (2, 2)
+EACH = 1
 
 
 def iota(shape, dim):
@@ -30,15 +30,20 @@
     return jnp.where(mask, 1.0, 0.0).astype(jnp.bfloat16)
 
 
-def dispatch_kernel(own_ref, row_ref, out_ref):
+def dispatch_kernel(own_ref, row_ref, length_ref, out_ref):
     before = ones_where(iota((256, 256), 0) < iota((256, 256), 1))
     r, c = iota((256, 256), 0), iota((256, 256), 1)
     earlier = ones_where(((r & 15) == (c & 15)) & ((c >> 4) < (r >> 4)))
     ones = jnp.ones((256, 256), jnp.bfloat16)
     same = ones_where(iota((16, 256), 0) == (iota((16, 256), 1) & 15))
     owner_iota = iota((16, 16, 256), 1)
+    count64 = iota((64, 256), 0).astype(jnp.float32).astype(jnp.bfloat16)
+    count128 = iota((128, 256), 0).astype(jnp.float32).astype(jnp.bfloat16)
+    bag = (iota((1, 256), 1) + 1).astype(jnp.float32).astype(jnp.bfloat16)
+    zero, one = jnp.bfloat16(0), jnp.bfloat16(1)
     for t in range(TABLES):
-        own = own_ref[t]
+        live = iota((BAG, SAMPLES), 0) < length_ref[t : t + 1, :]
+        own = jnp.where(live, own_ref[t], OWNERS)
         mark = (own[:, None, :] == owner_iota).reshape(256, 256)
         onehot = ones_where(mark)
         rank = jnp.dot(onehot, before, preferred_element_type=jnp.float32)
@@ -47,55 +52,78 @@
         rank = jnp.sum(jnp.where(mark, rank, 0.0).reshape(16, 16, 256), axis=1).astype(jnp.int32)
         total = jnp.dot(same, onehot, preferred_element_type=jnp.float32)
         total = jnp.dot(total.astype(jnp.bfloat16), ones, preferred_element_type=jnp.float32)
-        out_ref[:, 16 + t, :] = total[:, :128].astype(jnp.int32)
-        hi = own * 4 + (rank >> 7)
-        lo = rank & 127
+        hi = (own * 4 + (rank >> 7)).astype(jnp.float32)
+        lo = (rank & 127).astype(jnp.float32)
         row = row_ref[t]
         low = (row & 255).astype(jnp.float32)
         high = (row >> 8).astype(jnp.float32)
-        bag = (iota((1, 256), 1) + 1).astype(jnp.float32)
         acc = jnp.zeros((192, 128), jnp.float32)
         for s in range(BAG):
-            left = hi[s : s + 1, :] == iota((64, 256), 0)
+            line = slice(s, s + 1)
+            left = hi[line].astype(jnp.bfloat16) == count64
             planes = jnp.concatenate(
                 [
-                    jnp.where(left, low[s : s + 1, :], 0.0),
-                    jnp.where(left, high[s : s + 1, :], 0.0),
-                    jnp.where(left, bag, 0.0),
+                    jnp.where(left, low[line].astype(jnp.bfloat16), zero),
+                    jnp.where(left, high[line].astype(jnp.bfloat16), zero),
+                    jnp.where(left, bag, zero),
                 ],
                 axis=0,
-            ).astype(jnp.bfloat16)
-            right = ones_where(lo[s : s + 1, :] == iota((128, 256), 0))
+            )
+            right = jnp.where(lo[line].astype(jnp.bfloat16) == count128, one, zero)
             acc += lax.dot_general(
                 planes, right, (((1,), (1,)), ((), ())), preferred_element_type=jnp.float32
             )
         acc = acc.astype(jnp.int32)
         code = acc[:64] | (acc[64:128] << 8) | (acc[128:] << BAG_SHIFT)
-        out_ref[:, 4 * t : 4 * t + 4, :] = code.reshape(OWNERS, 4, 128)
-    out_ref[:, 20:, :] = jnp.zeros((OWNERS, 4, 128), jnp.int32)
-
-
-def pool_kernel(first, lists_ref, table_ref, out_ref, buf_ref, held_ref, rows_vmem, rows_ref, sem, row_sem):
-    tables = held_ref.shape[0]
+        out_ref[:, 8 * t : 8 * t + 4, :] = code.reshape(OWNERS, 4, 128)
+        out_ref[:, 8 * t + 4, :] = total[:, :128].astype(jnp.int32)
+        out_ref[:, 8 * t + 5 : 8 * t + 8, :] = jnp.zeros((OWNERS, 3, 128), jnp.int32)
+
+
+def pool_kernel(first, each, me_ref, lists_ref, table_ref, *refs):
+    outs, (buf_ref, stage_ref, held_ref, rows_vmem, rows_ref, sem, row_sem, out_sem) = (
+        refs[:8],
+        refs[8:],
+    )
+    tables = 2 * each
     turn, part = pl.program_id(0), pl.program_id(1)
+    my_y, my_z = me_ref[0] >> 2, me_ref[0] & 3
 
     def load(t, k):
-        piece = pl.ds(k * (ROWS_DEV // PIECES), ROWS_DEV // PIECES)
+        size = ROWS_DEV // PIECES
         return pltpu.make_async_copy(
-            table_ref.at[first + t, piece], held_ref.at[t, piece], sem.at[t, k]
+            table_ref.at[first + t, pl.ds(k * size, size)],
+            held_ref.at[pl.ds(t * ROWS_DEV + k * size, size)],
+            sem.at[t, k],
         )
 
     def load_rows():
         return pltpu.make_async_copy(rows_vmem, rows_ref, row_sem)
+
+    def unload(t, p, h):
+        slot = (2 * t + p) % 2
+        columns = pl.ds(t % each * EMB, EMB)
+        return pltpu.make_async_copy(
+            stage_ref.at[slot, pl.ds(4 * h, 4)],
+            outs[4 * (t // each) + 2 * p + h].at[:, :, columns],
+            out_sem.at[slot, h],
+        )
+
+    def source_of(place):
+        outer, inner = place >> 2, place & 3
+        step_y = jnp.where(turn < each, outer, inner)
+        step_z = jnp.where(turn < each, inner, outer)
+        return (((my_y + step_y) & 3) << 2) + ((my_z + step_z) & 3)
 
     @pl.when((turn == 0) & (part == 0))
     def _():
         for t in range(tables):
             for k in range(PIECES):
                 load(t, k).start()
-        codes = lists_ref[:, 4 * first : 4 * (first + tables), :]
-        rows_vmem[:, : 4 * tables, :] = codes & (ROWS_DEV - 1)
-        rows_vmem[:, 4 * tables : 5 * tables, :] = lists_ref[:, 16 + first : 16 + first + tables, :]
+        codes = lists_ref[:, 8 * first : 8 * (first + tables), :]
+        line = iota(codes.shape, 1)
+        rows = (codes & (ROWS_DEV - 1)) + (line >> 3) * ROWS_DEV
+        rows_vmem[...] = jnp.where((line & 7) == 4, codes, rows)
         load_rows().start()
         buf_ref[...] = jnp.zeros_like(buf_ref)
         load_rows().wait()
@@ -108,59 +136,126 @@
                 load(t, k).wait()
 
     def fetch(q, carry):
-        source = part * STEP + q
-        count = rows_ref[source, 4 * tables + turn, 0]
+        source = source_of(part * STEP + q)
+        count = rows_ref[source, 8 * turn + 4, 0]
         for line in range(CAP // 128):
             for base in range(0, 128, BLOCK):
 
                 @pl.when(count > line * 128 + base)
                 def _(line=line, base=base):
                     for k in range(base, base + BLOCK):
-                        row = rows_ref[source, 4 * turn + line, k]
-                        buf_ref[q, pl.ds(line * 128 + k, 1), :] = held_ref[turn, pl.ds(row, 1), :]
+                        ids = rows_ref.at[source, 8 * turn + line, pl.ds(k // 8 * 8, 8)]
+                        row = ids[k % 8]
+                        buf_ref[q, pl.ds(line * 128 + k, 1), :] = held_ref[pl.ds(row, 1), :]
 
         return carry
 
     lax.fori_loop(0, STEP, fetch, 0)
+    for t in range(1, tables):
+        for p in range(2):
+
+            @pl.when((turn == t) & (part == p))
+            def _(t=t, p=p):
+                for h in range(2):
+                    unload(t - 1, p, h).wait()
+
     bag = (iota((SAMPLES, 128), 0) + 1).astype(jnp.float32).astype(jnp.bfloat16)
     for q in range(STEP):
-        source = part * STEP + q
+        source = source_of(part * STEP + q)
         picks = []
         for line in range(CAP // 128):
-            named = lists_ref[source, pl.ds(4 * first + 4 * turn + line, 1), :] >> BAG_SHIFT
+            named = lists_ref[source, pl.ds(8 * first + 8 * turn + line, 1), :] >> BAG_SHIFT
             named = named.astype(jnp.float32).astype(jnp.bfloat16)
             picks.append(jnp.where(named == bag, jnp.bfloat16(1), jnp.bfloat16(0)))
-        out_ref[q] = jnp.dot(
+        stage_ref[part, q] = jnp.dot(
             jnp.concatenate(picks, axis=1),
             buf_ref[q].astype(jnp.bfloat16),
             preferred_element_type=jnp.float32,
-        ).astype(out_ref.dtype)
-
-
-def pool_tables(first, tables, lists, table):
-    width = -(-5 * tables // 8) * 8
+        ).astype(stage_ref.dtype)
+    for t in range(tables):
+        for p in range(2):
+
+            @pl.when((turn == t) & (part == p))
+            def _(t=t, p=p):
+                for h in range(2):
+                    unload(t, p, h).start()
+                if t == tables - 1 and p == 1:
+                    for h in range(2):
+                        unload(t, 0, h).wait()
+                    for h in range(2):
+                        unload(t, 1, h).wait()
+
+
+def pool_tables(first, each, me, lists, table):
+    tables = 2 * each
+    vmem = pl.BlockSpec(memory_space=pltpu.VMEM)
+    hbm = pl.BlockSpec(memory_space=pltpu.HBM)
     return pl.pallas_call(
-        functools.partial(pool_kernel, first),
+        functools.partial(pool_kernel, first, each),
         grid=(tables, OWNERS // STEP),
-        in_specs=[
-            pl.BlockSpec(lists.shape, lambda t, i: (0, 0, 0)),
-            pl.BlockSpec(memory_space=pltpu.HBM),
-        ],
-        out_specs=pl.BlockSpec((STEP, SAMPLES, EMB), lambda t, i: (i, 0, t)),
+        in_specs=[pl.BlockSpec(memory_space=pltpu.SMEM), vmem, hbm],
+        out_specs=[hbm] * 8,
         scratch_shapes=[
             pltpu.VMEM((STEP, CAP, EMB), jnp.float32),
-            pltpu.VMEM((tables, ROWS_DEV, EMB), jnp.float32),
-            pltpu.VMEM((OWNERS, width, 128), jnp.int32),
-            pltpu.SMEM((OWNERS, width, 128), jnp.int32),
+            pltpu.VMEM((2, STEP, SAMPLES, EMB), jnp.bfloat16),
+            pltpu.VMEM((tables * ROWS_DEV, EMB), jnp.float32),
+            pltpu.VMEM((OWNERS, 8 * tables, 128), jnp.int32),
+            pltpu.SMEM((OWNERS, 8 * tables, 128), jnp.int32),
             pltpu.SemaphoreType.DMA((tables, PIECES)),
             pltpu.SemaphoreType.DMA(()),
+            pltpu.SemaphoreType.DMA((2, 2)),
         ],
-        out_shape=jax.ShapeDtypeStruct((OWNERS, SAMPLES, tables * EMB), jnp.bfloat16),
-        compiler_params=pltpu.CompilerParams(vmem_limit_bytes=49 << 20),
+        out_shape=[jax.ShapeDtypeStruct((4, SAMPLES, each * EMB), jnp.bfloat16)] * 8,
+        compiler_params=pltpu.CompilerParams(vmem_limit_bytes=48 << 20),
         cost_estimate=pl.CostEstimate(
             flops=10_000_000_000 * tables, transcendentals=0, bytes_accessed=6_000_000
         ),
-    )(lists, table)
+    )(me, lists, table)
+
+
+def add_first_kernel(*refs):
+    ins, outs = refs[:8], refs[8:]
+    for half in range(2):
+        for k in range(4):
+            total = ins[4 * half][k].astype(jnp.float32)
+            for d in range(1, 4):
+                total += ins[4 * half + d][k].astype(jnp.float32)
+            outs[4 * half + k][...] = total.astype(jnp.bfloat16)
+
+
+def add_first(parts):
+    vmem = pl.BlockSpec(memory_space=pltpu.VMEM)
+    return pl.pallas_call(
+        add_first_kernel,
+        in_specs=[vmem] * 8,
+        out_specs=[vmem] * 8,
+        out_shape=[jax.ShapeDtypeStruct(parts[0].shape[1:], jnp.bfloat16)] * 8,
+        compiler_params=pltpu.CompilerParams(vmem_limit_bytes=16 << 20),
+        name="add_first",
+    )(*parts)
+
+
+def add_second_kernel(*refs):
+    ins, out_ref = refs[:8], refs[8]
+    width = ins[0].shape[1]
+    for half in range(2):
+        total = ins[4 * half][...].astype(jnp.float32)
+        for d in range(1, 4):
+            total += ins[4 * half + d][...].astype(jnp.float32)
+        out_ref[:, half * width : (half + 1) * width] = total.astype(jnp.bfloat16)
+
+
+def add_second(parts):
+    vmem = pl.BlockSpec(memory_space=pltpu.VMEM)
+    rows, width = parts[0].shape
+    return pl.pallas_call(
+        add_second_kernel,
+        in_specs=[vmem] * 8,
+        out_specs=vmem,
+        out_shape=jax.ShapeDtypeStruct((rows, 2 * width), jnp.bfloat16),
+        compiler_params=pltpu.CompilerParams(vmem_limit_bytes=16 << 20),
+        name="add_second",
+    )(*parts)
 
 
 def score_kernel(pieces, chunks, *refs):
@@ -232,6 +327,22 @@
     return 3 - x
 
 
+def along(array, axis, shift):
+    if axis == "y":
+        pairs = [(y * 4 + z, (y + shift) % 4 * 4 + z) for y in range(4) for z in range(4)]
+    else:
+        pairs = [(y * 4 + z, y * 4 + (z + shift) % 4) for y in range(4) for z in range(4)]
+    return lax.ppermute(array, "gx", pairs)
+
+
+def moved(parts, axes):
+    out = list(parts)
+    for shift in (2, 1, 3):
+        for half in range(2):
+            out[4 * half + shift] = along(parts[4 * half + shift], axes[half], shift)
+    return out
+
+
 def to_core(array):
     return lax.ppermute(array, "gy", [(k, k ^ 1) for k in range(8)])
 
@@ -246,25 +357,24 @@
     biases, w_in, w_out = zip(own, near, far, far_near)
 
     owner = jnp.transpose(lookup_owner[..., 0], (0, 2, 1))
-    live = jnp.arange(BAG, dtype=jnp.int32)[None, :, None] < bag_length[:, None, :]
-    owner = jnp.where(live, owner, OWNERS)
     row = jnp.transpose(lookup_row, (0, 2, 1))
     lists = pl.pallas_call(
         dispatch_kernel,
-        out_shape=jax.ShapeDtypeStruct((OWNERS, 24, 128), jnp.int32),
+        out_shape=jax.ShapeDtypeStruct((OWNERS, 8 * TABLES, 128), jnp.int32),
         name="dispatch",
-    )(owner, row)
+    )(owner, row, bag_length)
     lists = lax.all_to_all(lists, "gx", 0, 0, tiled=True)
 
+    me = lax.axis_index("gx").astype(jnp.int32).reshape(1)
     mine, theirs = [], []
-    first = 0
-    for number in CHUNKS:
-        share = pool_tables(first, number, lists, table)
-        share = lax.all_to_all(share, "gx", 0, 0, tiled=True)
-        chunk = jnp.sum(share.astype(jnp.float32), axis=0).astype(jnp.bfloat16)
+    for first in range(0, TABLES, 2 * EACH):
+        parts = pool_tables(first, EACH, me, lists, table)
+        parts = moved(parts, "yz")
+        parts = add_first(parts)
+        parts = moved(parts, "zy")
+        chunk = add_second(parts)
         mine.append(chunk)
         theirs.append(to_chip(chunk, (flip, mirror)))
-        first += number
     kept = score(mine, biases, w_in, w_out, jnp.float32)
     sent = score(theirs, biases, w_in, w_out, jnp.bfloat16)
     received = to_chip(sent, (flip, mirror))

time: 181 us -> 191 us (1.055)
  the two profiles are of different devices: /device:TPU:1 before, /device:TPU:2 now
where the time goes in v3:
time: 191 us
  waiting for transfers between devices  113 us (59%)
  Pallas kernels  42.8 us (22%)
  starting transfers between devices  33.1 us (17%)
    ppermute x24, waiting for transfers between devices, along(): return lax.ppermute(array, 'gx', pairs)  93.3 us
    pallas_call x2, Pallas kernels, pool_tables(): pl.pallas_call(functools.partial(pool_kernel, first, each), grid=(tables,...  27.1 us
    ppermute x24, starting transfers between devices, along(): return lax.ppermute(array, 'gx', pairs)  17.9 us
    ppermute x9, waiting for transfers between devices, to_chip(): lax.ppermute(array, 'gy', [(x * 2 + c, targets[c](x) * 2 + c) for x in ra...  13.8 us
    pallas_call x2, Pallas kernels, score(): pl.pallas_call(functools.partial(score_kernel, pieces, chunks), in_specs=...  10.6 us
    all_to_all x1, starting transfers between devices, local(): lists = lax.all_to_all(lists, 'gx', 0, 0, tiled=True)  8.05 us
    ppermute x9, starting transfers between devices, to_chip(): lax.ppermute(array, 'gy', [(x * 2 + c, targets[c](x) * 2 + c) for x in ra...  7.01 us
    all_to_all x1, waiting for transfers between devices, local(): lists = lax.all_to_all(lists, 'gx', 0, 0, tiled=True)  5.54 us
  transfers between devices with their start and end apart: 37, of which 21 were waited for; matrix products, arithmetic and copies ran while one was open for 0% of the time, Pallas kernels for 17%

profile of v3, /device:TPU:2, one launch (start us, length us, event | category | flops | bytes accessed | tf_op | source)
XLA Modules:
  0.0 191.1 jit_solution(854106006291171910)
XLA Ops:
  0.0 1.5 copy.10
  1.5 4.5 %dispatch.1 = s32[16,32,128]{2,1,0:T(8,128)} custom-call(s32[4,16,256]{2,1,0:T(8,128)} %bitcast.12, s32[4,16,256]{2,1,0:T(8,128)} %bitcast.13, s32[4,256]{1,0:T(4,128)} %length_ref.1), custom_call_target="tpu_custom_call" | custom-call | tf_op jit(solution)/shard_map/dispatch/pallas_call | solution.py:361
  6.0 8.0 %all-to-all-start = ((s32[16,32,128]{2,1,0:T(8,128)}), s32[16,32,128]{2,1,0:T(8,128)S(1)}, u32[]{:S(2)}, u32[]{:S(2)}) async-start(s32[16,32,128]{2,1,0:T(8,128)} %dispatch.1), calls=%async_computation | async-start | bytes 524288 | tf_op jit(solution)/shard_map/all_to_all | solution.py:366
  14.0 0.1 collective-permute-start.24
  14.1 1.5 collective-permute-start.25
  15.7 0.0 collective-permute-start.30
  15.7 0.0 collective-permute-done.24.refs_3_
  15.7 1.3 collective-permute-start.26
  17.0 5.5 %all-to-all-done.lists_ref = s32[16,32,128]{2,1,0:T(8,128)S(1)} async-done(((s32[16,32,128]{2,1,0:T(8,128)}), s32[16,32,128]{2,1,0:T(8,128)S(1)}, u32[]{:S(2)}, u32[]{:S(2)}) %all-to-all-start) | async-done | bytes 262176 | tf_op jit(solution)/shard_map/all_to_all | solution.py:366
  22.5 13.6 %shard_map.74 = (bf16[4,256,128]{2,1,0:T(8,128)(2,1)S(1)}, bf16[4,256,128]{2,1,0:T(8,128)(2,1)S(1)}, bf16[4,256,128]{2,1,0:T(8,128)(2,1)S(1)}, bf16[4,256,128]{2...) custom-call(s32[1]{0:T(128)} %bitcast.me_ref, ...), custom_call_target="tpu_custom_call" | custom-call | flops 20000000000 | bytes 6000000 | tf_op jit(solution)/shard_map/pallas_call | solution.py:193
  36.2 0.1 collective-permute-start.12
  36.2 0.1 collective-permute-start.13
  36.3 3.1 %collective-permute-start.14 = (bf16[4,256,128]{2,1,0:T(8,128)(2,1)S(1)}, bf16[4,256,128]{2,1,0:T(8,128)(2,1)S(1)}, u32[]{:S(2)}, u32[]{:S(2)}) collective-permute-start(bf16[4,256,128]{2,1,0:T(8,128)(2,1)S(1)} %get-tuple-element.56), channel_id=1, source_target_pairs={{0,96},{8,104},{16,112},{24,120},{32,0},{40,8},{48,16},{56,24},{64... | collective-permute-start | bytes 786440 | tf_op jit(solution)/shard_map/ppermute | solution.py:335
  39.5 10.3 %collective-permute-done.12.refs_1_ = bf16[4,256,128]{2,1,0:T(8,128)(2,1)S(1)} collective-permute-done((bf16[4,256,128]{2,1,0:T(8,128)(2,1)S(1)}, bf16[4,256,128]{2,1,0:T(8,128)(2,1)S(1)}, u32[]{:S(2)}, u32[]{:S(2)}) %collective-permute-start.12) | collective-permute-done | bytes 262176 | tf_op jit(solution)/shard_map/ppermute | solution.py:335
  49.8 1.6 collective-permute-start.31
  51.4 0.0 collective-permute-done.13.refs_2_
  51.4 0.0 collective-permute-done.14.refs_3_
  51.4 0.1 collective-permute-start.16
  51.5 1.1 collective-permute-start.17
  52.5 0.4 collective-permute-start.32
  53.0 13.4 %shard_map.73 = (bf16[4,256,128]{2,1,0:T(8,128)(2,1)S(1)}, bf16[4,256,128]{2,1,0:T(8,128)(2,1)S(1)}, bf16[4,256,128]{2,1,0:T(8,128)(2,1)S(1)}, bf16[4,256,128]{2...) custom-call(s32[1]{0:T(128)} %bitcast.me_ref, ...), custom_call_target="tpu_custom_call" | custom-call | flops 20000000000 | bytes 6000000 | tf_op jit(solution)/shard_map/pallas_call | solution.py:193
  66.4 0.0 collective-permute-done.16.refs_6_
  66.4 0.1 collective-permute-start
  66.5 1.7 collective-permute-start.1
  68.2 13.8 %collective-permute-done.refs_1_ = bf16[4,256,128]{2,1,0:T(8,128)(2,1)S(1)} collective-permute-done((bf16[4,256,128]{2,1,0:T(8,128)(2,1)S(1)}, bf16[4,256,128]{2,1,0:T(8,128)(2,1)S(1)}, u32[]{:S(2)}, u32[]{:S(2)}) %collective-permute-start) | collective-permute-done | bytes 262176 | tf_op jit(solution)/shard_map/ppermute | solution.py:335
  82.0 8.5 %collective-permute-done.2.refs_3_ = bf16[4,256,128]{2,1,0:T(8,128)(2,1)S(1)} collective-permute-done((bf16[4,256,128]{2,1,0:T(8,128)(2,1)S(1)}, bf16[4,256,128]{2,1,0:T(8,128)(2,1)S(1)}, u32[]{:S(2)}, u32[]{:S(2)}) %collective-permute-start.2) | collective-permute-done | bytes 262176 | tf_op jit(solution)/shard_map/ppermute | solution.py:335
  90.6 0.1 collective-permute-start.4
  90.7 1.4 collective-permute-done.3.refs_5_
  92.1 1.7 collective-permute-start.5
  93.9 0.3 add_first.3
  94.1 0.0 copy-start.2
  94.1 5.6 %collective-permute-done.4.refs_6_ = bf16[4,256,128]{2,1,0:T(8,128)(2,1)S(1)} collective-permute-done((bf16[4,256,128]{2,1,0:T(8,128)(2,1)S(1)}, bf16[4,256,128]{2,1,0:T(8,128)(2,1)S(1)}, u32[]{:S(2)}, u32[]{:S(2)}) %collective-permute-start.4) | collective-permute-done | bytes 262176 | tf_op jit(solution)/shard_map/ppermute | solution.py:335
  99.8 2.1 %collective-permute-start.18 = (bf16[256,128]{1,0:T(8,128)(2,1)S(1)}, bf16[256,128]{1,0:T(8,128)(2,1)S(1)}, u32[]{:S(2)}, u32[]{:S(2)}) collective-permute-start(bf16[256,128]{1,0:T(8,128)(2,1)S(1)} %get-tuple-element.62), channel_id=1, source_target_pairs={{0,8},{8,16},{16,24},{24,0},{32,40},{40,48},{48,56},{56,32},{64,72... | collective-permute-start | bytes 196616 | tf_op jit(solution)/shard_map/ppermute | solution.py:335
  101.9 3.8 %collective-permute-done.5.refs_7_ = bf16[4,256,128]{2,1,0:T(8,128)(2,1)S(1)} collective-permute-done((bf16[4,256,128]{2,1,0:T(8,128)(2,1)S(1)}, bf16[4,256,128]{2,1,0:T(8,128)(2,1)S(1)}, u32[]{:S(2)}, u32[]{:S(2)}) %collective-permute-start.5) | collective-permute-done | bytes 262176 | tf_op jit(solution)/shard_map/ppermute | solution.py:335
  105.7 2.0 %collective-permute-start.29 = (bf16[512,1024]{1,0:T(8,128)(2,1)S(1)}, bf16[512,1024]{1,0:T(8,128)(2,1)S(1)}, u32[]{:S(2)}, u32[]{:S(2)}) collective-permute-start(bf16[512,1024]{1,0:T(8,128)(2,1)S(1)} %collective-permute-done.27.refs_7_), channel_id=1, source_target_pairs={{0,6},{1,3},{2,4},{3,1},{4,2},{5,7},{6,0},{7,5},{8,14},{9,11},{10,... | collective-permute-start | bytes 3145736 | tf_op jit(solution)/shard_map/ppermute | solution.py:317
  107.8 0.9 collective-permute-start.19
  108.6 4.9 %collective-permute-done.19.refs_2_ = bf16[256,128]{1,0:T(8,128)(2,1)S(1)} collective-permute-done((bf16[256,128]{1,0:T(8,128)(2,1)S(1)}, bf16[256,128]{1,0:T(8,128)(2,1)S(1)}, u32[]{:S(2)}, u32[]{:S(2)}) %collective-permute-start.19) | collective-permute-done | bytes 65568 | tf_op jit(solution)/shard_map/ppermute | solution.py:335
  113.5 2.6 %collective-permute-start.20 = (bf16[256,128]{1,0:T(8,128)(2,1)S(1)}, bf16[256,128]{1,0:T(8,128)(2,1)S(1)}, u32[]{:S(2)}, u32[]{:S(2)}) collective-permute-start(bf16[256,128]{1,0:T(8,128)(2,1)S(1)} %get-tuple-element.64), channel_id=1, source_target_pairs={{0,24},{8,0},{16,8},{24,16},{32,56},{40,32},{48,40},{56,48},{64,88... | collective-permute-start | bytes 196616 | tf_op jit(solution)/shard_map/ppermute | solution.py:335
  116.1 1.9 collective-permute-done.20.refs_3_
  118.0 0.1 collective-permute-start.21
  118.2 6.1 %collective-permute-done.21.refs_5_ = bf16[256,128]{1,0:T(8,128)(2,1)S(1)} collective-permute-done((bf16[256,128]{1,0:T(8,128)(2,1)S(1)}, bf16[256,128]{1,0:T(8,128)(2,1)S(1)}, u32[]{:S(2)}, u32[]{:S(2)}) %collective-permute-start.21) | collective-permute-done | bytes 65568 | tf_op jit(solution)/shard_map/ppermute | solution.py:335
  124.2 5.8 %collective-permute-done.22.refs_6_ = bf16[256,128]{1,0:T(8,128)(2,1)S(1)} collective-permute-done((bf16[256,128]{1,0:T(8,128)(2,1)S(1)}, bf16[256,128]{1,0:T(8,128)(2,1)S(1)}, u32[]{:S(2)}, u32[]{:S(2)}) %collective-permute-start.22) | collective-permute-done | bytes 65568 | tf_op jit(solution)/shard_map/ppermute | solution.py:335
  130.0 0.2 collective-permute-start.23
  130.2 0.3 add_first.2
  130.5 3.8 %collective-permute-done.23.refs_7_ = bf16[256,128]{1,0:T(8,128)(2,1)S(1)} collective-permute-done((bf16[256,128]{1,0:T(8,128)(2,1)S(1)}, bf16[256,128]{1,0:T(8,128)(2,1)S(1)}, u32[]{:S(2)}, u32[]{:S(2)}) %collective-permute-start.23) | collective-permute-done | bytes 65568 | tf_op jit(solution)/shard_map/ppermute | solution.py:335
  134.3 5.8 %collective-permute-done.6.refs_1_ = bf16[256,128]{1,0:T(8,128)(2,1)S(1)} collective-permute-done((bf16[256,128]{1,0:T(8,128)(2,1)S(1)}, bf16[256,128]{1,0:T(8,128)(2,1)S(1)}, u32[]{:S(2)}, u32[]{:S(2)}) %collective-permute-start.6) | collective-permute-done | bytes 65568 | tf_op jit(solution)/shard_map/ppermute | solution.py:335
  140.1 1.1 collective-permute-start.7
  141.2 4.6 %collective-permute-done.7.refs_2_ = bf16[256,128]{1,0:T(8,128)(2,1)S(1)} collective-permute-done((bf16[256,128]{1,0:T(8,128)(2,1)S(1)}, bf16[256,128]{1,0:T(8,128)(2,1)S(1)}, u32[]{:S(2)}, u32[]{:S(2)}) %collective-permute-start.7) | collective-permute-done | bytes 65568 | tf_op jit(solution)/shard_map/ppermute | solution.py:335
  145.8 2.0 %collective-permute-start.8 = (bf16[256,128]{1,0:T(8,128)(2,1)S(1)}, bf16[256,128]{1,0:T(8,128)(2,1)S(1)}, u32[]{:S(2)}, u32[]{:S(2)}) collective-permute-start(bf16[256,128]{1,0:T(8,128)(2,1)S(1)} %get-tuple-element.48), channel_id=1, source_target_pairs={{0,24},{8,0},{16,8},{24,16},{32,56},{40,32},{48,40},{56,48},{64,88... | collective-permute-start | bytes 196616 | tf_op jit(solution)/shard_map/ppermute | solution.py:335
  147.9 2.2 %collective-permute-done.8.refs_3_ = bf16[256,128]{1,0:T(8,128)(2,1)S(1)} collective-permute-done((bf16[256,128]{1,0:T(8,128)(2,1)S(1)}, bf16[256,128]{1,0:T(8,128)(2,1)S(1)}, u32[]{:S(2)}, u32[]{:S(2)}) %collective-permute-start.8) | collective-permute-done | bytes 65568 | tf_op jit(solution)/shard_map/ppermute | solution.py:335
  150.1 5.5 %collective-permute-done.9.refs_5_ = bf16[256,128]{1,0:T(8,128)(2,1)S(1)} collective-permute-done((bf16[256,128]{1,0:T(8,128)(2,1)S(1)}, bf16[256,128]{1,0:T(8,128)(2,1)S(1)}, u32[]{:S(2)}, u32[]{:S(2)}) %collective-permute-start.9) | collective-permute-done | bytes 65568 | tf_op jit(solution)/shard_map/ppermute | solution.py:335
  155.6 5.8 %collective-permute-done.10.refs_6_ = bf16[256,128]{1,0:T(8,128)(2,1)S(1)} collective-permute-done((bf16[256,128]{1,0:T(8,128)(2,1)S(1)}, bf16[256,128]{1,0:T(8,128)(2,1)S(1)}, u32[]{:S(2)}, u32[]{:S(2)}) %collective-permute-start.10) | collective-permute-done | bytes 65568 | tf_op jit(solution)/shard_map/ppermute | solution.py:335
  161.4 0.7 collective-permute-start.11
  162.0 0.1 add_second.3.refs_1_
  162.1 3.5 %collective-permute-done.11.refs_7_ = bf16[256,128]{1,0:T(8,128)(2,1)S(1)} collective-permute-done((bf16[256,128]{1,0:T(8,128)(2,1)S(1)}, bf16[256,128]{1,0:T(8,128)(2,1)S(1)}, u32[]{:S(2)}, u32[]{:S(2)}) %collective-permute-start.11) | collective-permute-done | bytes 65568 | tf_op jit(solution)/shard_map/ppermute | solution.py:335
  165.6 0.1 add_second.2.refs_0_
  165.7 4.9 %collective-permute-done.34.refs_1_ = bf16[256,256]{1,0:T(8,128)(2,1)S(1)} collective-permute-done((bf16[256,256]{1,0:T(8,128)(2,1)S(1)}, bf16[256,256]{1,0:T(8,128)(2,1)S(1)}, u32[]{:S(2)}, u32[]{:S(2)}) %collective-permute-start.34) | collective-permute-done | bytes 131104 | tf_op jit(solution)/shard_map/ppermute | solution.py:317
  170.6 0.0 collective-permute-start.33
  170.6 5.0 %collective-permute-done.33.refs_0_ = bf16[256,256]{1,0:T(8,128)(2,1)S(1)} collective-permute-done((bf16[256,256]{1,0:T(8,128)(2,1)S(1)}, bf16[256,256]{1,0:T(8,128)(2,1)S(1)}, u32[]{:S(2)}, u32[]{:S(2)}) %collective-permute-start.33) | collective-permute-done | bytes 131104 | tf_op jit(solution)/shard_map/ppermute | solution.py:317
  175.6 5.3 %shard_map.76 = bf16[256,1024]{1,0:T(8,128)(2,1)S(1)} custom-call(bf16[256,256]{1,0:T(8,128)(2,1)S(1)} %collective-permute-done.33.refs_0_, bf16[256,256]{1,0:T(8,128)(2,1)S(1)} %collective-permute-done.34.refs_1_, f32[1,1024]{1,0:T(1,128)S(1)} %bitcast.10, f32[1,1024]{1,0:T(1,128)S(1)} %collective-permute-done.24.refs_3_, ...), custom_call_target="tpu_custom_call" | custom-call | flops 10000000000 | bytes 14000000 | tf_op jit(solution)/shard_map/pallas_call | solution.py:298
  180.9 0.1 collective-permute-start.35
  181.0 5.3 %shard_map.75 = f32[256,1024]{1,0:T(8,128)S(1)} custom-call(bf16[256,256]{1,0:T(8,128)(2,1)S(1)} %add_second.2.refs_0_, bf16[256,256]{1,0:T(8,128)(2,1)S(1)} %add_second.3.refs_1_, f32[1,1024]{1,0:T(1,128)S(1)} %bitcast.11, f32[1,1024]{1,0:T(1,128)S(1)} %collective-permute-done.24.refs_3_, f32[1,1024]{1,0:T(1,128)S(1)} %collective-permute-done.25.refs_4_, ...), custom_call_target="tpu_custom_call" | custom-call | flops 10000000000 | bytes 14000000 | tf_op jit(solution)/shard_map/pallas_call | solution.py:298
  186.2 3.9 %collective-permute-done.35 = bf16[256,1024]{1,0:T(8,128)(2,1)S(1)} collective-permute-done((bf16[256,1024]{1,0:T(8,128)(2,1)S(1)}, bf16[256,1024]{1,0:T(8,128)(2,1)S(1)}, u32[]{:S(2)}, u32[]{:S(2)}) %collective-permute-start.35) | collective-permute-done | bytes 524320 | tf_op jit(solution)/shard_map/ppermute | solution.py:317
  190.1 0.9 add_convert_fusion
  (27 shorter events, 0.1 us)
Async XLA Ops:
  6.0 16.6 %all-to-all-start = ((s32[16,32,128]{2,1,0:T(8,128)}), s32[16,32,128]{2,1,0:T(8,128)S(1)}, u32[]{:S(2)}, u32[]{:S(2)}) async-start(s32[16,32,128]{2,1,0:T(8,128)} %dispatch.1), calls=%async_computation | async-start | bytes 524288 | tf_op jit(solution)/shard_map/all_to_all | solution.py:366
  14.0 1.6 collective-permute-start.24
  14.1 22.2 %collective-permute-start.25 = (f32[1,1024]{1,0:T(1,128)}, f32[1,1024]{1,0:T(1,128)S(1)}, u32[]{:S(2)}, u32[]{:S(2)}) collective-permute-start(f32[1,1024]{1,0:T(1,128)} %bitcast.9), channel_id=1, source_target_pairs={{0,6},{1,3},{2,4},{3,1},{4,2},{5,7},{6,0},{7,5},{8,14},{9,11},{10,... | collective-permute-start | bytes 12296 | tf_op jit(solution)/shard_map/ppermute | solution.py:317
  15.7 36.9 %collective-permute-start.30 = (bf16[1024,1024]{1,0:T(8,128)(2,1)}, bf16[1024,1024]{1,0:T(8,128)(2,1)S(1)}, u32[]{:S(2)}, u32[]{:S(2)}) collective-permute-start(bf16[1024,1024]{1,0:T(8,128)(2,1)} %refs_10_.3), channel_id=1, source_target_pairs={{0,1},{1,0},{2,3},{3,2},{4,5},{5,4},{6,7},{7,6},{8,9},{9,8},{10,11... | collective-permute-start | bytes 6291464 | tf_op jit(solution)/shard_map/ppermute | solution.py:347
  15.7 23.8 %collective-permute-start.26 = (f32[1,1024]{1,0:T(1,128)S(1)}, f32[1,1024]{1,0:T(1,128)S(1)}, u32[]{:S(2)}, u32[]{:S(2)}) collective-permute-start(f32[1,1024]{1,0:T(1,128)S(1)} %collective-permute-done.24.refs_3_), channel_id=1, source_target_pairs={{0,6},{1,3},{2,4},{3,1},{4,2},{5,7},{6,0},{7,5},{8,14},{9,11},{10,... | collective-permute-start | bytes 12296 | tf_op jit(solution)/shard_map/ppermute | solution.py:317
  22.5 27.2 %copy-start = (bf16[1024,1024]{1,0:T(8,128)(2,1)S(1)}, bf16[1024,1024]{1,0:T(8,128)(2,1)}, u32[]{:S(2)}) copy-start(bf16[1024,1024]{1,0:T(8,128)(2,1)} %refs_10_.3) | copy-start | bytes 6291460
  22.5 28.8 %copy-start.1 = (bf16[512,1024]{1,0:T(8,128)(2,1)S(1)}, bf16[512,1024]{1,0:T(8,128)(2,1)}, u32[]{:S(2)}) copy-start(bf16[512,1024]{1,0:T(8,128)(2,1)} %refs_6_.3) | copy-start | bytes 3145732
  36.2 13.6 %collective-permute-start.12 = (bf16[4,256,128]{2,1,0:T(8,128)(2,1)S(1)}, bf16[4,256,128]{2,1,0:T(8,128)(2,1)S(1)}, u32[]{:S(2)}, u32[]{:S(2)}) collective-permute-start(bf16[4,256,128]{2,1,0:T(8,128)(2,1)S(1)} %get-tuple-element.54), channel_id=1, source_target_pairs={{0,32},{8,40},{16,48},{24,56},{32,64},{40,72},{48,80},{56,88},{64,... | collective-permute-start | bytes 786440 | tf_op jit(solution)/shard_map/ppermute | solution.py:335
  36.2 15.1 %collective-permute-start.13 = (bf16[4,256,128]{2,1,0:T(8,128)(2,1)S(1)}, bf16[4,256,128]{2,1,0:T(8,128)(2,1)S(1)}, u32[]{:S(2)}, u32[]{:S(2)}) collective-permute-start(bf16[4,256,128]{2,1,0:T(8,128)(2,1)S(1)} %get-tuple-element.55), channel_id=1, source_target_pairs={{0,64},{8,72},{16,80},{24,88},{32,96},{40,104},{48,112},{56,120},{... | collective-permute-start | bytes 786440 | tf_op jit(solution)/shard_map/ppermute | solution.py:335
  36.3 15.0 %collective-permute-start.14 = (bf16[4,256,128]{2,1,0:T(8,128)(2,1)S(1)}, bf16[4,256,128]{2,1,0:T(8,128)(2,1)S(1)}, u32[]{:S(2)}, u32[]{:S(2)}) collective-permute-start(bf16[4,256,128]{2,1,0:T(8,128)(2,1)S(1)} %get-tuple-element.56), channel_id=1, source_target_pairs={{0,96},{8,104},{16,112},{24,120},{32,0},{40,8},{48,16},{56,24},{64... | collective-permute-start | bytes 786440 | tf_op jit(solution)/shard_map/ppermute | solution.py:335
  39.5 12.0 %collective-permute-start.15 = (bf16[4,256,128]{2,1,0:T(8,128)(2,1)S(1)}, bf16[4,256,128]{2,1,0:T(8,128)(2,1)S(1)}, u32[]{:S(2)}, u32[]{:S(2)}) collective-permute-start(bf16[4,256,128]{2,1,0:T(8,128)(2,1)S(1)} %get-tuple-element.58), channel_id=1, source_target_pairs={{0,8},{8,16},{16,24},{24,0},{32,40},{40,48},{48,56},{56,32},{64,72... | collective-permute-start | bytes 786440 | tf_op jit(solution)/shard_map/ppermute | solution.py:335
  49.8 125.8 %collective-permute-start.31 = (bf16[1024,1024]{1,0:T(8,128)(2,1)S(1)}, bf16[1024,1024]{1,0:T(8,128)(2,1)S(1)}, u32[]{:S(2)}, u32[]{:S(2)}) collective-permute-start(bf16[1024,1024]{1,0:T(8,128)(2,1)S(1)} %copy-done), channel_id=1, source_target_pairs={{0,6},{1,3},{2,4},{3,1},{4,2},{5,7},{6,0},{7,5},{8,14},{9,11},{10,... | collective-permute-start | bytes 6291464 | tf_op jit(solution)/shard_map/ppermute | solution.py:317
  51.4 54.4 %collective-permute-start.27 = (bf16[512,1024]{1,0:T(8,128)(2,1)S(1)}, bf16[512,1024]{1,0:T(8,128)(2,1)S(1)}, u32[]{:S(2)}, u32[]{:S(2)}) collective-permute-start(bf16[512,1024]{1,0:T(8,128)(2,1)S(1)} %copy-done.1), channel_id=1, source_target_pairs={{0,1},{1,0},{2,3},{3,2},{4,5},{5,4},{6,7},{7,6},{8,9},{9,8},{10,11... | collective-permute-start | bytes 3145736 | tf_op jit(solution)/shard_map/ppermute | solution.py:347
  51.4 15.1 %collective-permute-start.16 = (bf16[4,256,128]{2,1,0:T(8,128)(2,1)S(1)}, bf16[4,256,128]{2,1,0:T(8,128)(2,1)S(1)}, u32[]{:S(2)}, u32[]{:S(2)}) collective-permute-start(bf16[4,256,128]{2,1,0:T(8,128)(2,1)S(1)} %get-tuple-element.59), channel_id=1, source_target_pairs={{0,16},{8,24},{16,0},{24,8},{32,48},{40,56},{48,32},{56,40},{64,80... | collective-permute-start | bytes 786440 | tf_op jit(solution)/shard_map/ppermute | solution.py:335
  51.5 15.1 %collective-permute-start.17 = (bf16[4,256,128]{2,1,0:T(8,128)(2,1)S(1)}, bf16[4,256,128]{2,1,0:T(8,128)(2,1)S(1)}, u32[]{:S(2)}, u32[]{:S(2)}) collective-permute-start(bf16[4,256,128]{2,1,0:T(8,128)(2,1)S(1)} %get-tuple-element.60), channel_id=1, source_target_pairs={{0,24},{8,0},{16,8},{24,16},{32,56},{40,32},{48,40},{56,48},{64,88... | collective-permute-start | bytes 786440 | tf_op jit(solution)/shard_map/ppermute | solution.py:335
  52.5 123.0 %collective-permute-start.32 = (bf16[1024,1024]{1,0:T(8,128)(2,1)S(1)}, bf16[1024,1024]{1,0:T(8,128)(2,1)S(1)}, u32[]{:S(2)}, u32[]{:S(2)}) collective-permute-start(bf16[1024,1024]{1,0:T(8,128)(2,1)S(1)} %collective-permute-done.30.refs_11_), channel_id=1, source_target_pairs={{0,6},{1,3},{2,4},{3,1},{4,2},{5,7},{6,0},{7,5},{8,14},{9,11},{10,... | collective-permute-start | bytes 6291464 | tf_op jit(solution)/shard_map/ppermute | solution.py:317
  66.4 15.5 %collective-permute-start = (bf16[4,256,128]{2,1,0:T(8,128)(2,1)S(1)}, bf16[4,256,128]{2,1,0:T(8,128)(2,1)S(1)}, u32[]{:S(2)}, u32[]{:S(2)}) collective-permute-start(bf16[4,256,128]{2,1,0:T(8,128)(2,1)S(1)} %get-tuple-element.38), channel_id=1, source_target_pairs={{0,32},{8,40},{16,48},{24,56},{32,64},{40,72},{48,80},{56,88},{64,... | collective-permute-start | bytes 786440 | tf_op jit(solution)/shard_map/ppermute | solution.py:335
  66.5 15.5 %collective-permute-start.1 = (bf16[4,256,128]{2,1,0:T(8,128)(2,1)S(1)}, bf16[4,256,128]{2,1,0:T(8,128)(2,1)S(1)}, u32[]{:S(2)}, u32[]{:S(2)}) collective-permute-start(bf16[4,256,128]{2,1,0:T(8,128)(2,1)S(1)} %get-tuple-element.39), channel_id=1, source_target_pairs={{0,64},{8,72},{16,80},{24,88},{32,96},{40,104},{48,112},{56,120},{... | collective-permute-start | bytes 786440 | tf_op jit(solution)/shard_map/ppermute | solution.py:335
  82.0 8.6 %collective-permute-start.2 = (bf16[4,256,128]{2,1,0:T(8,128)(2,1)S(1)}, bf16[4,256,128]{2,1,0:T(8,128)(2,1)S(1)}, u32[]{:S(2)}, u32[]{:S(2)}) collective-permute-start(bf16[4,256,128]{2,1,0:T(8,128)(2,1)S(1)} %get-tuple-element.40), channel_id=1, source_target_pairs={{0,96},{8,104},{16,112},{24,120},{32,0},{40,8},{48,16},{56,24},{64... | collective-permute-start | bytes 786440 | tf_op jit(solution)/shard_map/ppermute | solution.py:335
  82.0 10.1 %collective-permute-start.3 = (bf16[4,256,128]{2,1,0:T(8,128)(2,1)S(1)}, bf16[4,256,128]{2,1,0:T(8,128)(2,1)S(1)}, u32[]{:S(2)}, u32[]{:S(2)}) collective-permute-start(bf16[4,256,128]{2,1,0:T(8,128)(2,1)S(1)} %get-tuple-element.42), channel_id=1, source_target_pairs={{0,8},{8,16},{16,24},{24,0},{32,40},{40,48},{48,56},{56,32},{64,72... | collective-permute-start | bytes 786440 | tf_op jit(solution)/shard_map/ppermute | solution.py:335
  90.6 9.2 %collective-permute-start.4 = (bf16[4,256,128]{2,1,0:T(8,128)(2,1)S(1)}, bf16[4,256,128]{2,1,0:T(8,128)(2,1)S(1)}, u32[]{:S(2)}, u32[]{:S(2)}) collective-permute-start(bf16[4,256,128]{2,1,0:T(8,128)(2,1)S(1)} %get-tuple-element.43), channel_id=1, source_target_pairs={{0,16},{8,24},{16,0},{24,8},{32,48},{40,56},{48,32},{56,40},{64,80... | collective-permute-start | bytes 786440 | tf_op jit(solution)/shard_map/ppermute | solution.py:335
  92.1 13.6 %collective-permute-start.5 = (bf16[4,256,128]{2,1,0:T(8,128)(2,1)S(1)}, bf16[4,256,128]{2,1,0:T(8,128)(2,1)S(1)}, u32[]{:S(2)}, u32[]{:S(2)}) collective-permute-start(bf16[4,256,128]{2,1,0:T(8,128)(2,1)S(1)} %get-tuple-element.44), channel_id=1, source_target_pairs={{0,24},{8,0},{16,8},{24,16},{32,56},{40,32},{48,40},{56,48},{64,88... | collective-permute-start | bytes 786440 | tf_op jit(solution)/shard_map/ppermute | solution.py:335
  94.1 81.5 %copy-start.2 = (f32[1024]{0:T(1024)S(1)}, f32[1024]{0:T(1024)}, u32[]{:S(2)}) copy-start(f32[1024]{0:T(1024)} %param.12) | copy-start | bytes 12292
  99.8 8.0 %collective-permute-start.18 = (bf16[256,128]{1,0:T(8,128)(2,1)S(1)}, bf16[256,128]{1,0:T(8,128)(2,1)S(1)}, u32[]{:S(2)}, u32[]{:S(2)}) collective-permute-start(bf16[256,128]{1,0:T(8,128)(2,1)S(1)} %get-tuple-element.62), channel_id=1, source_target_pairs={{0,8},{8,16},{16,24},{24,0},{32,40},{40,48},{48,56},{56,32},{64,72... | collective-permute-start | bytes 196616 | tf_op jit(solution)/shard_map/ppermute | solution.py:335
  105.7 69.8 %collective-permute-start.28 = (bf16[512,1024]{1,0:T(8,128)(2,1)S(1)}, bf16[512,1024]{1,0:T(8,128)(2,1)S(1)}, u32[]{:S(2)}, u32[]{:S(2)}) collective-permute-start(bf16[512,1024]{1,0:T(8,128)(2,1)S(1)} %copy-done.1), channel_id=1, source_target_pairs={{0,6},{1,3},{2,4},{3,1},{4,2},{5,7},{6,0},{7,5},{8,14},{9,11},{10,... | collective-permute-start | bytes 3145736 | tf_op jit(solution)/shard_map/ppermute | solution.py:317
  105.7 69.8 %collective-permute-start.29 = (bf16[512,1024]{1,0:T(8,128)(2,1)S(1)}, bf16[512,1024]{1,0:T(8,128)(2,1)S(1)}, u32[]{:S(2)}, u32[]{:S(2)}) collective-permute-start(bf16[512,1024]{1,0:T(8,128)(2,1)S(1)} %collective-permute-done.27.refs_7_), channel_id=1, source_target_pairs={{0,6},{1,3},{2,4},{3,1},{4,2},{5,7},{6,0},{7,5},{8,14},{9,11},{10,... | collective-permute-start | bytes 3145736 | tf_op jit(solution)/shard_map/ppermute | solution.py:317
  107.8 5.8 %collective-permute-start.19 = (bf16[256,128]{1,0:T(8,128)(2,1)S(1)}, bf16[256,128]{1,0:T(8,128)(2,1)S(1)}, u32[]{:S(2)}, u32[]{:S(2)}) collective-permute-start(bf16[256,128]{1,0:T(8,128)(2,1)S(1)} %get-tuple-element.63), channel_id=1, source_target_pairs={{0,16},{8,24},{16,0},{24,8},{32,48},{40,56},{48,32},{56,40},{64,80... | collective-permute-start | bytes 196616 | tf_op jit(solution)/shard_map/ppermute | solution.py:335
  113.5 4.5 %collective-permute-start.20 = (bf16[256,128]{1,0:T(8,128)(2,1)S(1)}, bf16[256,128]{1,0:T(8,128)(2,1)S(1)}, u32[]{:S(2)}, u32[]{:S(2)}) collective-permute-start(bf16[256,128]{1,0:T(8,128)(2,1)S(1)} %get-tuple-element.64), channel_id=1, source_target_pairs={{0,24},{8,0},{16,8},{24,16},{32,56},{40,32},{48,40},{56,48},{64,88... | collective-permute-start | bytes 196616 | tf_op jit(solution)/shard_map/ppermute | solution.py:335
  118.0 6.2 %collective-permute-start.21 = (bf16[256,128]{1,0:T(8,128)(2,1)S(1)}, bf16[256,128]{1,0:T(8,128)(2,1)S(1)}, u32[]{:S(2)}, u32[]{:S(2)}) collective-permute-start(bf16[256,128]{1,0:T(8,128)(2,1)S(1)} %get-tuple-element.66), channel_id=1, source_target_pairs={{0,32},{8,40},{16,48},{24,56},{32,64},{40,72},{48,80},{56,88},{64,... | collective-permute-start | bytes 196616 | tf_op jit(solution)/shard_map/ppermute | solution.py:335
  124.2 5.8 %collective-permute-start.22 = (bf16[256,128]{1,0:T(8,128)(2,1)S(1)}, bf16[256,128]{1,0:T(8,128)(2,1)S(1)}, u32[]{:S(2)}, u32[]{:S(2)}) collective-permute-start(bf16[256,128]{1,0:T(8,128)(2,1)S(1)} %get-tuple-element.67), channel_id=1, source_target_pairs={{0,64},{8,72},{16,80},{24,88},{32,96},{40,104},{48,112},{56,120},{... | collective-permute-start | bytes 196616 | tf_op jit(solution)/shard_map/ppermute | solution.py:335
  130.0 4.3 %collective-permute-start.23 = (bf16[256,128]{1,0:T(8,128)(2,1)S(1)}, bf16[256,128]{1,0:T(8,128)(2,1)S(1)}, u32[]{:S(2)}, u32[]{:S(2)}) collective-permute-start(bf16[256,128]{1,0:T(8,128)(2,1)S(1)} %get-tuple-element.68), channel_id=1, source_target_pairs={{0,96},{8,104},{16,112},{24,120},{32,0},{40,8},{48,16},{56,24},{64... | collective-permute-start | bytes 196616 | tf_op jit(solution)/shard_map/ppermute | solution.py:335
  134.3 5.8 %collective-permute-start.6 = (bf16[256,128]{1,0:T(8,128)(2,1)S(1)}, bf16[256,128]{1,0:T(8,128)(2,1)S(1)}, u32[]{:S(2)}, u32[]{:S(2)}) collective-permute-start(bf16[256,128]{1,0:T(8,128)(2,1)S(1)} %get-tuple-element.46), channel_id=1, source_target_pairs={{0,8},{8,16},{16,24},{24,0},{32,40},{40,48},{48,56},{56,32},{64,72... | collective-permute-start | bytes 196616 | tf_op jit(solution)/shard_map/ppermute | solution.py:335
  140.1 5.8 %collective-permute-start.7 = (bf16[256,128]{1,0:T(8,128)(2,1)S(1)}, bf16[256,128]{1,0:T(8,128)(2,1)S(1)}, u32[]{:S(2)}, u32[]{:S(2)}) collective-permute-start(bf16[256,128]{1,0:T(8,128)(2,1)S(1)} %get-tuple-element.47), channel_id=1, source_target_pairs={{0,16},{8,24},{16,0},{24,8},{32,48},{40,56},{48,32},{56,40},{64,80... | collective-permute-start | bytes 196616 | tf_op jit(solution)/shard_map/ppermute | solution.py:335
  145.8 4.3 %collective-permute-start.8 = (bf16[256,128]{1,0:T(8,128)(2,1)S(1)}, bf16[256,128]{1,0:T(8,128)(2,1)S(1)}, u32[]{:S(2)}, u32[]{:S(2)}) collective-permute-start(bf16[256,128]{1,0:T(8,128)(2,1)S(1)} %get-tuple-element.48), channel_id=1, source_target_pairs={{0,24},{8,0},{16,8},{24,16},{32,56},{40,32},{48,40},{56,48},{64,88... | collective-permute-start | bytes 196616 | tf_op jit(solution)/shard_map/ppermute | solution.py:335
  150.1 5.5 %collective-permute-start.9 = (bf16[256,128]{1,0:T(8,128)(2,1)S(1)}, bf16[256,128]{1,0:T(8,128)(2,1)S(1)}, u32[]{:S(2)}, u32[]{:S(2)}) collective-permute-start(bf16[256,128]{1,0:T(8,128)(2,1)S(1)} %get-tuple-element.50), channel_id=1, source_target_pairs={{0,32},{8,40},{16,48},{24,56},{32,64},{40,72},{48,80},{56,88},{64,... | collective-permute-start | bytes 196616 | tf_op jit(solution)/shard_map/ppermute | solution.py:335
  155.6 5.8 %collective-permute-start.10 = (bf16[256,128]{1,0:T(8,128)(2,1)S(1)}, bf16[256,128]{1,0:T(8,128)(2,1)S(1)}, u32[]{:S(2)}, u32[]{:S(2)}) collective-permute-start(bf16[256,128]{1,0:T(8,128)(2,1)S(1)} %get-tuple-element.51), channel_id=1, source_target_pairs={{0,64},{8,72},{16,80},{24,88},{32,96},{40,104},{48,112},{56,120},{... | collective-permute-start | bytes 196616 | tf_op jit(solution)/shard_map/ppermute | solution.py:335
  161.4 4.3 %collective-permute-start.11 = (bf16[256,128]{1,0:T(8,128)(2,1)S(1)}, bf16[256,128]{1,0:T(8,128)(2,1)S(1)}, u32[]{:S(2)}, u32[]{:S(2)}) collective-permute-start(bf16[256,128]{1,0:T(8,128)(2,1)S(1)} %get-tuple-element.52), channel_id=1, source_target_pairs={{0,96},{8,104},{16,112},{24,120},{32,0},{40,8},{48,16},{56,24},{64... | collective-permute-start | bytes 196616 | tf_op jit(solution)/shard_map/ppermute | solution.py:335
  165.6 5.0 %collective-permute-start.34 = (bf16[256,256]{1,0:T(8,128)(2,1)S(1)}, bf16[256,256]{1,0:T(8,128)(2,1)S(1)}, u32[]{:S(2)}, u32[]{:S(2)}) collective-permute-start(bf16[256,256]{1,0:T(8,128)(2,1)S(1)} %add_second.3.refs_1_), channel_id=1, source_target_pairs={{0,2},{1,7},{2,0},{3,5},{4,6},{5,3},{6,4},{7,1},{8,10},{9,15},{10,... | collective-permute-start | bytes 393224 | tf_op jit(solution)/shard_map/ppermute | solution.py:317
  170.6 5.0 %collective-permute-start.33 = (bf16[256,256]{1,0:T(8,128)(2,1)S(1)}, bf16[256,256]{1,0:T(8,128)(2,1)S(1)}, u32[]{:S(2)}, u32[]{:S(2)}) collective-permute-start(bf16[256,256]{1,0:T(8,128)(2,1)S(1)} %add_second.2.refs_0_), channel_id=1, source_target_pairs={{0,2},{1,7},{2,0},{3,5},{4,6},{5,3},{6,4},{7,1},{8,10},{9,15},{10,... | collective-permute-start | bytes 393224 | tf_op jit(solution)/shard_map/ppermute | solution.py:317
  180.9 9.3 %collective-permute-start.35 = (bf16[256,1024]{1,0:T(8,128)(2,1)S(1)}, bf16[256,1024]{1,0:T(8,128)(2,1)S(1)}, u32[]{:S(2)}, u32[]{:S(2)}) collective-permute-start(bf16[256,1024]{1,0:T(8,128)(2,1)S(1)} %shard_map.76), channel_id=1, source_target_pairs={{0,2},{1,7},{2,0},{3,5},{4,6},{5,3},{6,4},{7,1},{8,10},{9,15},{10,... | collective-permute-start | bytes 1572872 | tf_op jit(solution)/shard_map/ppermute | solution.py:317

commit v4 on v3

--- a/solution.py
+++ b/solution.py
@@ -117,9 +117,8 @@
 
     @pl.when((turn == 0) & (part == 0))
     def _():
-        for t in range(tables):
-            for k in range(PIECES):
-                load(t, k).start()
+        for k in range(PIECES):
+            load(0, k).start()
         codes = lists_ref[:, 8 * first : 8 * (first + tables), :]
         line = iota(codes.shape, 1)
         rows = (codes & (ROWS_DEV - 1)) + (line >> 3) * ROWS_DEV
@@ -134,6 +133,9 @@
         def _(t=t):
             for k in range(PIECES):
                 load(t, k).wait()
+            if t + 1 < tables:
+                for k in range(PIECES):
+                    load(t + 1, k).start()
 
     def fetch(q, carry):
         source = source_of(part * STEP + q)

time: 191 us -> 191 us (level)
  no operation moved by 1% of the time
where the time goes in v4:
time: 191 us
  waiting for transfers between devices  113 us (59%)
  Pallas kernels  42.8 us (22%)
  starting transfers between devices  33.1 us (17%)
    ppermute x24, waiting for transfers between devices, along(): return lax.ppermute(array, 'gx', pairs)  93.3 us
    pallas_call x2, Pallas kernels, pool_tables(): pl.pallas_call(functools.partial(pool_kernel, first, each), grid=(tables,...  27.1 us
    ppermute x24, starting transfers between devices, along(): return lax.ppermute(array, 'gx', pairs)  17.9 us
    ppermute x9, waiting for transfers between devices, to_chip(): lax.ppermute(array, 'gy', [(x * 2 + c, targets[c](x) * 2 + c) for x in ra...  13.8 us
    pallas_call x2, Pallas kernels, score(): pl.pallas_call(functools.partial(score_kernel, pieces, chunks), in_specs=...  10.6 us
    all_to_all x1, starting transfers between devices, local(): lists = lax.all_to_all(lists, 'gx', 0, 0, tiled=True)  8.05 us
    ppermute x9, starting transfers between devices, to_chip(): lax.ppermute(array, 'gy', [(x * 2 + c, targets[c](x) * 2 + c) for x in ra...  7 us
    all_to_all x1, waiting for transfers between devices, local(): lists = lax.all_to_all(lists, 'gx', 0, 0, tiled=True)  5.54 us
  transfers between devices with their start and end apart: 37, of which 21 were waited for; matrix products, arithmetic and copies ran while one was open for 0% of the time, Pallas kernels for 17%

profile of v4, /device:TPU:2, one launch (start us, length us, event | category | flops | bytes accessed | tf_op | source)
XLA Modules:
  0.0 191.1 jit_solution(5916927417093753167)
XLA Ops:
  0.0 1.5 copy.10
  1.5 4.5 %dispatch.1 = s32[16,32,128]{2,1,0:T(8,128)} custom-call(s32[4,16,256]{2,1,0:T(8,128)} %bitcast.12, s32[4,16,256]{2,1,0:T(8,128)} %bitcast.13, s32[4,256]{1,0:T(4,128)} %length_ref.1), custom_call_target="tpu_custom_call" | custom-call | tf_op jit(solution)/shard_map/dispatch/pallas_call | solution.py:363
  6.0 8.0 %all-to-all-start = ((s32[16,32,128]{2,1,0:T(8,128)}), s32[16,32,128]{2,1,0:T(8,128)S(1)}, u32[]{:S(2)}, u32[]{:S(2)}) async-start(s32[16,32,128]{2,1,0:T(8,128)} %dispatch.1), calls=%async_computation | async-start | bytes 524288 | tf_op jit(solution)/shard_map/all_to_all | solution.py:368
  14.0 0.1 collective-permute-start.24
  14.1 1.5 collective-permute-start.25
  15.7 0.0 collective-permute-start.30
  15.7 0.0 collective-permute-done.24.refs_3_
  15.7 1.3 collective-permute-start.26
  17.0 5.5 %all-to-all-done.lists_ref = s32[16,32,128]{2,1,0:T(8,128)S(1)} async-done(((s32[16,32,128]{2,1,0:T(8,128)}), s32[16,32,128]{2,1,0:T(8,128)S(1)}, u32[]{:S(2)}, u32[]{:S(2)}) %all-to-all-start) | async-done | bytes 262176 | tf_op jit(solution)/shard_map/all_to_all | solution.py:368
  22.5 13.6 %shard_map.74 = (bf16[4,256,128]{2,1,0:T(8,128)(2,1)S(1)}, bf16[4,256,128]{2,1,0:T(8,128)(2,1)S(1)}, bf16[4,256,128]{2,1,0:T(8,128)(2,1)S(1)}, bf16[4,256,128]{2...) custom-call(s32[1]{0:T(128)} %bitcast.me_ref, ...), custom_call_target="tpu_custom_call" | custom-call | flops 20000000000 | bytes 6000000 | tf_op jit(solution)/shard_map/pallas_call | solution.py:195
  36.2 0.1 collective-permute-start.12
  36.2 0.1 collective-permute-start.13
  36.3 0.0 collective-permute-done.25.refs_4_
  36.4 3.1 %collective-permute-start.14 = (bf16[4,256,128]{2,1,0:T(8,128)(2,1)S(1)}, bf16[4,256,128]{2,1,0:T(8,128)(2,1)S(1)}, u32[]{:S(2)}, u32[]{:S(2)}) collective-permute-start(bf16[4,256,128]{2,1,0:T(8,128)(2,1)S(1)} %get-tuple-element.56), channel_id=1, source_target_pairs={{0,96},{8,104},{16,112},{24,120},{32,0},{40,8},{48,16},{56,24},{64... | collective-permute-start | bytes 786440 | tf_op jit(solution)/shard_map/ppermute | solution.py:337
  39.5 0.0 collective-permute-done.26.refs_5_
  39.5 0.0 collective-permute-start.15
  39.5 10.3 %collective-permute-done.12.refs_1_ = bf16[4,256,128]{2,1,0:T(8,128)(2,1)S(1)} collective-permute-done((bf16[4,256,128]{2,1,0:T(8,128)(2,1)S(1)}, bf16[4,256,128]{2,1,0:T(8,128)(2,1)S(1)}, u32[]{:S(2)}, u32[]{:S(2)}) %collective-permute-start.12) | collective-permute-done | bytes 262176 | tf_op jit(solution)/shard_map/ppermute | solution.py:337
  49.8 1.6 collective-permute-start.31
  51.4 0.1 collective-permute-start.16
  51.5 1.1 collective-permute-start.17
  52.6 0.4 collective-permute-start.32
  53.0 13.5 %shard_map.73 = (bf16[4,256,128]{2,1,0:T(8,128)(2,1)S(1)}, bf16[4,256,128]{2,1,0:T(8,128)(2,1)S(1)}, bf16[4,256,128]{2,1,0:T(8,128)(2,1)S(1)}, bf16[4,256,128]{2...) custom-call(s32[1]{0:T(128)} %bitcast.me_ref, ...), custom_call_target="tpu_custom_call" | custom-call | flops 20000000000 | bytes 6000000 | tf_op jit(solution)/shard_map/pallas_call | solution.py:195
  66.5 0.1 collective-permute-start
  66.5 1.7 collective-permute-start.1
  68.3 13.8 %collective-permute-done.refs_1_ = bf16[4,256,128]{2,1,0:T(8,128)(2,1)S(1)} collective-permute-done((bf16[4,256,128]{2,1,0:T(8,128)(2,1)S(1)}, bf16[4,256,128]{2,1,0:T(8,128)(2,1)S(1)}, u32[]{:S(2)}, u32[]{:S(2)}) %collective-permute-start) | collective-permute-done | bytes 262176 | tf_op jit(solution)/shard_map/ppermute | solution.py:337
  82.0 8.5 %collective-permute-done.2.refs_3_ = bf16[4,256,128]{2,1,0:T(8,128)(2,1)S(1)} collective-permute-done((bf16[4,256,128]{2,1,0:T(8,128)(2,1)S(1)}, bf16[4,256,128]{2,1,0:T(8,128)(2,1)S(1)}, u32[]{:S(2)}, u32[]{:S(2)}) %collective-permute-start.2) | collective-permute-done | bytes 262176 | tf_op jit(solution)/shard_map/ppermute | solution.py:337
  90.6 0.1 collective-permute-start.4
  90.7 1.4 collective-permute-done.3.refs_5_
  92.1 1.7 collective-permute-start.5
  93.9 0.3 add_first.3
  94.1 0.0 copy-start.2
  94.1 5.6 %collective-permute-done.4.refs_6_ = bf16[4,256,128]{2,1,0:T(8,128)(2,1)S(1)} collective-permute-done((bf16[4,256,128]{2,1,0:T(8,128)(2,1)S(1)}, bf16[4,256,128]{2,1,0:T(8,128)(2,1)S(1)}, u32[]{:S(2)}, u32[]{:S(2)}) %collective-permute-start.4) | collective-permute-done | bytes 262176 | tf_op jit(solution)/shard_map/ppermute | solution.py:337
  99.8 2.1 %collective-permute-start.18 = (bf16[256,128]{1,0:T(8,128)(2,1)S(1)}, bf16[256,128]{1,0:T(8,128)(2,1)S(1)}, u32[]{:S(2)}, u32[]{:S(2)}) collective-permute-start(bf16[256,128]{1,0:T(8,128)(2,1)S(1)} %get-tuple-element.62), channel_id=1, source_target_pairs={{0,8},{8,16},{16,24},{24,0},{32,40},{40,48},{48,56},{56,32},{64,72... | collective-permute-start | bytes 196616 | tf_op jit(solution)/shard_map/ppermute | solution.py:337
  101.9 3.8 %collective-permute-done.5.refs_7_ = bf16[4,256,128]{2,1,0:T(8,128)(2,1)S(1)} collective-permute-done((bf16[4,256,128]{2,1,0:T(8,128)(2,1)S(1)}, bf16[4,256,128]{2,1,0:T(8,128)(2,1)S(1)}, u32[]{:S(2)}, u32[]{:S(2)}) %collective-permute-start.5) | collective-permute-done | bytes 262176 | tf_op jit(solution)/shard_map/ppermute | solution.py:337
  105.7 2.0 %collective-permute-start.29 = (bf16[512,1024]{1,0:T(8,128)(2,1)S(1)}, bf16[512,1024]{1,0:T(8,128)(2,1)S(1)}, u32[]{:S(2)}, u32[]{:S(2)}) collective-permute-start(bf16[512,1024]{1,0:T(8,128)(2,1)S(1)} %collective-permute-done.27.refs_7_), channel_id=1, source_target_pairs={{0,6},{1,3},{2,4},{3,1},{4,2},{5,7},{6,0},{7,5},{8,14},{9,11},{10,... | collective-permute-start | bytes 3145736 | tf_op jit(solution)/shard_map/ppermute | solution.py:319
  107.8 0.9 collective-permute-start.19
  108.6 4.9 %collective-permute-done.19.refs_2_ = bf16[256,128]{1,0:T(8,128)(2,1)S(1)} collective-permute-done((bf16[256,128]{1,0:T(8,128)(2,1)S(1)}, bf16[256,128]{1,0:T(8,128)(2,1)S(1)}, u32[]{:S(2)}, u32[]{:S(2)}) %collective-permute-start.19) | collective-permute-done | bytes 65568 | tf_op jit(solution)/shard_map/ppermute | solution.py:337
  113.5 2.6 %collective-permute-start.20 = (bf16[256,128]{1,0:T(8,128)(2,1)S(1)}, bf16[256,128]{1,0:T(8,128)(2,1)S(1)}, u32[]{:S(2)}, u32[]{:S(2)}) collective-permute-start(bf16[256,128]{1,0:T(8,128)(2,1)S(1)} %get-tuple-element.64), channel_id=1, source_target_pairs={{0,24},{8,0},{16,8},{24,16},{32,56},{40,32},{48,40},{56,48},{64,88... | collective-permute-start | bytes 196616 | tf_op jit(solution)/shard_map/ppermute | solution.py:337
  116.1 1.9 collective-permute-done.20.refs_3_
  118.0 0.1 collective-permute-start.21
  118.2 6.1 %collective-permute-done.21.refs_5_ = bf16[256,128]{1,0:T(8,128)(2,1)S(1)} collective-permute-done((bf16[256,128]{1,0:T(8,128)(2,1)S(1)}, bf16[256,128]{1,0:T(8,128)(2,1)S(1)}, u32[]{:S(2)}, u32[]{:S(2)}) %collective-permute-start.21) | collective-permute-done | bytes 65568 | tf_op jit(solution)/shard_map/ppermute | solution.py:337
  124.2 5.8 %collective-permute-done.22.refs_6_ = bf16[256,128]{1,0:T(8,128)(2,1)S(1)} collective-permute-done((bf16[256,128]{1,0:T(8,128)(2,1)S(1)}, bf16[256,128]{1,0:T(8,128)(2,1)S(1)}, u32[]{:S(2)}, u32[]{:S(2)}) %collective-permute-start.22) | collective-permute-done | bytes 65568 | tf_op jit(solution)/shard_map/ppermute | solution.py:337
  130.0 0.2 collective-permute-start.23
  130.2 0.3 add_first.2
  130.5 3.8 %collective-permute-done.23.refs_7_ = bf16[256,128]{1,0:T(8,128)(2,1)S(1)} collective-permute-done((bf16[256,128]{1,0:T(8,128)(2,1)S(1)}, bf16[256,128]{1,0:T(8,128)(2,1)S(1)}, u32[]{:S(2)}, u32[]{:S(2)}) %collective-permute-start.23) | collective-permute-done | bytes 65568 | tf_op jit(solution)/shard_map/ppermute | solution.py:337
  134.3 5.8 %collective-permute-done.6.refs_1_ = bf16[256,128]{1,0:T(8,128)(2,1)S(1)} collective-permute-done((bf16[256,128]{1,0:T(8,128)(2,1)S(1)}, bf16[256,128]{1,0:T(8,128)(2,1)S(1)}, u32[]{:S(2)}, u32[]{:S(2)}) %collective-permute-start.6) | collective-permute-done | bytes 65568 | tf_op jit(solution)/shard_map/ppermute | solution.py:337
  140.1 1.1 collective-permute-start.7
  141.2 4.6 %collective-permute-done.7.refs_2_ = bf16[256,128]{1,0:T(8,128)(2,1)S(1)} collective-permute-done((bf16[256,128]{1,0:T(8,128)(2,1)S(1)}, bf16[256,128]{1,0:T(8,128)(2,1)S(1)}, u32[]{:S(2)}, u32[]{:S(2)}) %collective-permute-start.7) | collective-permute-done | bytes 65568 | tf_op jit(solution)/shard_map/ppermute | solution.py:337
  145.8 2.0 %collective-permute-start.8 = (bf16[256,128]{1,0:T(8,128)(2,1)S(1)}, bf16[256,128]{1,0:T(8,128)(2,1)S(1)}, u32[]{:S(2)}, u32[]{:S(2)}) collective-permute-start(bf16[256,128]{1,0:T(8,128)(2,1)S(1)} %get-tuple-element.48), channel_id=1, source_target_pairs={{0,24},{8,0},{16,8},{24,16},{32,56},{40,32},{48,40},{56,48},{64,88... | collective-permute-start | bytes 196616 | tf_op jit(solution)/shard_map/ppermute | solution.py:337
  147.9 2.2 %collective-permute-done.8.refs_3_ = bf16[256,128]{1,0:T(8,128)(2,1)S(1)} collective-permute-done((bf16[256,128]{1,0:T(8,128)(2,1)S(1)}, bf16[256,128]{1,0:T(8,128)(2,1)S(1)}, u32[]{:S(2)}, u32[]{:S(2)}) %collective-permute-start.8) | collective-permute-done | bytes 65568 | tf_op jit(solution)/shard_map/ppermute | solution.py:337
  150.1 5.5 %collective-permute-done.9.refs_5_ = bf16[256,128]{1,0:T(8,128)(2,1)S(1)} collective-permute-done((bf16[256,128]{1,0:T(8,128)(2,1)S(1)}, bf16[256,128]{1,0:T(8,128)(2,1)S(1)}, u32[]{:S(2)}, u32[]{:S(2)}) %collective-permute-start.9) | collective-permute-done | bytes 65568 | tf_op jit(solution)/shard_map/ppermute | solution.py:337
  155.6 5.8 %collective-permute-done.10.refs_6_ = bf16[256,128]{1,0:T(8,128)(2,1)S(1)} collective-permute-done((bf16[256,128]{1,0:T(8,128)(2,1)S(1)}, bf16[256,128]{1,0:T(8,128)(2,1)S(1)}, u32[]{:S(2)}, u32[]{:S(2)}) %collective-permute-start.10) | collective-permute-done | bytes 65568 | tf_op jit(solution)/shard_map/ppermute | solution.py:337
  161.4 0.7 collective-permute-start.11
  162.1 0.1 add_second.3.refs_1_
  162.1 3.5 %collective-permute-done.11.refs_7_ = bf16[256,128]{1,0:T(8,128)(2,1)S(1)} collective-permute-done((bf16[256,128]{1,0:T(8,128)(2,1)S(1)}, bf16[256,128]{1,0:T(8,128)(2,1)S(1)}, u32[]{:S(2)}, u32[]{:S(2)}) %collective-permute-start.11) | collective-permute-done | bytes 65568 | tf_op jit(solution)/shard_map/ppermute | solution.py:337
  165.6 0.1 add_second.2.refs_0_
  165.7 4.9 %collective-permute-done.34.refs_1_ = bf16[256,256]{1,0:T(8,128)(2,1)S(1)} collective-permute-done((bf16[256,256]{1,0:T(8,128)(2,1)S(1)}, bf16[256,256]{1,0:T(8,128)(2,1)S(1)}, u32[]{:S(2)}, u32[]{:S(2)}) %collective-permute-start.34) | collective-permute-done | bytes 131104 | tf_op jit(solution)/shard_map/ppermute | solution.py:319
  170.6 0.0 collective-permute-start.33
  170.6 5.0 %collective-permute-done.33.refs_0_ = bf16[256,256]{1,0:T(8,128)(2,1)S(1)} collective-permute-done((bf16[256,256]{1,0:T(8,128)(2,1)S(1)}, bf16[256,256]{1,0:T(8,128)(2,1)S(1)}, u32[]{:S(2)}, u32[]{:S(2)}) %collective-permute-start.33) | collective-permute-done | bytes 131104 | tf_op jit(solution)/shard_map/ppermute | solution.py:319
  175.6 5.3 %shard_map.76 = bf16[256,1024]{1,0:T(8,128)(2,1)S(1)} custom-call(bf16[256,256]{1,0:T(8,128)(2,1)S(1)} %collective-permute-done.33.refs_0_, bf16[256,256]{1,0:T(8,128)(2,1)S(1)} %collective-permute-done.34.refs_1_, f32[1,1024]{1,0:T(1,128)S(1)} %bitcast.10, f32[1,1024]{1,0:T(1,128)S(1)} %collective-permute-done.24.refs_3_, ...), custom_call_target="tpu_custom_call" | custom-call | flops 10000000000 | bytes 14000000 | tf_op jit(solution)/shard_map/pallas_call | solution.py:300
  180.9 0.1 collective-permute-start.35
  181.0 5.3 %shard_map.75 = f32[256,1024]{1,0:T(8,128)S(1)} custom-call(bf16[256,256]{1,0:T(8,128)(2,1)S(1)} %add_second.2.refs_0_, bf16[256,256]{1,0:T(8,128)(2,1)S(1)} %add_second.3.refs_1_, f32[1,1024]{1,0:T(1,128)S(1)} %bitcast.11, f32[1,1024]{1,0:T(1,128)S(1)} %collective-permute-done.24.refs_3_, f32[1,1024]{1,0:T(1,128)S(1)} %collective-permute-done.25.refs_4_, ...), custom_call_target="tpu_custom_call" | custom-call | flops 10000000000 | bytes 14000000 | tf_op jit(solution)/shard_map/pallas_call | solution.py:300
  186.3 3.9 %collective-permute-done.35 = bf16[256,1024]{1,0:T(8,128)(2,1)S(1)} collective-permute-done((bf16[256,1024]{1,0:T(8,128)(2,1)S(1)}, bf16[256,1024]{1,0:T(8,128)(2,1)S(1)}, u32[]{:S(2)}, u32[]{:S(2)}) %collective-permute-start.35) | collective-permute-done | bytes 524320 | tf_op jit(solution)/shard_map/ppermute | solution.py:319
  190.1 0.9 add_convert_fusion
  (27 shorter events, 0.1 us)
Async XLA Ops:
  6.0 16.6 %all-to-all-start = ((s32[16,32,128]{2,1,0:T(8,128)}), s32[16,32,128]{2,1,0:T(8,128)S(1)}, u32[]{:S(2)}, u32[]{:S(2)}) async-start(s32[16,32,128]{2,1,0:T(8,128)} %dispatch.1), calls=%async_computation | async-start | bytes 524288 | tf_op jit(solution)/shard_map/all_to_all | solution.py:368
  14.0 1.6 collective-permute-start.24
  14.1 22.2 %collective-permute-start.25 = (f32[1,1024]{1,0:T(1,128)}, f32[1,1024]{1,0:T(1,128)S(1)}, u32[]{:S(2)}, u32[]{:S(2)}) collective-permute-start(f32[1,1024]{1,0:T(1,128)} %bitcast.9), channel_id=1, source_target_pairs={{0,6},{1,3},{2,4},{3,1},{4,2},{5,7},{6,0},{7,5},{8,14},{9,11},{10,... | collective-permute-start | bytes 12296 | tf_op jit(solution)/shard_map/ppermute | solution.py:319
  15.7 36.9 %collective-permute-start.30 = (bf16[1024,1024]{1,0:T(8,128)(2,1)}, bf16[1024,1024]{1,0:T(8,128)(2,1)S(1)}, u32[]{:S(2)}, u32[]{:S(2)}) collective-permute-start(bf16[1024,1024]{1,0:T(8,128)(2,1)} %refs_10_.3), channel_id=1, source_target_pairs={{0,1},{1,0},{2,3},{3,2},{4,5},{5,4},{6,7},{7,6},{8,9},{9,8},{10,11... | collective-permute-start | bytes 6291464 | tf_op jit(solution)/shard_map/ppermute | solution.py:349
  15.7 23.8 %collective-permute-start.26 = (f32[1,1024]{1,0:T(1,128)S(1)}, f32[1,1024]{1,0:T(1,128)S(1)}, u32[]{:S(2)}, u32[]{:S(2)}) collective-permute-start(f32[1,1024]{1,0:T(1,128)S(1)} %collective-permute-done.24.refs_3_), channel_id=1, source_target_pairs={{0,6},{1,3},{2,4},{3,1},{4,2},{5,7},{6,0},{7,5},{8,14},{9,11},{10,... | collective-permute-start | bytes 12296 | tf_op jit(solution)/shard_map/ppermute | solution.py:319
  22.5 27.2 %copy-start = (bf16[1024,1024]{1,0:T(8,128)(2,1)S(1)}, bf16[1024,1024]{1,0:T(8,128)(2,1)}, u32[]{:S(2)}) copy-start(bf16[1024,1024]{1,0:T(8,128)(2,1)} %refs_10_.3) | copy-start | bytes 6291460
  22.5 28.8 %copy-start.1 = (bf16[512,1024]{1,0:T(8,128)(2,1)S(1)}, bf16[512,1024]{1,0:T(8,128)(2,1)}, u32[]{:S(2)}) copy-start(bf16[512,1024]{1,0:T(8,128)(2,1)} %refs_6_.3) | copy-start | bytes 3145732
  36.2 13.6 %collective-permute-start.12 = (bf16[4,256,128]{2,1,0:T(8,128)(2,1)S(1)}, bf16[4,256,128]{2,1,0:T(8,128)(2,1)S(1)}, u32[]{:S(2)}, u32[]{:S(2)}) collective-permute-start(bf16[4,256,128]{2,1,0:T(8,128)(2,1)S(1)} %get-tuple-element.54), channel_id=1, source_target_pairs={{0,32},{8,40},{16,48},{24,56},{32,64},{40,72},{48,80},{56,88},{64,... | collective-permute-start | bytes 786440 | tf_op jit(solution)/shard_map/ppermute | solution.py:337
  36.2 15.1 %collective-permute-start.13 = (bf16[4,256,128]{2,1,0:T(8,128)(2,1)S(1)}, bf16[4,256,128]{2,1,0:T(8,128)(2,1)S(1)}, u32[]{:S(2)}, u32[]{:S(2)}) collective-permute-start(bf16[4,256,128]{2,1,0:T(8,128)(2,1)S(1)} %get-tuple-element.55), channel_id=1, source_target_pairs={{0,64},{8,72},{16,80},{24,88},{32,96},{40,104},{48,112},{56,120},{... | collective-permute-start | bytes 786440 | tf_op jit(solution)/shard_map/ppermute | solution.py:337
  36.4 15.0 %collective-permute-start.14 = (bf16[4,256,128]{2,1,0:T(8,128)(2,1)S(1)}, bf16[4,256,128]{2,1,0:T(8,128)(2,1)S(1)}, u32[]{:S(2)}, u32[]{:S(2)}) collective-permute-start(bf16[4,256,128]{2,1,0:T(8,128)(2,1)S(1)} %get-tuple-element.56), channel_id=1, source_target_pairs={{0,96},{8,104},{16,112},{24,120},{32,0},{40,8},{48,16},{56,24},{64... | collective-permute-start | bytes 786440 | tf_op jit(solution)/shard_map/ppermute | solution.py:337
  39.5 12.0 %collective-permute-start.15 = (bf16[4,256,128]{2,1,0:T(8,128)(2,1)S(1)}, bf16[4,256,128]{2,1,0:T(8,128)(2,1)S(1)}, u32[]{:S(2)}, u32[]{:S(2)}) collective-permute-start(bf16[4,256,128]{2,1,0:T(8,128)(2,1)S(1)} %get-tuple-element.58), channel_id=1, source_target_pairs={{0,8},{8,16},{16,24},{24,0},{32,40},{40,48},{48,56},{56,32},{64,72... | collective-permute-start | bytes 786440 | tf_op jit(solution)/shard_map/ppermute | solution.py:337
  49.8 125.8 %collective-permute-start.31 = (bf16[1024,1024]{1,0:T(8,128)(2,1)S(1)}, bf16[1024,1024]{1,0:T(8,128)(2,1)S(1)}, u32[]{:S(2)}, u32[]{:S(2)}) collective-permute-start(bf16[1024,1024]{1,0:T(8,128)(2,1)S(1)} %copy-done), channel_id=1, source_target_pairs={{0,6},{1,3},{2,4},{3,1},{4,2},{5,7},{6,0},{7,5},{8,14},{9,11},{10,... | collective-permute-start | bytes 6291464 | tf_op jit(solution)/shard_map/ppermute | solution.py:319
  51.4 54.4 %collective-permute-start.27 = (bf16[512,1024]{1,0:T(8,128)(2,1)S(1)}, bf16[512,1024]{1,0:T(8,128)(2,1)S(1)}, u32[]{:S(2)}, u32[]{:S(2)}) collective-permute-start(bf16[512,1024]{1,0:T(8,128)(2,1)S(1)} %copy-done.1), channel_id=1, source_target_pairs={{0,1},{1,0},{2,3},{3,2},{4,5},{5,4},{6,7},{7,6},{8,9},{9,8},{10,11... | collective-permute-start | bytes 3145736 | tf_op jit(solution)/shard_map/ppermute | solution.py:349
  51.4 15.1 %collective-permute-start.16 = (bf16[4,256,128]{2,1,0:T(8,128)(2,1)S(1)}, bf16[4,256,128]{2,1,0:T(8,128)(2,1)S(1)}, u32[]{:S(2)}, u32[]{:S(2)}) collective-permute-start(bf16[4,256,128]{2,1,0:T(8,128)(2,1)S(1)} %get-tuple-element.59), channel_id=1, source_target_pairs={{0,16},{8,24},{16,0},{24,8},{32,48},{40,56},{48,32},{56,40},{64,80... | collective-permute-start | bytes 786440 | tf_op jit(solution)/shard_map/ppermute | solution.py:337
  51.5 15.1 %collective-permute-start.17 = (bf16[4,256,128]{2,1,0:T(8,128)(2,1)S(1)}, bf16[4,256,128]{2,1,0:T(8,128)(2,1)S(1)}, u32[]{:S(2)}, u32[]{:S(2)}) collective-permute-start(bf16[4,256,128]{2,1,0:T(8,128)(2,1)S(1)} %get-tuple-element.60), channel_id=1, source_target_pairs={{0,24},{8,0},{16,8},{24,16},{32,56},{40,32},{48,40},{56,48},{64,88... | collective-permute-start | bytes 786440 | tf_op jit(solution)/shard_map/ppermute | solution.py:337
  52.6 123.0 %collective-permute-start.32 = (bf16[1024,1024]{1,0:T(8,128)(2,1)S(1)}, bf16[1024,1024]{1,0:T(8,128)(2,1)S(1)}, u32[]{:S(2)}, u32[]{:S(2)}) collective-permute-start(bf16[1024,1024]{1,0:T(8,128)(2,1)S(1)} %collective-permute-done.30.refs_11_), channel_id=1, source_target_pairs={{0,6},{1,3},{2,4},{3,1},{4,2},{5,7},{6,0},{7,5},{8,14},{9,11},{10,... | collective-permute-start | bytes 6291464 | tf_op jit(solution)/shard_map/ppermute | solution.py:319
  66.5 15.5 %collective-permute-start = (bf16[4,256,128]{2,1,0:T(8,128)(2,1)S(1)}, bf16[4,256,128]{2,1,0:T(8,128)(2,1)S(1)}, u32[]{:S(2)}, u32[]{:S(2)}) collective-permute-start(bf16[4,256,128]{2,1,0:T(8,128)(2,1)S(1)} %get-tuple-element.38), channel_id=1, source_target_pairs={{0,32},{8,40},{16,48},{24,56},{32,64},{40,72},{48,80},{56,88},{64,... | collective-permute-start | bytes 786440 | tf_op jit(solution)/shard_map/ppermute | solution.py:337
  66.5 15.5 %collective-permute-start.1 = (bf16[4,256,128]{2,1,0:T(8,128)(2,1)S(1)}, bf16[4,256,128]{2,1,0:T(8,128)(2,1)S(1)}, u32[]{:S(2)}, u32[]{:S(2)}) collective-permute-start(bf16[4,256,128]{2,1,0:T(8,128)(2,1)S(1)} %get-tuple-element.39), channel_id=1, source_target_pairs={{0,64},{8,72},{16,80},{24,88},{32,96},{40,104},{48,112},{56,120},{... | collective-permute-start | bytes 786440 | tf_op jit(solution)/shard_map/ppermute | solution.py:337
  82.0 8.6 %collective-permute-start.2 = (bf16[4,256,128]{2,1,0:T(8,128)(2,1)S(1)}, bf16[4,256,128]{2,1,0:T(8,128)(2,1)S(1)}, u32[]{:S(2)}, u32[]{:S(2)}) collective-permute-start(bf16[4,256,128]{2,1,0:T(8,128)(2,1)S(1)} %get-tuple-element.40), channel_id=1, source_target_pairs={{0,96},{8,104},{16,112},{24,120},{32,0},{40,8},{48,16},{56,24},{64... | collective-permute-start | bytes 786440 | tf_op jit(solution)/shard_map/ppermute | solution.py:337
  82.0 10.1 %collective-permute-start.3 = (bf16[4,256,128]{2,1,0:T(8,128)(2,1)S(1)}, bf16[4,256,128]{2,1,0:T(8,128)(2,1)S(1)}, u32[]{:S(2)}, u32[]{:S(2)}) collective-permute-start(bf16[4,256,128]{2,1,0:T(8,128)(2,1)S(1)} %get-tuple-element.42), channel_id=1, source_target_pairs={{0,8},{8,16},{16,24},{24,0},{32,40},{40,48},{48,56},{56,32},{64,72... | collective-permute-start | bytes 786440 | tf_op jit(solution)/shard_map/ppermute | solution.py:337
  90.6 9.2 %collective-permute-start.4 = (bf16[4,256,128]{2,1,0:T(8,128)(2,1)S(1)}, bf16[4,256,128]{2,1,0:T(8,128)(2,1)S(1)}, u32[]{:S(2)}, u32[]{:S(2)}) collective-permute-start(bf16[4,256,128]{2,1,0:T(8,128)(2,1)S(1)} %get-tuple-element.43), channel_id=1, source_target_pairs={{0,16},{8,24},{16,0},{24,8},{32,48},{40,56},{48,32},{56,40},{64,80... | collective-permute-start | bytes 786440 | tf_op jit(solution)/shard_map/ppermute | solution.py:337
  92.1 13.6 %collective-permute-start.5 = (bf16[4,256,128]{2,1,0:T(8,128)(2,1)S(1)}, bf16[4,256,128]{2,1,0:T(8,128)(2,1)S(1)}, u32[]{:S(2)}, u32[]{:S(2)}) collective-permute-start(bf16[4,256,128]{2,1,0:T(8,128)(2,1)S(1)} %get-tuple-element.44), channel_id=1, source_target_pairs={{0,24},{8,0},{16,8},{24,16},{32,56},{40,32},{48,40},{56,48},{64,88... | collective-permute-start | bytes 786440 | tf_op jit(solution)/shard_map/ppermute | solution.py:337
  94.1 81.5 %copy-start.2 = (f32[1024]{0:T(1024)S(1)}, f32[1024]{0:T(1024)}, u32[]{:S(2)}) copy-start(f32[1024]{0:T(1024)} %param.12) | copy-start | bytes 12292
  99.8 8.0 %collective-permute-start.18 = (bf16[256,128]{1,0:T(8,128)(2,1)S(1)}, bf16[256,128]{1,0:T(8,128)(2,1)S(1)}, u32[]{:S(2)}, u32[]{:S(2)}) collective-permute-start(bf16[256,128]{1,0:T(8,128)(2,1)S(1)} %get-tuple-element.62), channel_id=1, source_target_pairs={{0,8},{8,16},{16,24},{24,0},{32,40},{40,48},{48,56},{56,32},{64,72... | collective-permute-start | bytes 196616 | tf_op jit(solution)/shard_map/ppermute | solution.py:337
  105.7 69.8 %collective-permute-start.28 = (bf16[512,1024]{1,0:T(8,128)(2,1)S(1)}, bf16[512,1024]{1,0:T(8,128)(2,1)S(1)}, u32[]{:S(2)}, u32[]{:S(2)}) collective-permute-start(bf16[512,1024]{1,0:T(8,128)(2,1)S(1)} %copy-done.1), channel_id=1, source_target_pairs={{0,6},{1,3},{2,4},{3,1},{4,2},{5,7},{6,0},{7,5},{8,14},{9,11},{10,... | collective-permute-start | bytes 3145736 | tf_op jit(solution)/shard_map/ppermute | solution.py:319
  105.7 69.8 %collective-permute-start.29 = (bf16[512,1024]{1,0:T(8,128)(2,1)S(1)}, bf16[512,1024]{1,0:T(8,128)(2,1)S(1)}, u32[]{:S(2)}, u32[]{:S(2)}) collective-permute-start(bf16[512,1024]{1,0:T(8,128)(2,1)S(1)} %collective-permute-done.27.refs_7_), channel_id=1, source_target_pairs={{0,6},{1,3},{2,4},{3,1},{4,2},{5,7},{6,0},{7,5},{8,14},{9,11},{10,... | collective-permute-start | bytes 3145736 | tf_op jit(solution)/shard_map/ppermute | solution.py:319
  107.8 5.8 %collective-permute-start.19 = (bf16[256,128]{1,0:T(8,128)(2,1)S(1)}, bf16[256,128]{1,0:T(8,128)(2,1)S(1)}, u32[]{:S(2)}, u32[]{:S(2)}) collective-permute-start(bf16[256,128]{1,0:T(8,128)(2,1)S(1)} %get-tuple-element.63), channel_id=1, source_target_pairs={{0,16},{8,24},{16,0},{24,8},{32,48},{40,56},{48,32},{56,40},{64,80... | collective-permute-start | bytes 196616 | tf_op jit(solution)/shard_map/ppermute | solution.py:337
  113.5 4.5 %collective-permute-start.20 = (bf16[256,128]{1,0:T(8,128)(2,1)S(1)}, bf16[256,128]{1,0:T(8,128)(2,1)S(1)}, u32[]{:S(2)}, u32[]{:S(2)}) collective-permute-start(bf16[256,128]{1,0:T(8,128)(2,1)S(1)} %get-tuple-element.64), channel_id=1, source_target_pairs={{0,24},{8,0},{16,8},{24,16},{32,56},{40,32},{48,40},{56,48},{64,88... | collective-permute-start | bytes 196616 | tf_op jit(solution)/shard_map/ppermute | solution.py:337
  118.0 6.2 %collective-permute-start.21 = (bf16[256,128]{1,0:T(8,128)(2,1)S(1)}, bf16[256,128]{1,0:T(8,128)(2,1)S(1)}, u32[]{:S(2)}, u32[]{:S(2)}) collective-permute-start(bf16[256,128]{1,0:T(8,128)(2,1)S(1)} %get-tuple-element.66), channel_id=1, source_target_pairs={{0,32},{8,40},{16,48},{24,56},{32,64},{40,72},{48,80},{56,88},{64,... | collective-permute-start | bytes 196616 | tf_op jit(solution)/shard_map/ppermute | solution.py:337
  124.2 5.8 %collective-permute-start.22 = (bf16[256,128]{1,0:T(8,128)(2,1)S(1)}, bf16[256,128]{1,0:T(8,128)(2,1)S(1)}, u32[]{:S(2)}, u32[]{:S(2)}) collective-permute-start(bf16[256,128]{1,0:T(8,128)(2,1)S(1)} %get-tuple-element.67), channel_id=1, source_target_pairs={{0,64},{8,72},{16,80},{24,88},{32,96},{40,104},{48,112},{56,120},{... | collective-permute-start | bytes 196616 | tf_op jit(solution)/shard_map/ppermute | solution.py:337
  130.0 4.3 %collective-permute-start.23 = (bf16[256,128]{1,0:T(8,128)(2,1)S(1)}, bf16[256,128]{1,0:T(8,128)(2,1)S(1)}, u32[]{:S(2)}, u32[]{:S(2)}) collective-permute-start(bf16[256,128]{1,0:T(8,128)(2,1)S(1)} %get-tuple-element.68), channel_id=1, source_target_pairs={{0,96},{8,104},{16,112},{24,120},{32,0},{40,8},{48,16},{56,24},{64... | collective-permute-start | bytes 196616 | tf_op jit(solution)/shard_map/ppermute | solution.py:337
  134.3 5.8 %collective-permute-start.6 = (bf16[256,128]{1,0:T(8,128)(2,1)S(1)}, bf16[256,128]{1,0:T(8,128)(2,1)S(1)}, u32[]{:S(2)}, u32[]{:S(2)}) collective-permute-start(bf16[256,128]{1,0:T(8,128)(2,1)S(1)} %get-tuple-element.46), channel_id=1, source_target_pairs={{0,8},{8,16},{16,24},{24,0},{32,40},{40,48},{48,56},{56,32},{64,72... | collective-permute-start | bytes 196616 | tf_op jit(solution)/shard_map/ppermute | solution.py:337
  140.1 5.8 %collective-permute-start.7 = (bf16[256,128]{1,0:T(8,128)(2,1)S(1)}, bf16[256,128]{1,0:T(8,128)(2,1)S(1)}, u32[]{:S(2)}, u32[]{:S(2)}) collective-permute-start(bf16[256,128]{1,0:T(8,128)(2,1)S(1)} %get-tuple-element.47), channel_id=1, source_target_pairs={{0,16},{8,24},{16,0},{24,8},{32,48},{40,56},{48,32},{56,40},{64,80... | collective-permute-start | bytes 196616 | tf_op jit(solution)/shard_map/ppermute | solution.py:337
  145.8 4.3 %collective-permute-start.8 = (bf16[256,128]{1,0:T(8,128)(2,1)S(1)}, bf16[256,128]{1,0:T(8,128)(2,1)S(1)}, u32[]{:S(2)}, u32[]{:S(2)}) collective-permute-start(bf16[256,128]{1,0:T(8,128)(2,1)S(1)} %get-tuple-element.48), channel_id=1, source_target_pairs={{0,24},{8,0},{16,8},{24,16},{32,56},{40,32},{48,40},{56,48},{64,88... | collective-permute-start | bytes 196616 | tf_op jit(solution)/shard_map/ppermute | solution.py:337
  150.1 5.5 %collective-permute-start.9 = (bf16[256,128]{1,0:T(8,128)(2,1)S(1)}, bf16[256,128]{1,0:T(8,128)(2,1)S(1)}, u32[]{:S(2)}, u32[]{:S(2)}) collective-permute-start(bf16[256,128]{1,0:T(8,128)(2,1)S(1)} %get-tuple-element.50), channel_id=1, source_target_pairs={{0,32},{8,40},{16,48},{24,56},{32,64},{40,72},{48,80},{56,88},{64,... | collective-permute-start | bytes 196616 | tf_op jit(solution)/shard_map/ppermute | solution.py:337
  155.6 5.8 %collective-permute-start.10 = (bf16[256,128]{1,0:T(8,128)(2,1)S(1)}, bf16[256,128]{1,0:T(8,128)(2,1)S(1)}, u32[]{:S(2)}, u32[]{:S(2)}) collective-permute-start(bf16[256,128]{1,0:T(8,128)(2,1)S(1)} %get-tuple-element.51), channel_id=1, source_target_pairs={{0,64},{8,72},{16,80},{24,88},{32,96},{40,104},{48,112},{56,120},{... | collective-permute-start | bytes 196616 | tf_op jit(solution)/shard_map/ppermute | solution.py:337
  161.4 4.3 %collective-permute-start.11 = (bf16[256,128]{1,0:T(8,128)(2,1)S(1)}, bf16[256,128]{1,0:T(8,128)(2,1)S(1)}, u32[]{:S(2)}, u32[]{:S(2)}) collective-permute-start(bf16[256,128]{1,0:T(8,128)(2,1)S(1)} %get-tuple-element.52), channel_id=1, source_target_pairs={{0,96},{8,104},{16,112},{24,120},{32,0},{40,8},{48,16},{56,24},{64... | collective-permute-start | bytes 196616 | tf_op jit(solution)/shard_map/ppermute | solution.py:337
  165.6 5.0 %collective-permute-start.34 = (bf16[256,256]{1,0:T(8,128)(2,1)S(1)}, bf16[256,256]{1,0:T(8,128)(2,1)S(1)}, u32[]{:S(2)}, u32[]{:S(2)}) collective-permute-start(bf16[256,256]{1,0:T(8,128)(2,1)S(1)} %add_second.3.refs_1_), channel_id=1, source_target_pairs={{0,2},{1,7},{2,0},{3,5},{4,6},{5,3},{6,4},{7,1},{8,10},{9,15},{10,... | collective-permute-start | bytes 393224 | tf_op jit(solution)/shard_map/ppermute | solution.py:319
  170.6 5.0 %collective-permute-start.33 = (bf16[256,256]{1,0:T(8,128)(2,1)S(1)}, bf16[256,256]{1,0:T(8,128)(2,1)S(1)}, u32[]{:S(2)}, u32[]{:S(2)}) collective-permute-start(bf16[256,256]{1,0:T(8,128)(2,1)S(1)} %add_second.2.refs_0_), channel_id=1, source_target_pairs={{0,2},{1,7},{2,0},{3,5},{4,6},{5,3},{6,4},{7,1},{8,10},{9,15},{10,... | collective-permute-start | bytes 393224 | tf_op jit(solution)/shard_map/ppermute | solution.py:319
  180.9 9.3 %collective-permute-start.35 = (bf16[256,1024]{1,0:T(8,128)(2,1)S(1)}, bf16[256,1024]{1,0:T(8,128)(2,1)S(1)}, u32[]{:S(2)}, u32[]{:S(2)}) collective-permute-start(bf16[256,1024]{1,0:T(8,128)(2,1)S(1)} %shard_map.76), channel_id=1, source_target_pairs={{0,2},{1,7},{2,0},{3,5},{4,6},{5,3},{6,4},{7,1},{8,10},{9,15},{10,... | collective-permute-start | bytes 1572872 | tf_op jit(solution)/shard_map/ppermute | solution.py:319

commit v5 on v4

--- a/solution.py
+++ b/solution.py
@@ -19,7 +19,6 @@
 PIECES = 4
 STEP = 8
 BAG_SHIFT = 13
-EACH = 1
 
 
 def iota(shape, dim):
@@ -43,7 +42,7 @@
     zero, one = jnp.bfloat16(0), jnp.bfloat16(1)
     for t in range(TABLES):
         live = iota((BAG, SAMPLES), 0) < length_ref[t : t + 1, :]
-        own = jnp.where(live, own_ref[t], OWNERS)
+        own = jnp.where(live, own_ref[t, :, 0, :], OWNERS)
         mark = (own[:, None, :] == owner_iota).reshape(256, 256)
         onehot = ones_where(mark)
         rank = jnp.dot(onehot, before, preferred_element_type=jnp.float32)
@@ -216,35 +215,41 @@
 
 
 def add_first_kernel(*refs):
-    ins, outs = refs[:8], refs[8:]
+    chunks = len(refs) // 8 - 1
+    outs = refs[8 * chunks :]
     for half in range(2):
         for k in range(4):
-            total = ins[4 * half][k].astype(jnp.float32)
-            for d in range(1, 4):
-                total += ins[4 * half + d][k].astype(jnp.float32)
-            outs[4 * half + k][...] = total.astype(jnp.bfloat16)
+            for c in range(chunks):
+                ins = refs[8 * c + 4 * half : 8 * c + 4 * half + 4]
+                total = ins[0][k].astype(jnp.float32)
+                for d in range(1, 4):
+                    total += ins[d][k].astype(jnp.float32)
+                outs[4 * half + k][:, c * EMB : (c + 1) * EMB] = total.astype(jnp.bfloat16)
 
 
 def add_first(parts):
     vmem = pl.BlockSpec(memory_space=pltpu.VMEM)
+    width = len(parts) // 8 * EMB
     return pl.pallas_call(
         add_first_kernel,
-        in_specs=[vmem] * 8,
+        in_specs=[vmem] * len(parts),
         out_specs=[vmem] * 8,
-        out_shape=[jax.ShapeDtypeStruct(parts[0].shape[1:], jnp.bfloat16)] * 8,
-        compiler_params=pltpu.CompilerParams(vmem_limit_bytes=16 << 20),
+        out_shape=[jax.ShapeDtypeStruct((SAMPLES, width), jnp.bfloat16)] * 8,
+        compiler_params=pltpu.CompilerParams(vmem_limit_bytes=20 << 20),
         name="add_first",
     )(*parts)
 
 
 def add_second_kernel(*refs):
     ins, out_ref = refs[:8], refs[8]
-    width = ins[0].shape[1]
     for half in range(2):
         total = ins[4 * half][...].astype(jnp.float32)
         for d in range(1, 4):
             total += ins[4 * half + d][...].astype(jnp.float32)
-        out_ref[:, half * width : (half + 1) * width] = total.astype(jnp.bfloat16)
+        total = total.astype(jnp.bfloat16)
+        for c in range(total.shape[1] // EMB):
+            table = 2 * c + half
+            out_ref[:, table * EMB : (table + 1) * EMB] = total[:, c * EMB : (c + 1) * EMB]
 
 
 def add_second(parts):
@@ -358,7 +363,7 @@
         far_near.append(to_chip(near[k], (mirror, flip)))
     biases, w_in, w_out = zip(own, near, far, far_near)
 
-    owner = jnp.transpose(lookup_owner[..., 0], (0, 2, 1))
+    owner = jnp.transpose(lookup_owner, (0, 2, 3, 1))
     row = jnp.transpose(lookup_row, (0, 2, 1))
     lists = pl.pallas_call(
         dispatch_kernel,
@@ -368,17 +373,15 @@
     lists = lax.all_to_all(lists, "gx", 0, 0, tiled=True)
 
     me = lax.axis_index("gx").astype(jnp.int32).reshape(1)
-    mine, theirs = [], []
-    for first in range(0, TABLES, 2 * EACH):
-        parts = pool_tables(first, EACH, me, lists, table)
-        parts = moved(parts, "yz")
-        parts = add_first(parts)
-        parts = moved(parts, "zy")
-        chunk = add_second(parts)
-        mine.append(chunk)
-        theirs.append(to_chip(chunk, (flip, mirror)))
-    kept = score(mine, biases, w_in, w_out, jnp.float32)
-    sent = score(theirs, biases, w_in, w_out, jnp.bfloat16)
+    parts = []
+    for first in range(0, TABLES, 2):
+        shares = pool_tables(first, 1, me, lists, table)
+        parts += moved(shares, "yz")
+    parts = moved(add_first(parts), "zy")
+    mine = add_second(parts)
+    theirs = to_chip(mine, (flip, mirror))
+    kept = score([mine], biases, w_in, w_out, jnp.float32)
+    sent = score([theirs], biases, w_in, w_out, jnp.bfloat16)
     received = to_chip(sent, (flip, mirror))
     return (kept + received.astype(jnp.float32)).astype(jnp.bfloat16)
 

time: 191 us -> 167 us (0.87)
  waiting for transfers between devices: 113 us -> 98.2 us
  starting transfers between devices: 33.1 us -> 24.7 us
    ppermute x24 -> x18, waiting for transfers between devices: 93.3 us -> 74.9 us  [along(): return lax.ppermute(array, 'gx', pairs)]
    ppermute x24 -> x18, starting transfers between devices: 17.9 us -> 12.4 us  [along(): return lax.ppermute(array, 'gx', pairs)]
    all_to_all x1, waiting for transfers between devices: 5.54 us -> 8.41 us  [local(): lists = lax.all_to_all(lists, 'gx', 0, 0, tiled=True)]
    ppermute x9 -> x8, starting transfers between devices: 7 us -> 4.18 us  [to_chip(): lax.ppermute(array, 'gy', [(x * 2 + c, targets[c](x) * 2 + c) for x in ra...]
    ppermute x9 -> x8, waiting for transfers between devices: 13.8 us -> 13.7 us  [to_chip(): lax.ppermute(array, 'gy', [(x * 2 + c, targets[c](x) * 2 + c) for x in ra...]
  transfers between devices with their start and end apart: 37 -> 30, of which waited for: 21 -> 17; matrix products, arithmetic and copies ran while one was open for 0% -> 0% of each run, Pallas kernels for 17% -> 20%
where the time goes in v5:
time: 167 us
  waiting for transfers between devices  98.2 us (59%)
  Pallas kernels  42.8 us (26%)
  starting transfers between devices  24.7 us (15%)
    ppermute x18, waiting for transfers between devices, along(): return lax.ppermute(array, 'gx', pairs)  74.9 us
    pallas_call x2, Pallas kernels, pool_tables(): pl.pallas_call(functools.partial(pool_kernel, first, each), grid=(tables,...  27.1 us
    ppermute x8, waiting for transfers between devices, to_chip(): lax.ppermute(array, 'gy', [(x * 2 + c, targets[c](x) * 2 + c) for x in ra...  13.7 us
    ppermute x18, starting transfers between devices, along(): return lax.ppermute(array, 'gx', pairs)  12.4 us
    pallas_call x2, Pallas kernels, score(): pl.pallas_call(functools.partial(score_kernel, pieces, chunks), in_specs=...  10.5 us
    all_to_all x1, waiting for transfers between devices, local(): lists = lax.all_to_all(lists, 'gx', 0, 0, tiled=True)  8.41 us
    all_to_all x1, starting transfers between devices, local(): lists = lax.all_to_all(lists, 'gx', 0, 0, tiled=True)  8.05 us
    pallas_call x1, Pallas kernels, local(): pl.pallas_call(dispatch_kernel, out_shape=jax.ShapeDtypeStruct((OWNERS, 8...  4.52 us
  transfers between devices with their start and end apart: 30, of which 17 were waited for; matrix products, arithmetic and copies ran while one was open for 0% of the time, Pallas kernels for 20%

profile of v5, /device:TPU:2, one launch (start us, length us, event | category | flops | bytes accessed | tf_op | source)
XLA Modules:
  0.0 166.9 jit_solution(13199811880618150355)
XLA Ops:
  0.0 4.5 %dispatch.1 = s32[16,32,128]{2,1,0:T(8,128)} custom-call(s32[4,16,1,256]{3,2,1,0:T(1,128)} %bitcast.8, s32[4,16,256]{2,1,0:T(8,128)} %bitcast.9, s32[4,256]{1,0:T(4,128)} %length_ref.1), custom_call_target="tpu_custom_call" | custom-call | tf_op jit(solution)/shard_map/dispatch/pallas_call | solution.py:368
  4.5 8.0 %all-to-all-start = ((s32[16,32,128]{2,1,0:T(8,128)}), s32[16,32,128]{2,1,0:T(8,128)S(1)}, u32[]{:S(2)}, u32[]{:S(2)}) async-start(s32[16,32,128]{2,1,0:T(8,128)} %dispatch.1), calls=%async_computation | async-start | bytes 524288 | tf_op jit(solution)/shard_map/all_to_all | solution.py:373
  12.6 0.1 collective-permute-start.24
  12.7 8.4 %all-to-all-done.lists_ref = s32[16,32,128]{2,1,0:T(8,128)S(1)} async-done(((s32[16,32,128]{2,1,0:T(8,128)}), s32[16,32,128]{2,1,0:T(8,128)S(1)}, u32[]{:S(2)}, u32[]{:S(2)}) %all-to-all-start) | async-done | bytes 262176 | tf_op jit(solution)/shard_map/all_to_all | solution.py:373
  21.1 13.6 %shard_map.74 = (bf16[4,256,128]{2,1,0:T(8,128)(2,1)S(1)}, bf16[4,256,128]{2,1,0:T(8,128)(2,1)S(1)}, bf16[4,256,128]{2,1,0:T(8,128)(2,1)S(1)}, bf16[4,256,128]{2...) custom-call(s32[1]{0:T(128)} %bitcast.me_ref, ...), custom_call_target="tpu_custom_call" | custom-call | flops 20000000000 | bytes 6000000 | tf_op jit(solution)/shard_map/pallas_call | solution.py:194
  34.7 0.1 collective-permute-start.6
  34.8 0.1 collective-permute-start.7
  34.9 3.1 %collective-permute-start.8 = (bf16[4,256,128]{2,1,0:T(8,128)(2,1)S(1)}, bf16[4,256,128]{2,1,0:T(8,128)(2,1)S(1)}, u32[]{:S(2)}, u32[]{:S(2)}) collective-permute-start(bf16[4,256,128]{2,1,0:T(8,128)(2,1)S(1)} %get-tuple-element.40), channel_id=1, source_target_pairs={{0,96},{8,104},{16,112},{24,120},{32,0},{40,8},{48,16},{56,24},{64... | collective-permute-start | bytes 786440 | tf_op jit(solution)/shard_map/ppermute | solution.py:342
  38.0 0.0 collective-permute-start.9
  38.0 10.3 %collective-permute-done.6.refs_9_ = bf16[4,256,128]{2,1,0:T(8,128)(2,1)S(1)} collective-permute-done((bf16[4,256,128]{2,1,0:T(8,128)(2,1)S(1)}, bf16[4,256,128]{2,1,0:T(8,128)(2,1)S(1)}, u32[]{:S(2)}, u32[]{:S(2)}) %collective-permute-start.6) | collective-permute-done | bytes 262176 | tf_op jit(solution)/shard_map/ppermute | solution.py:342
  48.4 1.6 collective-permute-start.25
  49.9 0.0 collective-permute-done.7.refs_10_
  49.9 0.0 collective-permute-start.21
  49.9 0.0 collective-permute-done.8.refs_11_
  50.0 0.1 collective-permute-start.10
  50.0 0.0 collective-permute-done.9.refs_13_
  50.1 0.0 copy-start.2
  50.1 1.1 collective-permute-start.11
  51.1 0.0 collective-permute-done.24.refs_10_
  51.1 0.5 collective-permute-start.26
  51.6 13.5 %shard_map.73 = (bf16[4,256,128]{2,1,0:T(8,128)(2,1)S(1)}, bf16[4,256,128]{2,1,0:T(8,128)(2,1)S(1)}, bf16[4,256,128]{2,1,0:T(8,128)(2,1)S(1)}, bf16[4,256,128]{2...) custom-call(s32[1]{0:T(128)} %bitcast.me_ref, ...), custom_call_target="tpu_custom_call" | custom-call | flops 20000000000 | bytes 6000000 | tf_op jit(solution)/shard_map/pallas_call | solution.py:194
  65.1 0.0 collective-permute-done.10.refs_14_
  65.1 0.1 collective-permute-start
  65.2 0.0 collective-permute-done.11.refs_15_
  65.2 1.7 %collective-permute-start.1 = (bf16[4,256,128]{2,1,0:T(8,128)(2,1)S(1)}, bf16[4,256,128]{2,1,0:T(8,128)(2,1)S(1)}, u32[]{:S(2)}, u32[]{:S(2)}) collective-permute-start(bf16[4,256,128]{2,1,0:T(8,128)(2,1)S(1)} %get-tuple-element.31), channel_id=1, source_target_pairs={{0,64},{8,72},{16,80},{24,88},{32,96},{40,104},{48,112},{56,120},{... | collective-permute-start | bytes 786440 | tf_op jit(solution)/shard_map/ppermute | solution.py:342
  66.9 13.8 %collective-permute-done.refs_1_ = bf16[4,256,128]{2,1,0:T(8,128)(2,1)S(1)} collective-permute-done((bf16[4,256,128]{2,1,0:T(8,128)(2,1)S(1)}, bf16[4,256,128]{2,1,0:T(8,128)(2,1)S(1)}, u32[]{:S(2)}, u32[]{:S(2)}) %collective-permute-start) | collective-permute-done | bytes 262176 | tf_op jit(solution)/shard_map/ppermute | solution.py:342
  80.7 0.0 collective-permute-start.2
  80.7 0.0 collective-permute-done.1.refs_2_
  80.7 0.0 collective-permute-start.3
  80.7 8.5 %collective-permute-done.2.refs_3_ = bf16[4,256,128]{2,1,0:T(8,128)(2,1)S(1)} collective-permute-done((bf16[4,256,128]{2,1,0:T(8,128)(2,1)S(1)}, bf16[4,256,128]{2,1,0:T(8,128)(2,1)S(1)}, u32[]{:S(2)}, u32[]{:S(2)}) %collective-permute-start.2) | collective-permute-done | bytes 262176 | tf_op jit(solution)/shard_map/ppermute | solution.py:342
  89.2 0.1 collective-permute-start.4
  89.3 1.4 collective-permute-done.3.refs_5_
  90.7 1.7 %collective-permute-start.5 = (bf16[4,256,128]{2,1,0:T(8,128)(2,1)S(1)}, bf16[4,256,128]{2,1,0:T(8,128)(2,1)S(1)}, u32[]{:S(2)}, u32[]{:S(2)}) collective-permute-start(bf16[4,256,128]{2,1,0:T(8,128)(2,1)S(1)} %get-tuple-element.36), channel_id=1, source_target_pairs={{0,24},{8,0},{16,8},{24,16},{32,56},{40,32},{48,40},{56,48},{64,88... | collective-permute-start | bytes 786440 | tf_op jit(solution)/shard_map/ppermute | solution.py:342
  92.4 6.0 %collective-permute-done.4.refs_6_ = bf16[4,256,128]{2,1,0:T(8,128)(2,1)S(1)} collective-permute-done((bf16[4,256,128]{2,1,0:T(8,128)(2,1)S(1)}, bf16[4,256,128]{2,1,0:T(8,128)(2,1)S(1)}, u32[]{:S(2)}, u32[]{:S(2)}) %collective-permute-start.4) | collective-permute-done | bytes 262176 | tf_op jit(solution)/shard_map/ppermute | solution.py:342
  98.4 0.0 collective-permute-start.19
  98.4 5.9 %collective-permute-done.5.refs_7_ = bf16[4,256,128]{2,1,0:T(8,128)(2,1)S(1)} collective-permute-done((bf16[4,256,128]{2,1,0:T(8,128)(2,1)S(1)}, bf16[4,256,128]{2,1,0:T(8,128)(2,1)S(1)}, u32[]{:S(2)}, u32[]{:S(2)}) %collective-permute-start.5) | collective-permute-done | bytes 262176 | tf_op jit(solution)/shard_map/ppermute | solution.py:342
  104.3 0.5 add_first.1
  104.8 0.5 collective-permute-start.12
  105.3 0.0 collective-permute-done.19.refs_3_
  105.3 0.0 collective-permute-start.18
  105.3 1.2 collective-permute-done.18.refs_2_
  106.5 0.0 collective-permute-start.22
  106.5 0.0 collective-permute-done.21.refs_6_
  106.5 2.0 %collective-permute-start.23 = (bf16[512,1024]{1,0:T(8,128)(2,1)S(1)}, bf16[512,1024]{1,0:T(8,128)(2,1)S(1)}, u32[]{:S(2)}, u32[]{:S(2)}) collective-permute-start(bf16[512,1024]{1,0:T(8,128)(2,1)S(1)} %collective-permute-done.21.refs_6_), channel_id=1, source_target_pairs={{0,6},{1,3},{2,4},{3,1},{4,2},{5,7},{6,0},{7,5},{8,14},{9,11},{10,... | collective-permute-start | bytes 3145736 | tf_op jit(solution)/shard_map/ppermute | solution.py:324
  108.5 2.7 %collective-permute-done.12.refs_1_ = bf16[256,256]{1,0:T(8,128)(2,1)S(1)} collective-permute-done((bf16[256,256]{1,0:T(8,128)(2,1)S(1)}, bf16[256,256]{1,0:T(8,128)(2,1)S(1)}, u32[]{:S(2)}, u32[]{:S(2)}) %collective-permute-start.12) | collective-permute-done | bytes 131104 | tf_op jit(solution)/shard_map/ppermute | solution.py:342
  111.2 0.8 collective-permute-start.13
  112.1 5.6 %collective-permute-done.13.refs_2_ = bf16[256,256]{1,0:T(8,128)(2,1)S(1)} collective-permute-done((bf16[256,256]{1,0:T(8,128)(2,1)S(1)}, bf16[256,256]{1,0:T(8,128)(2,1)S(1)}, u32[]{:S(2)}, u32[]{:S(2)}) %collective-permute-start.13) | collective-permute-done | bytes 131104 | tf_op jit(solution)/shard_map/ppermute | solution.py:342
  117.7 1.3 collective-permute-start.14
  119.0 3.7 %collective-permute-done.14.refs_3_ = bf16[256,256]{1,0:T(8,128)(2,1)S(1)} collective-permute-done((bf16[256,256]{1,0:T(8,128)(2,1)S(1)}, bf16[256,256]{1,0:T(8,128)(2,1)S(1)}, u32[]{:S(2)}, u32[]{:S(2)}) %collective-permute-start.14) | collective-permute-done | bytes 131104 | tf_op jit(solution)/shard_map/ppermute | solution.py:342
  122.7 7.3 %collective-permute-done.15.refs_5_ = bf16[256,256]{1,0:T(8,128)(2,1)S(1)} collective-permute-done((bf16[256,256]{1,0:T(8,128)(2,1)S(1)}, bf16[256,256]{1,0:T(8,128)(2,1)S(1)}, u32[]{:S(2)}, u32[]{:S(2)}) %collective-permute-start.15) | collective-permute-done | bytes 131104 | tf_op jit(solution)/shard_map/ppermute | solution.py:342
  130.0 6.5 %collective-permute-done.16.refs_6_ = bf16[256,256]{1,0:T(8,128)(2,1)S(1)} collective-permute-done((bf16[256,256]{1,0:T(8,128)(2,1)S(1)}, bf16[256,256]{1,0:T(8,128)(2,1)S(1)}, u32[]{:S(2)}, u32[]{:S(2)}) %collective-permute-start.16) | collective-permute-done | bytes 131104 | tf_op jit(solution)/shard_map/ppermute | solution.py:342
  136.4 1.7 %collective-permute-start.17 = (bf16[256,256]{1,0:T(8,128)(2,1)S(1)}, bf16[256,256]{1,0:T(8,128)(2,1)S(1)}, u32[]{:S(2)}, u32[]{:S(2)}) collective-permute-start(bf16[256,256]{1,0:T(8,128)(2,1)S(1)} %get-tuple-element.52), channel_id=1, source_target_pairs={{0,96},{8,104},{16,112},{24,120},{32,0},{40,8},{48,16},{56,24},{64... | collective-permute-start | bytes 393224 | tf_op jit(solution)/shard_map/ppermute | solution.py:342
  138.2 3.2 %collective-permute-done.17.refs_7_ = bf16[256,256]{1,0:T(8,128)(2,1)S(1)} collective-permute-done((bf16[256,256]{1,0:T(8,128)(2,1)S(1)}, bf16[256,256]{1,0:T(8,128)(2,1)S(1)}, u32[]{:S(2)}, u32[]{:S(2)}) %collective-permute-start.17) | collective-permute-done | bytes 131104 | tf_op jit(solution)/shard_map/ppermute | solution.py:342
  141.4 0.0 collective-permute-start.20
  141.4 0.1 add_second.1.refs_0_
  141.5 3.5 %collective-permute-done.20.refs_4_ = f32[1,1024]{1,0:T(1,128)S(1)} collective-permute-done((f32[1,1024]{1,0:T(1,128)S(1)}, f32[1,1024]{1,0:T(1,128)S(1)}, u32[]{:S(2)}, u32[]{:S(2)}) %collective-permute-start.20) | collective-permute-done | bytes 4128 | tf_op jit(solution)/shard_map/ppermute | solution.py:324
  145.0 0.0 collective-permute-start.27
  145.0 6.4 %collective-permute-done.27.refs_0_ = bf16[256,512]{1,0:T(8,128)(2,1)S(1)} collective-permute-done((bf16[256,512]{1,0:T(8,128)(2,1)S(1)}, bf16[256,512]{1,0:T(8,128)(2,1)S(1)}, u32[]{:S(2)}, u32[]{:S(2)}) %collective-permute-start.27) | collective-permute-done | bytes 262176 | tf_op jit(solution)/shard_map/ppermute | solution.py:324
  151.4 0.0 collective-permute-done.26.refs_12_
  151.4 5.3 %shard_map.76 = bf16[256,1024]{1,0:T(8,128)(2,1)S(1)} custom-call(bf16[256,512]{1,0:T(8,128)(2,1)S(1)} %collective-permute-done.27.refs_0_, f32[1,1024]{1,0:T(1,128)S(1)} %bitcast.6, f32[1,1024]{1,0:T(1,128)S(1)} %collective-permute-done.18.refs_2_, f32[1,1024]{1,0:T(1,128)S(1)} %collective-permute-done.19.refs_3_, ...), custom_call_target="tpu_custom_call" | custom-call | flops 10000000000 | bytes 14000000 | tf_op jit(solution)/shard_map/pallas_call | solution.py:305
  156.7 0.1 collective-permute-start.28
  156.8 5.3 %shard_map.75 = f32[256,1024]{1,0:T(8,128)S(1)} custom-call(bf16[256,512]{1,0:T(8,128)(2,1)S(1)} %add_second.1.refs_0_, f32[1,1024]{1,0:T(1,128)S(1)} %bitcast.7, f32[1,1024]{1,0:T(1,128)S(1)} %collective-permute-done.18.refs_2_, f32[1,1024]{1,0:T(1,128)S(1)} %collective-permute-done.19.refs_3_, f32[1,1024]{1,0:T(1,128)S(1)} %collective-permute-done.20.refs_4_, ...), custom_call_target="tpu_custom_call" | custom-call | flops 10000000000 | bytes 14000000 | tf_op jit(solution)/shard_map/pallas_call | solution.py:305
  162.0 3.9 %collective-permute-done.28 = bf16[256,1024]{1,0:T(8,128)(2,1)S(1)} collective-permute-done((bf16[256,1024]{1,0:T(8,128)(2,1)S(1)}, bf16[256,1024]{1,0:T(8,128)(2,1)S(1)}, u32[]{:S(2)}, u32[]{:S(2)}) %collective-permute-start.28) | collective-permute-done | bytes 524320 | tf_op jit(solution)/shard_map/ppermute | solution.py:324
  165.9 0.9 add_convert_fusion
  (10 shorter events, 0.0 us)
Async XLA Ops:
  4.5 16.6 %all-to-all-start = ((s32[16,32,128]{2,1,0:T(8,128)}), s32[16,32,128]{2,1,0:T(8,128)S(1)}, u32[]{:S(2)}, u32[]{:S(2)}) async-start(s32[16,32,128]{2,1,0:T(8,128)} %dispatch.1), calls=%async_computation | async-start | bytes 524288 | tf_op jit(solution)/shard_map/all_to_all | solution.py:373
  12.6 38.6 %collective-permute-start.24 = (bf16[1024,1024]{1,0:T(8,128)(2,1)}, bf16[1024,1024]{1,0:T(8,128)(2,1)S(1)}, u32[]{:S(2)}, u32[]{:S(2)}) collective-permute-start(bf16[1024,1024]{1,0:T(8,128)(2,1)} %refs_9_.3), channel_id=1, source_target_pairs={{0,1},{1,0},{2,3},{3,2},{4,5},{5,4},{6,7},{7,6},{8,9},{9,8},{10,11... | collective-permute-start | bytes 6291464 | tf_op jit(solution)/shard_map/ppermute | solution.py:354
  21.1 27.3 %copy-start = (bf16[1024,1024]{1,0:T(8,128)(2,1)S(1)}, bf16[1024,1024]{1,0:T(8,128)(2,1)}, u32[]{:S(2)}) copy-start(bf16[1024,1024]{1,0:T(8,128)(2,1)} %refs_9_.3) | copy-start | bytes 6291460
  21.1 28.8 %copy-start.1 = (bf16[512,1024]{1,0:T(8,128)(2,1)S(1)}, bf16[512,1024]{1,0:T(8,128)(2,1)}, u32[]{:S(2)}) copy-start(bf16[512,1024]{1,0:T(8,128)(2,1)} %refs_5_.3) | copy-start | bytes 3145732
  34.7 13.6 %collective-permute-start.6 = (bf16[4,256,128]{2,1,0:T(8,128)(2,1)S(1)}, bf16[4,256,128]{2,1,0:T(8,128)(2,1)S(1)}, u32[]{:S(2)}, u32[]{:S(2)}) collective-permute-start(bf16[4,256,128]{2,1,0:T(8,128)(2,1)S(1)} %get-tuple-element.38), channel_id=1, source_target_pairs={{0,32},{8,40},{16,48},{24,56},{32,64},{40,72},{48,80},{56,88},{64,... | collective-permute-start | bytes 786440 | tf_op jit(solution)/shard_map/ppermute | solution.py:342
  34.8 15.1 %collective-permute-start.7 = (bf16[4,256,128]{2,1,0:T(8,128)(2,1)S(1)}, bf16[4,256,128]{2,1,0:T(8,128)(2,1)S(1)}, u32[]{:S(2)}, u32[]{:S(2)}) collective-permute-start(bf16[4,256,128]{2,1,0:T(8,128)(2,1)S(1)} %get-tuple-element.39), channel_id=1, source_target_pairs={{0,64},{8,72},{16,80},{24,88},{32,96},{40,104},{48,112},{56,120},{... | collective-permute-start | bytes 786440 | tf_op jit(solution)/shard_map/ppermute | solution.py:342
  34.9 15.1 %collective-permute-start.8 = (bf16[4,256,128]{2,1,0:T(8,128)(2,1)S(1)}, bf16[4,256,128]{2,1,0:T(8,128)(2,1)S(1)}, u32[]{:S(2)}, u32[]{:S(2)}) collective-permute-start(bf16[4,256,128]{2,1,0:T(8,128)(2,1)S(1)} %get-tuple-element.40), channel_id=1, source_target_pairs={{0,96},{8,104},{16,112},{24,120},{32,0},{40,8},{48,16},{56,24},{64... | collective-permute-start | bytes 786440 | tf_op jit(solution)/shard_map/ppermute | solution.py:342
  38.0 12.0 %collective-permute-start.9 = (bf16[4,256,128]{2,1,0:T(8,128)(2,1)S(1)}, bf16[4,256,128]{2,1,0:T(8,128)(2,1)S(1)}, u32[]{:S(2)}, u32[]{:S(2)}) collective-permute-start(bf16[4,256,128]{2,1,0:T(8,128)(2,1)S(1)} %get-tuple-element.42), channel_id=1, source_target_pairs={{0,8},{8,16},{16,24},{24,0},{32,40},{40,48},{48,56},{56,32},{64,72... | collective-permute-start | bytes 786440 | tf_op jit(solution)/shard_map/ppermute | solution.py:342
  48.4 103.0 %collective-permute-start.25 = (bf16[1024,1024]{1,0:T(8,128)(2,1)S(1)}, bf16[1024,1024]{1,0:T(8,128)(2,1)S(1)}, u32[]{:S(2)}, u32[]{:S(2)}) collective-permute-start(bf16[1024,1024]{1,0:T(8,128)(2,1)S(1)} %copy-done), channel_id=1, source_target_pairs={{0,6},{1,3},{2,4},{3,1},{4,2},{5,7},{6,0},{7,5},{8,14},{9,11},{10,... | collective-permute-start | bytes 6291464 | tf_op jit(solution)/shard_map/ppermute | solution.py:324
  49.9 56.5 %collective-permute-start.21 = (bf16[512,1024]{1,0:T(8,128)(2,1)S(1)}, bf16[512,1024]{1,0:T(8,128)(2,1)S(1)}, u32[]{:S(2)}, u32[]{:S(2)}) collective-permute-start(bf16[512,1024]{1,0:T(8,128)(2,1)S(1)} %copy-done.1), channel_id=1, source_target_pairs={{0,1},{1,0},{2,3},{3,2},{4,5},{5,4},{6,7},{7,6},{8,9},{9,8},{10,11... | collective-permute-start | bytes 3145736 | tf_op jit(solution)/shard_map/ppermute | solution.py:354
  50.0 15.1 %collective-permute-start.10 = (bf16[4,256,128]{2,1,0:T(8,128)(2,1)S(1)}, bf16[4,256,128]{2,1,0:T(8,128)(2,1)S(1)}, u32[]{:S(2)}, u32[]{:S(2)}) collective-permute-start(bf16[4,256,128]{2,1,0:T(8,128)(2,1)S(1)} %get-tuple-element.43), channel_id=1, source_target_pairs={{0,16},{8,24},{16,0},{24,8},{32,48},{40,56},{48,32},{56,40},{64,80... | collective-permute-start | bytes 786440 | tf_op jit(solution)/shard_map/ppermute | solution.py:342
  50.1 48.3 %copy-start.2 = (f32[1024]{0:T(1024)S(1)}, f32[1024]{0:T(1024)}, u32[]{:S(2)}) copy-start(f32[1024]{0:T(1024)} %param.12) | copy-start | bytes 12292
  50.1 15.1 %collective-permute-start.11 = (bf16[4,256,128]{2,1,0:T(8,128)(2,1)S(1)}, bf16[4,256,128]{2,1,0:T(8,128)(2,1)S(1)}, u32[]{:S(2)}, u32[]{:S(2)}) collective-permute-start(bf16[4,256,128]{2,1,0:T(8,128)(2,1)S(1)} %get-tuple-element.44), channel_id=1, source_target_pairs={{0,24},{8,0},{16,8},{24,16},{32,56},{40,32},{48,40},{56,48},{64,88... | collective-permute-start | bytes 786440 | tf_op jit(solution)/shard_map/ppermute | solution.py:342
  51.1 100.2 %collective-permute-start.26 = (bf16[1024,1024]{1,0:T(8,128)(2,1)S(1)}, bf16[1024,1024]{1,0:T(8,128)(2,1)S(1)}, u32[]{:S(2)}, u32[]{:S(2)}) collective-permute-start(bf16[1024,1024]{1,0:T(8,128)(2,1)S(1)} %collective-permute-done.24.refs_10_), channel_id=1, source_target_pairs={{0,6},{1,3},{2,4},{3,1},{4,2},{5,7},{6,0},{7,5},{8,14},{9,11},{10,... | collective-permute-start | bytes 6291464 | tf_op jit(solution)/shard_map/ppermute | solution.py:324
  65.1 15.6 %collective-permute-start = (bf16[4,256,128]{2,1,0:T(8,128)(2,1)S(1)}, bf16[4,256,128]{2,1,0:T(8,128)(2,1)S(1)}, u32[]{:S(2)}, u32[]{:S(2)}) collective-permute-start(bf16[4,256,128]{2,1,0:T(8,128)(2,1)S(1)} %get-tuple-element.30), channel_id=1, source_target_pairs={{0,32},{8,40},{16,48},{24,56},{32,64},{40,72},{48,80},{56,88},{64,... | collective-permute-start | bytes 786440 | tf_op jit(solution)/shard_map/ppermute | solution.py:342
  65.2 15.5 %collective-permute-start.1 = (bf16[4,256,128]{2,1,0:T(8,128)(2,1)S(1)}, bf16[4,256,128]{2,1,0:T(8,128)(2,1)S(1)}, u32[]{:S(2)}, u32[]{:S(2)}) collective-permute-start(bf16[4,256,128]{2,1,0:T(8,128)(2,1)S(1)} %get-tuple-element.31), channel_id=1, source_target_pairs={{0,64},{8,72},{16,80},{24,88},{32,96},{40,104},{48,112},{56,120},{... | collective-permute-start | bytes 786440 | tf_op jit(solution)/shard_map/ppermute | solution.py:342
  80.7 8.5 %collective-permute-start.2 = (bf16[4,256,128]{2,1,0:T(8,128)(2,1)S(1)}, bf16[4,256,128]{2,1,0:T(8,128)(2,1)S(1)}, u32[]{:S(2)}, u32[]{:S(2)}) collective-permute-start(bf16[4,256,128]{2,1,0:T(8,128)(2,1)S(1)} %get-tuple-element.32), channel_id=1, source_target_pairs={{0,96},{8,104},{16,112},{24,120},{32,0},{40,8},{48,16},{56,24},{64... | collective-permute-start | bytes 786440 | tf_op jit(solution)/shard_map/ppermute | solution.py:342
  80.7 9.9 %collective-permute-start.3 = (bf16[4,256,128]{2,1,0:T(8,128)(2,1)S(1)}, bf16[4,256,128]{2,1,0:T(8,128)(2,1)S(1)}, u32[]{:S(2)}, u32[]{:S(2)}) collective-permute-start(bf16[4,256,128]{2,1,0:T(8,128)(2,1)S(1)} %get-tuple-element.34), channel_id=1, source_target_pairs={{0,8},{8,16},{16,24},{24,0},{32,40},{40,48},{48,56},{56,32},{64,72... | collective-permute-start | bytes 786440 | tf_op jit(solution)/shard_map/ppermute | solution.py:342
  89.2 9.2 %collective-permute-start.4 = (bf16[4,256,128]{2,1,0:T(8,128)(2,1)S(1)}, bf16[4,256,128]{2,1,0:T(8,128)(2,1)S(1)}, u32[]{:S(2)}, u32[]{:S(2)}) collective-permute-start(bf16[4,256,128]{2,1,0:T(8,128)(2,1)S(1)} %get-tuple-element.35), channel_id=1, source_target_pairs={{0,16},{8,24},{16,0},{24,8},{32,48},{40,56},{48,32},{56,40},{64,80... | collective-permute-start | bytes 786440 | tf_op jit(solution)/shard_map/ppermute | solution.py:342
  90.7 13.6 %collective-permute-start.5 = (bf16[4,256,128]{2,1,0:T(8,128)(2,1)S(1)}, bf16[4,256,128]{2,1,0:T(8,128)(2,1)S(1)}, u32[]{:S(2)}, u32[]{:S(2)}) collective-permute-start(bf16[4,256,128]{2,1,0:T(8,128)(2,1)S(1)} %get-tuple-element.36), channel_id=1, source_target_pairs={{0,24},{8,0},{16,8},{24,16},{32,56},{40,32},{48,40},{56,48},{64,88... | collective-permute-start | bytes 786440 | tf_op jit(solution)/shard_map/ppermute | solution.py:342
  98.4 6.9 %collective-permute-start.19 = (f32[1,1024]{1,0:T(1,128)S(1)}, f32[1,1024]{1,0:T(1,128)S(1)}, u32[]{:S(2)}, u32[]{:S(2)}) collective-permute-start(f32[1,1024]{1,0:T(1,128)S(1)} %bitcast.4), channel_id=1, source_target_pairs={{0,6},{1,3},{2,4},{3,1},{4,2},{5,7},{6,0},{7,5},{8,14},{9,11},{10,... | collective-permute-start | bytes 12296 | tf_op jit(solution)/shard_map/ppermute | solution.py:324
  104.8 6.4 %collective-permute-start.12 = (bf16[256,256]{1,0:T(8,128)(2,1)S(1)}, bf16[256,256]{1,0:T(8,128)(2,1)S(1)}, u32[]{:S(2)}, u32[]{:S(2)}) collective-permute-start(bf16[256,256]{1,0:T(8,128)(2,1)S(1)} %get-tuple-element.46), channel_id=1, source_target_pairs={{0,8},{8,16},{16,24},{24,0},{32,40},{40,48},{48,56},{56,32},{64,72... | collective-permute-start | bytes 393224 | tf_op jit(solution)/shard_map/ppermute | solution.py:342
  105.3 1.2 collective-permute-start.18
  106.5 44.9 %collective-permute-start.22 = (bf16[512,1024]{1,0:T(8,128)(2,1)S(1)}, bf16[512,1024]{1,0:T(8,128)(2,1)S(1)}, u32[]{:S(2)}, u32[]{:S(2)}) collective-permute-start(bf16[512,1024]{1,0:T(8,128)(2,1)S(1)} %copy-done.1), channel_id=1, source_target_pairs={{0,6},{1,3},{2,4},{3,1},{4,2},{5,7},{6,0},{7,5},{8,14},{9,11},{10,... | collective-permute-start | bytes 3145736 | tf_op jit(solution)/shard_map/ppermute | solution.py:324
  106.5 44.9 %collective-permute-start.23 = (bf16[512,1024]{1,0:T(8,128)(2,1)S(1)}, bf16[512,1024]{1,0:T(8,128)(2,1)S(1)}, u32[]{:S(2)}, u32[]{:S(2)}) collective-permute-start(bf16[512,1024]{1,0:T(8,128)(2,1)S(1)} %collective-permute-done.21.refs_6_), channel_id=1, source_target_pairs={{0,6},{1,3},{2,4},{3,1},{4,2},{5,7},{6,0},{7,5},{8,14},{9,11},{10,... | collective-permute-start | bytes 3145736 | tf_op jit(solution)/shard_map/ppermute | solution.py:324
  111.2 6.5 %collective-permute-start.13 = (bf16[256,256]{1,0:T(8,128)(2,1)S(1)}, bf16[256,256]{1,0:T(8,128)(2,1)S(1)}, u32[]{:S(2)}, u32[]{:S(2)}) collective-permute-start(bf16[256,256]{1,0:T(8,128)(2,1)S(1)} %get-tuple-element.47), channel_id=1, source_target_pairs={{0,16},{8,24},{16,0},{24,8},{32,48},{40,56},{48,32},{56,40},{64,80... | collective-permute-start | bytes 393224 | tf_op jit(solution)/shard_map/ppermute | solution.py:342
  117.7 5.0 %collective-permute-start.14 = (bf16[256,256]{1,0:T(8,128)(2,1)S(1)}, bf16[256,256]{1,0:T(8,128)(2,1)S(1)}, u32[]{:S(2)}, u32[]{:S(2)}) collective-permute-start(bf16[256,256]{1,0:T(8,128)(2,1)S(1)} %get-tuple-element.48), channel_id=1, source_target_pairs={{0,24},{8,0},{16,8},{24,16},{32,56},{40,32},{48,40},{56,48},{64,88... | collective-permute-start | bytes 393224 | tf_op jit(solution)/shard_map/ppermute | solution.py:342
  122.7 7.3 %collective-permute-start.15 = (bf16[256,256]{1,0:T(8,128)(2,1)S(1)}, bf16[256,256]{1,0:T(8,128)(2,1)S(1)}, u32[]{:S(2)}, u32[]{:S(2)}) collective-permute-start(bf16[256,256]{1,0:T(8,128)(2,1)S(1)} %get-tuple-element.50), channel_id=1, source_target_pairs={{0,32},{8,40},{16,48},{24,56},{32,64},{40,72},{48,80},{56,88},{64,... | collective-permute-start | bytes 393224 | tf_op jit(solution)/shard_map/ppermute | solution.py:342
  129.9 6.5 %collective-permute-start.16 = (bf16[256,256]{1,0:T(8,128)(2,1)S(1)}, bf16[256,256]{1,0:T(8,128)(2,1)S(1)}, u32[]{:S(2)}, u32[]{:S(2)}) collective-permute-start(bf16[256,256]{1,0:T(8,128)(2,1)S(1)} %get-tuple-element.51), channel_id=1, source_target_pairs={{0,64},{8,72},{16,80},{24,88},{32,96},{40,104},{48,112},{56,120},{... | collective-permute-start | bytes 393224 | tf_op jit(solution)/shard_map/ppermute | solution.py:342
  136.4 5.0 %collective-permute-start.17 = (bf16[256,256]{1,0:T(8,128)(2,1)S(1)}, bf16[256,256]{1,0:T(8,128)(2,1)S(1)}, u32[]{:S(2)}, u32[]{:S(2)}) collective-permute-start(bf16[256,256]{1,0:T(8,128)(2,1)S(1)} %get-tuple-element.52), channel_id=1, source_target_pairs={{0,96},{8,104},{16,112},{24,120},{32,0},{40,8},{48,16},{56,24},{64... | collective-permute-start | bytes 393224 | tf_op jit(solution)/shard_map/ppermute | solution.py:342
  141.4 3.6 %collective-permute-start.20 = (f32[1,1024]{1,0:T(1,128)S(1)}, f32[1,1024]{1,0:T(1,128)S(1)}, u32[]{:S(2)}, u32[]{:S(2)}) collective-permute-start(f32[1,1024]{1,0:T(1,128)S(1)} %collective-permute-done.18.refs_2_), channel_id=1, source_target_pairs={{0,6},{1,3},{2,4},{3,1},{4,2},{5,7},{6,0},{7,5},{8,14},{9,11},{10,... | collective-permute-start | bytes 12296 | tf_op jit(solution)/shard_map/ppermute | solution.py:324
  145.0 6.4 %collective-permute-start.27 = (bf16[256,512]{1,0:T(8,128)(2,1)S(1)}, bf16[256,512]{1,0:T(8,128)(2,1)S(1)}, u32[]{:S(2)}, u32[]{:S(2)}) collective-permute-start(bf16[256,512]{1,0:T(8,128)(2,1)S(1)} %add_second.1.refs_0_), channel_id=1, source_target_pairs={{0,2},{1,7},{2,0},{3,5},{4,6},{5,3},{6,4},{7,1},{8,10},{9,15},{10,... | collective-permute-start | bytes 786440 | tf_op jit(solution)/shard_map/ppermute | solution.py:324
  156.7 9.3 %collective-permute-start.28 = (bf16[256,1024]{1,0:T(8,128)(2,1)S(1)}, bf16[256,1024]{1,0:T(8,128)(2,1)S(1)}, u32[]{:S(2)}, u32[]{:S(2)}) collective-permute-start(bf16[256,1024]{1,0:T(8,128)(2,1)S(1)} %shard_map.76), channel_id=1, source_target_pairs={{0,2},{1,7},{2,0},{3,5},{4,6},{5,3},{6,4},{7,1},{8,10},{9,15},{10,... | collective-permute-start | bytes 1572872 | tf_op jit(solution)/shard_map/ppermute | solution.py:324
